TPU v7x, 32 devices: a whole 2x2x4 slice. The times are simulated.
32 devices in a mesh: batch: 2 (over x), row: 4 (over z), col: 4 (over y, core).
Axes of the slice: x: 2, y: 2, z: 4, core: 2. Of those that a mesh axis runs over, the one named last changes fastest.
Arguments:
- a_mat: bfloat16 [2048, 32768], P(('batch', 'row'), 'col'), parts along dimension 0
Outputs:
- output: bfloat16 [2048, 1024], P(('batch', 'row'), 'col'), parts along dimension 0
There are 2 independent parts. A program takes and returns all parts, laid end to end along the dimension named above; each array names one.
All inputs are finite; a program needn't handle non-finite values.
Results may differ from a plain program's by a relative error of at most 0.001.
Values are sent between devices in bfloat16 or wider.
A program may use at most 1 GiB of HBM per device.

v0:
```python
import jax
import jax.numpy as jnp
from jax import lax
from jax.sharding import PartitionSpec as P

BLOCK = 256


def lower_part(row_panel, col_panel, row_step, row_pos, col_step, col_pos):
    row_blocks = row_panel.shape[0] // BLOCK
    col_blocks = col_panel.shape[0] // BLOCK
    col_total = col_panel.shape[0]
    band_size = max(1, row_blocks // 8)
    col_local = jnp.arange(col_total)
    col_index = ((col_local // BLOCK) * col_step + col_pos) * BLOCK + col_local % BLOCK
    pieces = []
    for first_blk in range(0, row_blocks, band_size):
        last_blk = min(first_blk + band_size, row_blocks)
        col_width = BLOCK * min(col_blocks, (last_blk * row_step - 1) // col_step + 1)
        product = lax.dot_general(row_panel[first_blk * BLOCK:last_blk * BLOCK], col_panel[:col_width], (((1,), (1,)), ((), ())), preferred_element_type=jnp.float32)
        row_local = jnp.arange(first_blk * BLOCK, last_blk * BLOCK)
        row_index = ((row_local // BLOCK) * row_step + row_pos) * BLOCK + row_local % BLOCK
        kept_vals = jnp.where(row_index[:, None] >= col_index[None, :col_width], product, 0.0).astype(jnp.bfloat16)
        pieces.append(jnp.pad(kept_vals, ((0, 0), (0, col_total - col_width))))
    return jnp.concatenate(pieces, axis=0)


def solution(mesh):
    row_count = mesh.shape['row']
    col_count = mesh.shape['col']

    def local_fn(a_local):
        local_rows, m_local = a_local.shape
        n_total = local_rows * row_count
        row_pos = lax.axis_index('row')
        col_pos = lax.axis_index('col')
        row_panel = lax.all_gather(a_local, 'col', axis=1, tiled=True)
        gathered = lax.all_gather(a_local.reshape(local_rows // BLOCK, BLOCK, m_local), 'row', axis=1)
        grouped = gathered.reshape(n_total // (BLOCK * col_count), col_count, BLOCK, m_local)
        swapped = lax.all_to_all(grouped, 'col', 1, 3, tiled=True)
        col_panel = swapped.reshape(n_total // col_count, m_local * col_count)
        return lower_part(row_panel, col_panel, row_count, row_pos, col_count, col_pos)

    part_spec = P(('batch', 'row'), 'col')
    return jax.shard_map(local_fn, mesh=mesh, in_specs=(part_spec,), out_specs=part_spec, check_vma=False)
```

profile of v0, /device:TPU:24, one launch (start us, length us, event | category | flops | bytes accessed | tf_op | source)
XLA Modules:
  0.0 618.0 jit_solution(14343409966692598571)
XLA Ops:
  6.5 0.0 all-gather.6.cloned.1.call-start
  6.5 0.7 all-gather.6.cloned.1.call-update
  7.3 0.0 all-gather.4.cloned.1.call-start
  7.3 0.7 all-gather.4.cloned.1.call-update
  8.0 286.8 %all-gather.6.cloned.1.call-done = bf16[1024,8192]{1,0:T(8,128)(2,1)} async-done(((bf16[256,8192]{1,0:T(8,128)(2,1)}), bf16[1024,8192]{1,0:T(8,128)(2,1)}) %all-gather.6.cloned.1.call-update) | async-done | bytes 16777232 | tf_op jit(solution)/shard_map/all_gather | solution.py:38
  294.8 7.0 %all-to-all-start = ((bf16[1,4,256,8192]{3,2,0,1:T(8,128)(2,1)}), bf16[1,4,256,8192]{3,2,0,1:T(8,128)(2,1)}, u32[]{:S(2)}, u32[]{:S(2)}) async-start(bf16[1,4,256,8192]{3,2,0,1:T(8,128)(2,1)} %bitcast.10), calls=%async_computation | async-start | bytes 33554432 | tf_op jit(solution)/shard_map/all_to_all | solution.py:40
  301.8 272.6 %all-to-all-done = bf16[1,4,256,8192]{3,2,0,1:T(8,128)(2,1)} async-done(((bf16[1,4,256,8192]{3,2,0,1:T(8,128)(2,1)}), bf16[1,4,256,8192]{3,2,0,1:T(8,128)(2,1)}, u32[]{:S(2)}, u32[]{:S(2)}) %all-to-all-start) | async-done | bytes 16777248 | tf_op jit(solution)/shard_map/all_to_all | solution.py:40
  574.3 21.1 %copy.4 = bf16[1,4,256,8192]{2,3,1,0:T(8,128)(2,1)} copy(bf16[1,4,256,8192]{3,2,0,1:T(8,128)(2,1)} %all-to-all-done) | data formatting | bytes 33554432 | tf_op jit(solution)/shard_map/all_to_all | solution.py:40
  595.5 0.0 all-gather.4.cloned.1.call-done
  595.5 15.7 %fusion = bf16[256,256]{1,0:T(8,128)(2,1)} fusion(bf16[256,32768]{1,0:T(8,128)(2,1)} %all-gather.4.cloned.1.call-done, bf16[256,32768]{0,1:T(8,128)(2,1)} %bitcast.11, s32[256]{0:T(256)S(1)} %get-tuple-element.5, s32[256]{0:T(256)S(1)} %get-tuple-element.6), kind=kOutput, calls=%fused_computation.1 | convolution fusion | flops 4295163904 | bytes 33687552 | tf_op jit(solution)/shard_map/dot_general | solution.py:20
  (1 shorter events, 0.0 us)
Async XLA Ops:
  6.5 288.2 %all-gather.6.cloned.1.call-start = ((), (), s32[]{:S(2)}) async-start(), calls=%async_computation.2 | async-start | bytes 20971520 | tf_op jit(solution)/shard_map/all_gather | solution.py:38
  7.3 588.2 %all-gather.4.cloned.1.call-start = ((), (), s32[]{:S(2)}) async-start(), calls=%async_computation.1 | async-start | bytes 20971520 | tf_op jit(solution)/shard_map/all_gather | solution.py:37
  294.8 279.6 %all-to-all-start = ((bf16[1,4,256,8192]{3,2,0,1:T(8,128)(2,1)}), bf16[1,4,256,8192]{3,2,0,1:T(8,128)(2,1)}, u32[]{:S(2)}, u32[]{:S(2)}) async-start(bf16[1,4,256,8192]{3,2,0,1:T(8,128)(2,1)} %bitcast.10), calls=%async_computation | async-start | bytes 33554432 | tf_op jit(solution)/shard_map/all_to_all | solution.py:40
Sparse Core Ops, SparseCore 0:
  8.9 285.8 all-gather.5
  296.3 198.2 all-gather.3
where the time goes:
time: 623 us; the launch traced here: 618 us
  waiting for transfers between devices  561 us (90%)
  local copies, waits for them, and re-layouts  21.1 us (3%)
  matrix products  15.7 us (3%)
  between operations  13.4 us (2%)
  starting transfers between devices  7.01 us (1%)
    all_gather x1, waiting for transfers between devices, local_fn(): lax.all_gather(a_local.reshape(local_rows // BLOCK, BLOCK, m_local), 'row...  287 us
    all_to_all x1, waiting for transfers between devices, local_fn(): swapped = lax.all_to_all(grouped, 'col', 1, 3, tiled=True)  273 us
    all_to_all x1, local copies, waits for them, and re-layouts, local_fn(): swapped = lax.all_to_all(grouped, 'col', 1, 3, tiled=True)  21.1 us
    dot_general x1, matrix products, lower_part(): lax.dot_general(row_panel[first_blk * BLOCK:last_blk * BLOCK], col_panel[...  15.7 us
  transfers between devices with their start and end apart: 3, of which 2 were waited for; matrix products, arithmetic and copies ran while one was open for 3% of the time, Pallas kernels for 0%

commit v1 on v0

v1 whole, which is shorter than its diff:
```python
import functools

import jax
import jax.numpy as jnp
from jax import lax
from jax.experimental import pallas as pl
from jax.experimental.pallas import tpu as pltpu
from jax.sharding import PartitionSpec as P

MESH = pl.DeviceIdType.MESH
NP = 8
NS = 8


def mm(a, b):
    return lax.dot_general(a, b, (((1,), (1,)), ((), ())), preferred_element_type=jnp.float32)


def kernel(a_ref, o_ref, X, Y, W, Pa, Qa, R, PR, ld, s_z, r_y, s_d, r_d, r_w, s_p, r_p, s_q, r_r):
    rows, m = a_ref.shape
    pw = m // (2 * NP)
    ul, dl = pw - pw // 4, pw + pw // 4
    ku = (NP - 1) * pw + ul
    kd = m - ku
    st = rows // NS
    z = lax.axis_index("row")
    c = lax.axis_index("col")
    y = c // 2
    k = c % 2
    sib = 2 * y + 1 - k

    def rcopy(src, dst, ss, rs, row, col):
        return pltpu.make_async_remote_copy(
            src_ref=src, dst_ref=dst, send_sem=ss, recv_sem=rs, device_id={"row": row, "col": col}, device_id_type=MESH)

    def wait_recv(ref, sem):
        pltpu.make_async_copy(ref, ref, sem).wait()

    def up(p, w):
        return pl.ds(pl.multiple_of(p * pw, 128), w)

    def dn(p, w):
        return pl.ds(pl.multiple_of(ku + p * pw, 128), w)

    def off(p, w):
        return pl.ds(pl.multiple_of(p * pw, 128), w)

    def strip(s):
        return pl.ds(pl.multiple_of(s * st, st), st)

    DALL = pl.ds(ku, kd)

    def each(n, fn):
        lax.fori_loop(0, n, lambda i, u: (fn(i), u)[1], 0)

    load = pltpu.make_async_copy(a_ref, X.at[k], ld.at[0])
    load.start()
    bar = pltpu.get_barrier_semaphore()
    for dz in range(4):
        for dc in range(4):
            if dz or dc:
                pl.semaphore_signal(bar, inc=1, device_id={"row": (z + dz) % 4, "col": (c + dc) % 4}, device_id_type=MESH)
    pl.semaphore_wait(bar, 15)

    def z0_send(kind, p):
        if kind == "d":
            cs = dn(p, dl if p == NP - 1 else pw)
            n = p
        else:
            cs = up(p, ul if p == NP - 1 else pw)
            n = NP + p
        return rcopy(a_ref.at[:, cs], Y.at[k, :, cs], s_z.at[n], r_y.at[n], 1, c)

    def z3_send(kind, p):
        if kind == "u":
            cs = up(p, ul if p == NP - 1 else pw)
            return rcopy(a_ref.at[:, cs], Y.at[k, :, cs], s_z.at[p], r_y.at[p], 2, c)
        return rcopy(a_ref.at[strip(p), DALL], Y.at[k, strip(p), DALL], s_z.at[NP + p], r_y.at[NP + p], 2, c)

    def z1_send(p):
        w = ul if p == NP - 1 else pw
        return rcopy(a_ref.at[:, up(p, w)], W.at[k, :, up(p, w)], s_z.at[p], r_w.at[k, p], 2, 2 * y + 1)

    def z2_send(p):
        w = dl if p == NP - 1 else pw
        return rcopy(a_ref.at[:, dn(p, w)], W.at[k, :, off(p, w)], s_z.at[p], r_w.at[k, p], 1, 2 * y)

    @pl.when(z == 0)
    def _():
        for p in range(NP - 2):
            z0_send("d", p).start()
        z0_send("u", 0).start()
        for p in range(NP - 2, NP):
            z0_send("d", p).start()
        for p in range(1, NP):
            z0_send("u", p).start()

    @pl.when(z == 3)
    def _():
        for p in range(NP - 2):
            z3_send("u", p).start()
        z3_send("d", 0).start()
        for p in range(NP - 2, NP):
            z3_send("u", p).start()
        for p in range(1, NS):
            z3_send("d", p).start()

    x_d = rcopy(a_ref.at[:, DALL], X.at[k, :, DALL], s_d.at[NP], r_d.at[NP], z, sib)
    x_u = rcopy(a_ref.at[:, pl.ds(0, ku)], X.at[k, :, pl.ds(0, ku)], s_d.at[NP], r_d.at[NP], z, sib)

    @pl.when(z == 1)
    def _():
        for p in range(NP):
            z1_send(p).start()
        x_d.start()

    @pl.when(z == 2)
    def _():
        for p in range(NP):
            z2_send(p).start()
        x_u.start()

    Pa[...] = jnp.zeros_like(Pa)
    Qa[...] = jnp.zeros_like(Qa)
    load.wait()
    dq = jnp.where(z == 1, 1, 0)

    def diag(p):
        cs = off(p, pw)
        Qa[dq] += mm(X[k, :, cs], X[k, :, cs])

    each(2 * NP, diag)

    def slot(owner):
        return (c - owner + 3) % 4

    dsend = rcopy(Qa.at[dq], R.at[slot(z)], s_q.at[NS], r_r.at[slot(z), 0], z, z)

    @pl.when(c != z)
    def _():
        dsend.start()

    def a_fwd(p, w):
        return rcopy(Y.at[k, :, dn(p, w)], Y.at[k, :, dn(p, w)], s_d.at[p], r_d.at[p], z, sib)

    def zA(p, w):
        cs = dn(p, w)
        wait_recv(Y.at[k, :, cs], r_y.at[p])
        a_fwd(p, w).start()
        Qa[0] += mm(X[k, :, cs], Y[k, :, cs])

    def zC(q, w):
        cs, ws = dn(q, w), off(q, w)
        wait_recv(Y.at[1 - k, :, cs], r_d.at[q])
        for h in range(2):
            wait_recv(W.at[h, :, ws], r_w.at[h, q])
        for h in range(2):
            Pa[0] += mm(W[h, :, ws], Y[h, :, cs])
            Pa[1] += mm(W[h, :, ws], X[h, :, cs])

    def b_fwd(p, w):
        return rcopy(Y.at[k, :, up(p, w)], W.at[k, :, up(p, w)], s_z.at[NP + p], r_w.at[k, p], 2, 2 * y)

    def zB(p, w):
        cs = up(p, w)
        wait_recv(Y.at[k, :, cs], r_y.at[NP + p])
        b_fwd(p, w).start()
        Qa[0] += mm(X[k, :, cs], Y[k, :, cs])

    def p_send(j):
        return rcopy(Pa.at[j], PR.at[0], s_p.at[j], r_p.at[NS], 2, 2 * y + j)

    def ps_send(j, s):
        return rcopy(Pa.at[j, strip(s)], PR.at[1, strip(s)], s_p.at[2 * s + j], r_p.at[s], 2, 2 * y + j)

    def zS(s):
        for h in range(2):
            wait_recv(W.at[h, strip(s), pl.ds(0, kd)], r_w.at[h, s])
        for j, B in ((0, Y), (1, X)):
            acc = mm(W[0, strip(s), :kd], B[0, :, DALL])
            acc += mm(W[1, strip(s), :kd], B[1, :, DALL])
            Pa[j, strip(s), :] = acc
        for j in range(2):
            ps_send(j, s).start()

    q0send = rcopy(Qa.at[0], R.at[slot(0)], s_q.at[0], r_r.at[slot(0), 0], 1, 0)

    @pl.when(z == 1)
    def _():
        wait_recv(X.at[1 - k, :, DALL], r_d.at[NP])

        def step_a(p):
            zA(p, pw)

            @pl.when((k == 0) & (p >= 1))
            def _():
                zC(p - 1, pw)

        each(NP - 1, step_a)
        zA(NP - 1, dl)

        @pl.when(k == 0)
        def _():
            zC(NP - 2, pw)

        zB(0, pw)

        @pl.when(k == 0)
        def _():
            zC(NP - 1, dl)
            p_send(0).start()
            p_send(1).start()

        @pl.when(k == 1)
        def _():
            each(NP - 1, lambda p: wait_recv(Y.at[0, :, dn(p, pw)], r_d.at[p]))
            wait_recv(Y.at[0, :, dn(NP - 1, dl)], r_d.at[NP - 1])

        def step_b(i):
            zB(i + 1, pw)

            @pl.when((k == 1) & (i >= 1))
            def _():
                zS(i - 1)

        each(NP - 2, step_b)
        zB(NP - 1, ul)

        @pl.when(c != 0)
        def _():
            q0send.start()

        @pl.when(k == 1)
        def _():
            each(NS - (NP - 3), lambda i: zS(i + NP - 3))

    def u_fwd(p, w):
        return rcopy(Y.at[k, :, up(p, w)], Y.at[k, :, up(p, w)], s_d.at[p], r_d.at[p], z, sib)

    def yA(p, w):
        cs = up(p, w)
        wait_recv(Y.at[k, :, cs], r_y.at[p])
        u_fwd(p, w).start()
        Qa[1] += mm(Y[k, :, cs], X[k, :, cs])

    def yC(q, w):
        cs = up(q, w)
        for h in range(2):
            wait_recv(W.at[h, :, cs], r_w.at[h, q])
        for h in range(2):
            Pa[0] += mm(X[h, :, cs], W[h, :, cs])
            Pa[1] += mm(Y[h, :, cs], W[h, :, cs])

    def d_fwd(s):
        return rcopy(Y.at[k, strip(s), DALL], W.at[k, strip(s), pl.ds(0, kd)], s_z.at[NP + s], r_w.at[k, s], 1, 2 * y + 1)

    def q1send(s):
        return rcopy(Qa.at[1, strip(s)], R.at[c, strip(s)], s_q.at[s], r_r.at[c, s], 3, 2)

    def yB(s):
        wait_recv(Y.at[k, strip(s), DALL], r_y.at[NP + s])
        d_fwd(s).start()
        Qa[1, strip(s), :] += mm(Y[k, strip(s), DALL], X[k, :, DALL])
        q1send(s).start()

    s2send = rcopy(Pa.at[0], R.at[0], s_p.at[NS], r_r.at[0, 0], 2, k)

    def s3send(s):
        return rcopy(Pa.at[1, strip(s)], R.at[y, strip(s)], s_p.at[s], r_r.at[y, s], 3, k)

    def fin(s):
        wait_recv(PR.at[1, strip(s)], r_p.at[s])
        Pa[1, strip(s), :] += PR[1, strip(s), :]
        s3send(s).start()

    @pl.when(z == 2)
    def _():
        wait_recv(X.at[1 - k, :, pl.ds(0, ku)], r_d.at[NP])

        def step_a(p):
            yA(p, pw)

            @pl.when((k == 1) & (p >= 1))
            def _():
                wait_recv(Y.at[0, :, up(p - 1, pw)], r_d.at[p - 1])
                yC(p - 1, pw)

        each(NP - 1, step_a)
        yA(NP - 1, ul)

        @pl.when(k == 1)
        def _():
            wait_recv(Y.at[0, :, up(NP - 2, pw)], r_d.at[NP - 2])
            yC(NP - 2, pw)

        yB(0)

        @pl.when(k == 1)
        def _():
            wait_recv(Y.at[0, :, up(NP - 1, ul)], r_d.at[NP - 1])
            yC(NP - 1, ul)

        @pl.when(k == 0)
        def _():
            each(NP - 1, lambda p: wait_recv(Y.at[1, :, up(p, pw)], r_d.at[p]))
            wait_recv(Y.at[1, :, up(NP - 1, ul)], r_d.at[NP - 1])

        def step_b(i):
            yB(i + 1)

            @pl.when((k == 0) & (i >= 1))
            def _():
                yC(i - 1, pw)

        each(NS - 1, step_b)

        @pl.when(k == 0)
        def _():
            each(NP - 1 - (NS - 2), lambda i: yC(i + NS - 2, pw))
            yC(NP - 1, ul)

        wait_recv(PR.at[0], r_p.at[NS])
        Pa[0] += PR[0]

        @pl.when(y == 1)
        def _():
            s2send.start()

        each(NS, fin)

    diff = lax.broadcasted_iota(jnp.int32, (rows, rows), 0) - lax.broadcasted_iota(jnp.int32, (rows, rows), 1)

    @pl.when(c > z)
    def _():
        o_ref[...] = jnp.zeros_like(o_ref)

    @pl.when(c == z)
    def _():
        for i in range(3):
            wait_recv(R.at[i], r_r.at[i, 0])
        total = Qa[dq] + R[0] + R[1] + R[2]
        o_ref[...] = jnp.where(diff >= 0, total, 0.0).astype(o_ref.dtype)

    @pl.when((z == 1) & (c == 0))
    def _():
        for i in range(3):
            wait_recv(R.at[i], r_r.at[i, 0])
        o_ref[...] = (Qa[0] + R[0] + R[1] + R[2]).astype(o_ref.dtype)

    @pl.when((z == 2) & (y == 0))
    def _():
        wait_recv(R.at[0], r_r.at[0, 0])
        o_ref[...] = (Pa[0] + R[0]).astype(o_ref.dtype)

    @pl.when((z == 3) & (c == 2))
    def _():
        for s in range(NS):
            for i in range(4):
                wait_recv(R.at[i, strip(s)], r_r.at[i, s])
        o_ref[...] = (R[0] + R[1] + R[2] + R[3]).astype(o_ref.dtype)

    @pl.when((z == 3) & (y == 0))
    def _():
        for s in range(NS):
            for i in range(2):
                wait_recv(R.at[i, strip(s)], r_r.at[i, s])
        o_ref[...] = (R[0] + R[1]).astype(o_ref.dtype)

    @pl.when(c != z)
    def _():
        dsend.wait_send()

    @pl.when(z == 0)
    def _():
        for p in range(NP):
            z0_send("d", p).wait_send()
            z0_send("u", p).wait_send()

    @pl.when(z == 3)
    def _():
        for p in range(NP):
            z3_send("u", p).wait_send()
        for p in range(NS):
            z3_send("d", p).wait_send()

    @pl.when(z == 1)
    def _():
        x_d.wait_send()
        for p in range(NP):
            z1_send(p).wait_send()
            a_fwd(p, dl if p == NP - 1 else pw).wait_send()
            b_fwd(p, ul if p == NP - 1 else pw).wait_send()

        @pl.when(k == 0)
        def _():
            for j in range(2):
                p_send(j).wait_send()

        @pl.when(k == 1)
        def _():
            for s in range(NS):
                for j in range(2):
                    ps_send(j, s).wait_send()

        @pl.when(c != 0)
        def _():
            q0send.wait_send()

    @pl.when(z == 2)
    def _():
        x_u.wait_send()
        for p in range(NP):
            z2_send(p).wait_send()
            u_fwd(p, ul if p == NP - 1 else pw).wait_send()
        for s in range(NS):
            d_fwd(s).wait_send()
            q1send(s).wait_send()
            s3send(s).wait_send()

        @pl.when(y == 1)
        def _():
            s2send.wait_send()


def solution(mesh):
    def local_fn(a_local):
        rows, m = a_local.shape
        pw = m // (2 * NP)
        kd = NP * pw + pw // 4
        f32, bf16 = jnp.float32, jnp.bfloat16
        dma = pltpu.SemaphoreType.DMA
        return pl.pallas_call(
            kernel,
            out_shape=jax.ShapeDtypeStruct((rows, rows), bf16),
            in_specs=[pl.BlockSpec(memory_space=pl.ANY)],
            out_specs=pl.BlockSpec(memory_space=pltpu.VMEM),
            scratch_shapes=[
                pltpu.VMEM((2, rows, m), bf16),
                pltpu.VMEM((2, rows, m), bf16),
                pltpu.VMEM((2, rows, kd), bf16),
                pltpu.VMEM((2, rows, rows), f32),
                pltpu.VMEM((2, rows, rows), f32),
                pltpu.VMEM((4, rows, rows), f32),
                pltpu.VMEM((2, rows, rows), f32),
                dma((1,)), dma((2 * NP,)), dma((2 * NP,)), dma((NP + 1,)), dma((NP + 1,)), dma((2, NP,)),
                dma((2 * NS,)), dma((NS + 1,)), dma((NS + 1,)), dma((4, NS)),
            ],
            compiler_params=pltpu.CompilerParams(
                collective_id=0, has_side_effects=True, vmem_limit_bytes=50 * 1024 * 1024),
        )(a_local)

    part_spec = P(("batch", "row"), "col")
    return jax.shard_map(local_fn, mesh=mesh, in_specs=(part_spec,), out_specs=part_spec, check_vma=False)
```

time: 623 us -> 121 us (0.19)
  waiting for transfers between devices: 561 us -> 0 us
  Pallas kernels: 0 us -> 121 us
  local copies, waits for them, and re-layouts: 21.1 us -> 0.66 us
  matrix products: 15.7 us -> 0 us
  between operations: 13.4 us -> 0.01 us
  starting transfers between devices: 7.01 us -> 0 us
    all_gather x2 -> x0, waiting for transfers between devices: 287 us -> none  [the longest x1 287 us: local_fn(): lax.all_gather(a_local.reshape(local_rows // BLOCK, BLOCK, m_local), 'row...]
    all_to_all x1 -> x0, waiting for transfers between devices: 273 us -> none  [local_fn(): swapped = lax.all_to_all(grouped, 'col', 1, 3, tiled=True)]
    pallas_call x0 -> x1, Pallas kernels: none -> 121 us  [local_fn(): pl.pallas_call(kernel, out_shape=jax.ShapeDtypeStruct((rows, rows), bf16)...]
    all_to_all x1 -> x0, local copies, waits for them, and re-layouts: 21.1 us -> none  [local_fn(): swapped = lax.all_to_all(grouped, 'col', 1, 3, tiled=True)]
    dot_general x1 -> x0, matrix products: 15.7 us -> none  [lower_part(): lax.dot_general(row_panel[first_blk * BLOCK:last_blk * BLOCK], col_panel[...]
    all_to_all x1 -> x0, starting transfers between devices: 6.97 us -> none  [local_fn(): swapped = lax.all_to_all(grouped, 'col', 1, 3, tiled=True)]
  transfers between devices with their start and end apart: 3 -> 0, of which waited for: 2 -> 0; matrix products, arithmetic and copies ran while one was open for 3% -> 0% of each run, Pallas kernels for 0% -> 0%
where the time goes in v1:
time: 121 us
  Pallas kernels  121 us (100%)
    pallas_call x1, Pallas kernels, local_fn(): pl.pallas_call(kernel, out_shape=jax.ShapeDtypeStruct((rows, rows), bf16)...  121 us

profile of v1, /device:TPU:24, one launch (start us, length us, event | category | flops | bytes accessed | tf_op | source)
XLA Modules:
  0.0 121.2 jit_solution(3023417761533384045)
XLA Ops:
  0.0 120.5 %shard_map.17 = bf16[256,256]{1,0:T(8,128)(2,1)S(1)} custom-call(bf16[256,8192]{1,0:T(8,128)(2,1)} %a_ref.1), custom_call_target="tpu_custom_call" | custom-call | tf_op jit(solution)/shard_map/pallas_call | solution.py:432
  120.5 0.7 copy.3

commit v2 on v0

v2 whole, which is shorter than its diff:
```python
import jax
import jax.numpy as jnp
from jax import lax
from jax.experimental import pallas as pl
from jax.experimental.pallas import tpu as pltpu
from jax.sharding import PartitionSpec as P

MESH = pl.DeviceIdType.MESH
PW = 256
NU = 15
NL = 2
NS = 8
G0 = 5
NG = NS - G0 + 1


def mm(a, b):
    return lax.dot_general(a, b, (((1,), (1,)), ((), ())), preferred_element_type=jnp.float32)


def kernel(a_ref, o_ref, X, Y, W, Pa, Qa, R, PR, far, ld, s_z, r_y, s_d, r_d, r_w, s_p, r_p, s_q, r_r):
    rows, m = a_ref.shape
    ku = NU * PW
    kd = m - ku
    nd = kd // PW
    half = rows // 2
    st = half // NS
    us = rows // NS
    z = lax.axis_index("row")
    c = lax.axis_index("col")
    y = c // 2
    k = c % 2
    sib = 2 * y + 1 - k

    def rcopy(src, dst, ss, rs, row, col):
        return pltpu.make_async_remote_copy(
            src_ref=src, dst_ref=dst, send_sem=ss, recv_sem=rs, device_id={"row": row, "col": col}, device_id_type=MESH)

    def wait_recv(ref, sem):
        pltpu.make_async_copy(ref, ref, sem).wait()

    def up(p):
        return pl.ds(pl.multiple_of(p * PW, 128), PW)

    def dn(p):
        return pl.ds(pl.multiple_of(ku + p * PW, 128), PW)

    def rs_(h, s, n=1):
        return pl.ds(pl.multiple_of(h * half + s * st, st), n * st)

    def ws_(i, s, n=1):
        return pl.ds(pl.multiple_of(i * half + s * st, st), n * st)

    def us_(s):
        return pl.ds(pl.multiple_of(s * us, us), us)

    DALL = pl.ds(ku, kd)
    UALL = pl.ds(0, ku)

    def each(lo, hi, fn):
        lax.fori_loop(lo, hi, lambda i, u: (fn(i), u)[1], 0)

    load = pltpu.make_async_copy(a_ref, X.at[k], ld.at[0])
    load.start()

    def near(sem):
        for dz in (-1, 1):
            @pl.when((z + dz >= 0) & (z + dz <= 3))
            def _():
                for kk in range(2):
                    pl.semaphore_signal(sem, inc=1, device_id={"row": z + dz, "col": 2 * y + kk}, device_id_type=MESH)
        for dc in range(1, 4):
            pl.semaphore_signal(sem, inc=1, device_id={"row": z, "col": (c + dc) % 4}, device_id_type=MESH)

    n_near = jnp.where((z == 0) | (z == 3), 5, 7)
    bar = pltpu.get_barrier_semaphore()
    near(bar)
    pl.semaphore_wait(bar, n_near)

    def z0_u(q):
        return rcopy(a_ref.at[:, up(q)], Y.at[k, :, up(q)], s_z.at[q], r_y.at[q], 1, c)

    def z0_d(p):
        return rcopy(a_ref.at[:, dn(p)], Y.at[k, :, dn(p)], s_z.at[NU + p], r_y.at[NU + p], 1, c)

    def z3_d(t):
        r = rs_(t % 2, t // 2)
        return rcopy(a_ref.at[r, DALL], Y.at[k, r, DALL], s_z.at[t], r_y.at[t], 2, c)

    def z3_u(s):
        r = us_(s)
        return rcopy(a_ref.at[r, UALL], Y.at[k, r, UALL], s_z.at[2 * NS + s], r_y.at[2 * NS + s], 2, c)

    def z1_u(q):
        return rcopy(a_ref.at[:, up(q)], W.at[k, :, up(q)], s_z.at[q], r_w.at[k, q], 2, 2 * y + 1)

    def z2_d(t):
        h, s = t % 2, t // 2
        return rcopy(a_ref.at[rs_(h, s), DALL], W.at[k, ws_(1, s), pl.ds(0, kd)], s_z.at[t], r_w.at[k, NS + s], 1, 2 * y + h)

    @pl.when(z == 0)
    def _():
        each(0, NU - NL, lambda q: z0_u(q).start())
        each(0, nd, lambda p: z0_d(p).start())
        each(NU - NL, NU, lambda q: z0_u(q).start())

    @pl.when(z == 3)
    def _():
        each(0, 2 * NS, lambda t: z3_d(t).start())
        each(0, NS, lambda s: z3_u(s).start())

    x_d = rcopy(a_ref.at[:, DALL], X.at[k, :, DALL], s_d.at[nd], r_d.at[nd], z, sib)
    x_u = rcopy(a_ref.at[:, UALL], X.at[k, :, UALL], s_d.at[nd], r_d.at[nd], z, sib)

    @pl.when(z == 1)
    def _():
        each(0, NU, lambda q: z1_u(q).start())
        x_d.start()

    @pl.when(z == 2)
    def _():
        z2_d(0).start()
        z2_d(1).start()
        x_u.start()

    near(far)

    Pa[...] = jnp.zeros_like(Pa)
    Qa[...] = jnp.zeros_like(Qa)
    load.wait()
    dq = jnp.where(z == 1, 1, 0)

    def diag(p):
        cs = pl.ds(pl.multiple_of(p * 512, 512), 512)
        Qa[dq] += mm(X[k, :, cs], X[k, :, cs])

    each(0, m // 512, diag)

    def slot(owner):
        return (c - owner + 3) % 4

    dsend = rcopy(Qa.at[dq], R.at[slot(z)], s_q.at[NS], r_r.at[slot(z), 0], z, z)

    @pl.when(c != z)
    def _():
        dsend.start()

    def u_fwd(q):
        return rcopy(Y.at[k, :, up(q)], W.at[k, :, up(q)], s_z.at[NU + q], r_w.at[k, q], 2, 2 * y)

    def zU(q):
        wait_recv(Y.at[k, :, up(q)], r_y.at[q])
        u_fwd(q).start()
        Qa[0] += mm(X[k, :, up(q)], Y[k, :, up(q)])

    def d_sib(p):
        return rcopy(Y.at[k, :, dn(p)], Y.at[k, :, dn(p)], s_d.at[p], r_d.at[p], z, sib)

    def zD(p):
        wait_recv(Y.at[k, :, dn(p)], r_y.at[NU + p])
        d_sib(p).start()
        Qa[0] += mm(X[k, :, dn(p)], Y[k, :, dn(p)])

    def p3send(j):
        return rcopy(Pa.at[j, ws_(0, 0, NS)], PR.at[1, rs_(k, 0, NS)], s_p.at[j], r_p.at[k], 2, 2 * y + j)

    def p2send(g, s, n, j):
        return rcopy(Pa.at[j, ws_(1, s, n)], PR.at[0, rs_(k, s, n)], s_p.at[2 + 2 * g + j], r_p.at[2 + 2 * g + k], 2, 2 * y + j)

    def part(i, s, n, j):
        B = X if j == 1 else Y
        r = ws_(i, s, n)
        Pa[j, r, :] = mm(W[0, r, :kd], B[0, :, DALL]) + mm(W[1, r, :kd], B[1, :, DALL])

    def wait_w(i, s):
        for h in range(2):
            wait_recv(W.at[h, ws_(i, s), pl.ds(0, kd)], r_w.at[h, i * NS + s])

    q0send = rcopy(Qa.at[0], R.at[slot(0)], s_q.at[0], r_r.at[slot(0), 0], 1, 0)

    @pl.when(z == 1)
    def _():
        each(0, NU - NL, zU)
        each(0, 8, zD)
        wait_recv(X.at[1 - k, :, DALL], r_d.at[nd])
        each(0, NS, lambda s: wait_w(0, s))
        part(0, 0, NS, 1)
        p3send(1).start()
        each(8, nd - 2, zD)
        each(0, G0, lambda s: wait_w(1, s))
        part(1, 0, G0, 1)
        p2send(0, 0, G0, 1).start()
        each(nd - 2, nd, zD)
        each(0, nd, lambda p: wait_recv(Y.at[1 - k, :, dn(p)], r_d.at[p]))
        part(0, 0, NS, 0)
        p3send(0).start()
        part(1, 0, G0, 0)
        p2send(0, 0, G0, 0).start()

        def last(i):
            @pl.when(i < NL)
            def _():
                zU(NU - NL + i)

            s = G0 + i
            wait_w(1, s)
            for j in range(2):
                part(1, s, 1, j)
                p2send(1 + i, s, 1, j).start()

        each(0, NS - G0, last)

        @pl.when(c != 0)
        def _():
            q0send.start()

    def d_fwd(t):
        h, s = t % 2, t // 2
        return rcopy(Y.at[k, rs_(h, s), DALL], W.at[k, ws_(0, s), pl.ds(0, kd)], s_z.at[2 * NS + t], r_w.at[k, s], 1, 2 * y + h)

    def u_sib(s):
        return rcopy(Y.at[k, us_(s), UALL], Y.at[k, us_(s), UALL], s_d.at[s], r_d.at[s], z, sib)

    def q1send(s):
        return rcopy(Qa.at[1, us_(s)], R.at[c, us_(s)], s_q.at[s], r_r.at[c, s], 3, 2)

    def y2(q):
        for h in range(2):
            wait_recv(W.at[h, :, up(q)], r_w.at[h, q])
        Pa[0] += mm(X[0, :, up(q)], W[0, :, up(q)]) + mm(X[1, :, up(q)], W[1, :, up(q)])

    def y3(q):
        Pa[1] += mm(Y[0, :, up(q)], W[0, :, up(q)]) + mm(Y[1, :, up(q)], W[1, :, up(q)])

    s3send = rcopy(Pa.at[1], R.at[y], s_p.at[0], r_r.at[y, 0], 3, k)

    def grp(g, h):
        return rs_(h, 0, G0) if g == 0 else rs_(h, G0 + g - 1)

    def s2send(g, h):
        r = grp(g, h)
        return rcopy(Pa.at[0, r], R.at[0, r], s_p.at[1 + 2 * g + h], r_r.at[0, 2 * g + h], 2, k)

    @pl.when(z == 2)
    def _():
        def step_d(t):
            wait_recv(Y.at[k, rs_(t % 2, t // 2), DALL], r_y.at[t])
            d_fwd(t).start()

            @pl.when(t == 1)
            def _():
                wait_recv(X.at[1 - k, :, UALL], r_d.at[nd])

            @pl.when((k == 1) & (t >= 1) & (t <= NU))
            def _():
                y2(t - 1)

        each(0, 2 * NS, step_d)
        each(2, 2 * NS, lambda t: z2_d(t).start())
        pl.semaphore_wait(far, n_near)

        def step_u(s):
            wait_recv(Y.at[k, us_(s), UALL], r_y.at[2 * NS + s])
            u_sib(s).start()
            Qa[1, us_(s), :] = mm(Y[k, us_(s), :], X[k])
            q1send(s).start()
            for dq_ in range(2):
                q = 2 * s - 2 + dq_

                @pl.when((k == 0) & (q >= 0) & (q < NU - NL))
                def _():
                    y2(q)

        each(0, NS, step_u)
        each(0, NS, lambda s: wait_recv(Y.at[1 - k, us_(s), UALL], r_d.at[s]))
        each(0, NU - NL, y3)

        def last(q):
            @pl.when(k == 0)
            def _():
                y2(q)

            y3(q)

        each(NU - NL, NU, last)
        for h in range(2):
            wait_recv(PR.at[1, rs_(h, 0, NS)], r_p.at[h])
        Pa[1] += PR[1]
        s3send.start()
        for g in range(NG):
            for h in range(2):
                r = grp(g, h)
                wait_recv(PR.at[0, r], r_p.at[2 + 2 * g + h])
                Pa[0, r, :] += PR[0, r, :]

                @pl.when(y == 1)
                def _():
                    s2send(g, h).start()

    @pl.when(z != 2)
    def _():
        pl.semaphore_wait(far, n_near)

    @pl.when(c > z)
    def _():
        o_ref[...] = jnp.zeros_like(o_ref)

    @pl.when(c == z)
    def _():
        for i in range(3):
            wait_recv(R.at[i], r_r.at[i, 0])
        total = Qa[dq] + R[0] + R[1] + R[2]
        diff = lax.broadcasted_iota(jnp.int32, (rows, rows), 0) - lax.broadcasted_iota(jnp.int32, (rows, rows), 1)
        o_ref[...] = jnp.where(diff >= 0, total, 0.0).astype(o_ref.dtype)

    @pl.when((z == 1) & (c == 0))
    def _():
        for i in range(3):
            wait_recv(R.at[i], r_r.at[i, 0])
        o_ref[...] = (Qa[0] + R[0] + R[1] + R[2]).astype(o_ref.dtype)

    @pl.when((z == 2) & (y == 0))
    def _():
        for g in range(NG):
            for h in range(2):
                wait_recv(R.at[0, grp(g, h)], r_r.at[0, 2 * g + h])
        o_ref[...] = (Pa[0] + R[0]).astype(o_ref.dtype)

    @pl.when((z == 3) & (c == 2))
    def _():
        def take(s):
            for i in range(4):
                wait_recv(R.at[i, us_(s)], r_r.at[i, s])

        each(0, NS, take)
        o_ref[...] = (R[0] + R[1] + R[2] + R[3]).astype(o_ref.dtype)

    @pl.when((z == 3) & (y == 0))
    def _():
        for i in range(2):
            wait_recv(R.at[i], r_r.at[i, 0])
        o_ref[...] = (R[0] + R[1]).astype(o_ref.dtype)

    @pl.when(c != z)
    def _():
        dsend.wait_send()

    @pl.when(z == 0)
    def _():
        each(0, NU, lambda q: z0_u(q).wait_send())
        each(0, nd, lambda p: z0_d(p).wait_send())

    @pl.when(z == 3)
    def _():
        each(0, 2 * NS, lambda t: z3_d(t).wait_send())
        each(0, NS, lambda s: z3_u(s).wait_send())

    @pl.when(z == 1)
    def _():
        x_d.wait_send()
        each(0, NU, lambda q: z1_u(q).wait_send())
        each(0, NU, lambda q: u_fwd(q).wait_send())
        each(0, nd, lambda p: d_sib(p).wait_send())
        for j in range(2):
            p3send(j).wait_send()
            p2send(0, 0, G0, j).wait_send()
            for g in range(1, NG):
                p2send(g, G0 + g - 1, 1, j).wait_send()

        @pl.when(c != 0)
        def _():
            q0send.wait_send()

    @pl.when(z == 2)
    def _():
        x_u.wait_send()
        each(0, 2 * NS, lambda t: z2_d(t).wait_send())
        each(0, 2 * NS, lambda t: d_fwd(t).wait_send())
        each(0, NS, lambda s: u_sib(s).wait_send())
        each(0, NS, lambda s: q1send(s).wait_send())
        s3send.wait_send()

        @pl.when(y == 1)
        def _():
            for g in range(NG):
                for h in range(2):
                    s2send(g, h).wait_send()


def solution(mesh):
    def local_fn(a_local):
        rows, m = a_local.shape
        nd = m // PW - NU
        wide = max(NU, nd) * PW
        f32, bf16 = jnp.float32, jnp.bfloat16
        dma = pltpu.SemaphoreType.DMA
        return pl.pallas_call(
            kernel,
            out_shape=jax.ShapeDtypeStruct((rows, rows), bf16),
            in_specs=[pl.BlockSpec(memory_space=pl.ANY)],
            out_specs=pl.BlockSpec(memory_space=pltpu.VMEM),
            scratch_shapes=[
                pltpu.VMEM((2, rows, m), bf16),
                pltpu.VMEM((2, rows, m), bf16),
                pltpu.VMEM((2, rows, wide), bf16),
                pltpu.VMEM((2, rows, rows), f32),
                pltpu.VMEM((2, rows, rows), f32),
                pltpu.VMEM((4, rows, rows), f32),
                pltpu.VMEM((2, rows, rows), f32),
                pltpu.SemaphoreType.REGULAR,
                dma((1,)), dma((2 * max(NU, 2 * NS) + 2,)), dma((NU + nd,)), dma((nd + 1,)), dma((nd + 1,)),
                dma((2, max(NU, 2 * NS))), dma((2 + 2 * NG,)), dma((2 + 2 * NG,)), dma((NS + 1,)),
                dma((4, max(NS, 2 * NG))),
            ],
            compiler_params=pltpu.CompilerParams(
                collective_id=0, has_side_effects=True, vmem_limit_bytes=50 * 1024 * 1024),
        )(a_local)

    part_spec = P(("batch", "row"), "col")
    return jax.shard_map(local_fn, mesh=mesh, in_specs=(part_spec,), out_specs=part_spec, check_vma=False)
```

time: 623 us -> 120 us (0.19)
  the two profiles are of different devices: /device:TPU:24 before, /device:TPU:8 now
where the time goes in v2:
time: 120 us
  Pallas kernels  119 us (99%)
    pallas_call x1, Pallas kernels, local_fn(): pl.pallas_call(kernel, out_shape=jax.ShapeDtypeStruct((rows, rows), bf16)...  119 us

profile of v2, /device:TPU:8, one launch (start us, length us, event | category | flops | bytes accessed | tf_op | source)
XLA Modules:
  0.0 119.5 jit_solution(13837442867658741489)
XLA Ops:
  0.0 118.9 %shard_map.17 = bf16[256,256]{1,0:T(8,128)(2,1)S(1)} custom-call(bf16[256,8192]{1,0:T(8,128)(2,1)} %a_ref.1), custom_call_target="tpu_custom_call" | custom-call | tf_op jit(solution)/shard_map/pallas_call | solution.py:397
  118.9 0.7 copy.3

commit v3 on v2

--- a/solution.py
+++ b/solution.py
@@ -10,7 +10,7 @@
 NU = 15
 NL = 2
 NS = 8
-G0 = 5
+G0 = 6
 NG = NS - G0 + 1
 
 
@@ -167,10 +167,21 @@
     def p2send(g, s, n, j):
         return rcopy(Pa.at[j, ws_(1, s, n)], PR.at[0, rs_(k, s, n)], s_p.at[2 + 2 * g + j], r_p.at[2 + 2 * g + k], 2, 2 * y + j)
 
-    def part(i, s, n, j):
+    def part(i, s, n, j, lo, hi, new=True):
         B = X if j == 1 else Y
         r = ws_(i, s, n)
-        Pa[j, r, :] = mm(W[0, r, :kd], B[0, :, DALL]) + mm(W[1, r, :kd], B[1, :, DALL])
+        w, b = pl.ds(lo, hi - lo), pl.ds(ku + lo, hi - lo)
+        acc = mm(W[0, r, w], B[0, :, b]) + mm(W[1, r, w], B[1, :, b])
+        if new:
+            Pa[j, r, :] = acc
+        else:
+            Pa[j, r, :] += acc
+
+    def thin(s, j):
+        B = X if j == 1 else Y
+        r = ws_(1, s)
+        acc = mm(B[0, :, DALL], W[0, r, :kd]) + mm(B[1, :, DALL], W[1, r, :kd])
+        Pa[j, r, :] = acc.T
 
     def wait_w(i, s):
         for h in range(2):
@@ -180,39 +191,38 @@
 
     @pl.when(z == 1)
     def _():
+        early = nd - 2
         each(0, NU - NL, zU)
         each(0, 8, zD)
         wait_recv(X.at[1 - k, :, DALL], r_d.at[nd])
         each(0, NS, lambda s: wait_w(0, s))
-        part(0, 0, NS, 1)
+        part(0, 0, NS, 1, 0, kd)
         p3send(1).start()
-        each(8, nd - 2, zD)
+        each(8, early, zD)
         each(0, G0, lambda s: wait_w(1, s))
-        part(1, 0, G0, 1)
+        part(1, 0, G0, 1, 0, kd)
         p2send(0, 0, G0, 1).start()
-        each(nd - 2, nd, zD)
-        each(0, nd, lambda p: wait_recv(Y.at[1 - k, :, dn(p)], r_d.at[p]))
-        part(0, 0, NS, 0)
+        each(0, early, lambda p: wait_recv(Y.at[1 - k, :, dn(p)], r_d.at[p]))
+        part(0, 0, NS + G0, 0, 0, early * PW)
+        each(early, nd, zD)
+        each(early, nd, lambda p: wait_recv(Y.at[1 - k, :, dn(p)], r_d.at[p]))
+        part(0, 0, NS + G0, 0, early * PW, kd, new=False)
         p3send(0).start()
-        part(1, 0, G0, 0)
-        p2send(0, 0, G0, 0).start()
-
-        def last(i):
-            @pl.when(i < NL)
-            def _():
-                zU(NU - NL + i)
-
-            s = G0 + i
-            wait_w(1, s)
-            for j in range(2):
-                part(1, s, 1, j)
-                p2send(1 + i, s, 1, j).start()
-
-        each(0, NS - G0, last)
+        each(NU - NL, NU, zU)
 
         @pl.when(c != 0)
         def _():
             q0send.start()
+
+        p2send(0, 0, G0, 0).start()
+
+        def last(s):
+            wait_w(1, s)
+            for j in (1, 0):
+                thin(s, j)
+                p2send(1 + s - G0, s, 1, j).start()
+
+        each(G0, NS, last)
 
     def d_fwd(t):
         h, s = t % 2, t // 2
@@ -282,10 +292,10 @@
 
             y3(q)
 
-        each(NU - NL, NU, last)
         for h in range(2):
             wait_recv(PR.at[1, rs_(h, 0, NS)], r_p.at[h])
         Pa[1] += PR[1]
+        each(NU - NL, NU, last)
         s3send.start()
         for g in range(NG):
             for h in range(2):

time: 120 us -> 115 us (0.958)
  the two profiles are of different devices: /device:TPU:8 before, /device:TPU:24 now
where the time goes in v3:
time: 115 us; the launch traced here: 114 us
  Pallas kernels  113 us (98%)
    pallas_call x1, Pallas kernels, local_fn(): pl.pallas_call(kernel, out_shape=jax.ShapeDtypeStruct((rows, rows), bf16)...  113 us

profile of v3, /device:TPU:24, one launch (start us, length us, event | category | flops | bytes accessed | tf_op | source)
XLA Modules:
  0.0 113.7 jit_solution(7240030605348306027)
XLA Ops:
  0.0 113.1 %shard_map.17 = bf16[256,256]{1,0:T(8,128)(2,1)S(1)} custom-call(bf16[256,8192]{1,0:T(8,128)(2,1)} %a_ref.1), custom_call_target="tpu_custom_call" | custom-call | tf_op jit(solution)/shard_map/pallas_call | solution.py:407
  113.1 0.7 copy.3

commit v4 on v2

v4 whole, which is shorter than its diff:
```python
import jax
import jax.numpy as jnp
from jax import lax
from jax.experimental import pallas as pl
from jax.experimental.pallas import tpu as pltpu
from jax.sharding import PartitionSpec as P

MESH = pl.DeviceIdType.MESH
PW = 256
NU = 15
XU = 128
NS = 8
GROUPS = ((0, 5), (5, 2), (7, 1))


def mm(a, b):
    return lax.dot_general(a, b, (((1,), (1,)), ((), ())), preferred_element_type=jnp.float32)


def mn(a, b):
    return lax.dot_general(a, b, (((1,), (0,)), ((), ())), preferred_element_type=jnp.float32)


def kernel(a_ref, o_ref, X, Y, W, T, Pa, Qa, R, PR, far, ld, s_z, r_y, s_d, r_d, r_w, s_p, r_p, s_q, r_r):
    rows, m = a_ref.shape
    ku = NU * PW + XU
    kd = m - ku
    nd, xd = kd // PW, kd % PW
    half = rows // 2
    st = half // NS
    us = rows // NS
    z = lax.axis_index("row")
    c = lax.axis_index("col")
    y = c // 2
    k = c % 2
    sib = 2 * y + 1 - k

    def rcopy(src, dst, ss, rs, row, col):
        return pltpu.make_async_remote_copy(
            src_ref=src, dst_ref=dst, send_sem=ss, recv_sem=rs, device_id={"row": row, "col": col}, device_id_type=MESH)

    def wait_recv(ref, sem):
        pltpu.make_async_copy(ref, ref, sem).wait()

    def up(p, w=PW):
        return pl.ds(pl.multiple_of(p * PW, 128), w)

    def dn(p, w=PW):
        return pl.ds(pl.multiple_of(ku + p * PW, 128), w)

    def rs_(h, s, n=1):
        return pl.ds(pl.multiple_of(h * half + s * st, st), n * st)

    def us_(s):
        return pl.ds(pl.multiple_of(s * us, us), us)

    DALL = pl.ds(ku, kd)
    UALL = pl.ds(0, ku)
    C0, C1 = pl.ds(0, half), pl.ds(half, half)
    COLS = (C0, C1)

    def each(lo, hi, fn):
        lax.fori_loop(lo, hi, lambda i, u: (fn(i), u)[1], 0)

    load = pltpu.make_async_copy(a_ref, X.at[k], ld.at[0])
    load.start()

    def near(sem):
        for dz in (-1, 1):
            @pl.when((z + dz >= 0) & (z + dz <= 3))
            def _():
                for kk in range(2):
                    pl.semaphore_signal(sem, inc=1, device_id={"row": z + dz, "col": 2 * y + kk}, device_id_type=MESH)
        for dc in range(1, 4):
            pl.semaphore_signal(sem, inc=1, device_id={"row": z, "col": (c + dc) % 4}, device_id_type=MESH)

    n_near = jnp.where((z == 0) | (z == 3), 5, 7)
    bar = pltpu.get_barrier_semaphore()
    near(bar)
    pl.semaphore_wait(bar, n_near)

    def z0_u(q, w=PW):
        return rcopy(a_ref.at[:, up(q, w)], Y.at[k, :, up(q, w)], s_z.at[q], r_y.at[q], 1, c)

    def z0_d(t):
        r = rs_(0, t)
        return rcopy(a_ref.at[r, DALL], Y.at[k, r, DALL], s_z.at[2 * NS + t], r_y.at[2 * NS + t], 1, c)

    def z3_d(t):
        r = rs_(t % 2, t // 2)
        return rcopy(a_ref.at[r, DALL], Y.at[k, r, DALL], s_z.at[t], r_y.at[t], 2, c)

    def z3_u(s):
        r = us_(s)
        return rcopy(a_ref.at[r, UALL], Y.at[k, r, UALL], s_z.at[2 * NS + s], r_y.at[2 * NS + s], 2, c)

    def z1_u(q, w=PW):
        return rcopy(a_ref.at[:, up(q, w)], W.at[k, :, up(q, w)], s_z.at[q], r_w.at[k, q], 2, 2 * y + 1)

    def z2_d(t):
        h, s = t % 2, t // 2
        return rcopy(a_ref.at[rs_(h, s), DALL], W.at[k, rs_(1, s), pl.ds(0, kd)], s_z.at[t], r_w.at[k, NS + s], 1, 2 * y + h)

    @pl.when(z == 0)
    def _():
        each(0, NU, lambda q: z0_u(q).start())
        z0_u(NU, XU).start()
        each(0, 2 * NS, lambda t: z0_d(t).start())

    @pl.when(z == 3)
    def _():
        each(0, 2 * NS, lambda t: z3_d(t).start())
        each(0, NS, lambda s: z3_u(s).start())

    x_d = rcopy(a_ref.at[:, DALL], X.at[k, :, DALL], s_d.at[2 * NS], r_d.at[2 * NS], z, sib)
    x_u = rcopy(a_ref.at[:, UALL], X.at[k, :, UALL], s_d.at[2 * NS], r_d.at[2 * NS], z, sib)

    @pl.when(z == 1)
    def _():
        each(0, NU, lambda q: z1_u(q).start())
        z1_u(NU, XU).start()
        x_d.start()

    @pl.when(z == 2)
    def _():
        z2_d(0).start()
        z2_d(1).start()
        x_u.start()

    near(far)

    Pa[...] = jnp.zeros_like(Pa)
    Qa[...] = jnp.zeros_like(Qa)
    load.wait()
    dq = jnp.where(z == 1, 1, 0)

    def diag(p):
        cs = pl.ds(pl.multiple_of(p * 512, 512), 512)
        Qa[dq] += mm(X[k, :, cs], X[k, :, cs])

    each(0, m // 512, diag)

    def slot(owner):
        return (c - owner + 3) % 4

    dsend = rcopy(Qa.at[dq], R.at[slot(z)], s_q.at[NS], r_r.at[slot(z), 0], z, z)

    @pl.when(c != z)
    def _():
        dsend.start()

    def u_fwd(q, w=PW):
        return rcopy(Y.at[k, :, up(q, w)], W.at[k, :, up(q, w)], s_z.at[2 * NS + q], r_w.at[k, q], 2, 2 * y)

    def zU(q, w=PW):
        wait_recv(Y.at[k, :, up(q, w)], r_y.at[q])
        Qa[0] += mm(X[k, :, up(q, w)], Y[k, :, up(q, w)])

    def turn(p, w=PW):
        for h in range(2):
            T[h, up(p, w), 2 * half:] = X[h, :, dn(p, w)].T

    def d_sib(t):
        return rcopy(Y.at[k, rs_(0, t), DALL], Y.at[k, rs_(0, t), DALL], s_d.at[t], r_d.at[t], z, sib)

    def zD(t):
        wait_recv(Y.at[k, rs_(0, t), DALL], r_y.at[2 * NS + t])
        d_sib(t).start()

    def wait_sib(lo, hi):
        each(lo, hi, lambda t: wait_recv(Y.at[1 - k, rs_(0, t), DALL], r_d.at[t]))

    def turn_half(b):
        for h in range(2):
            T[h, :, b * half:(b + 1) * half] = Y[h, b * half:(b + 1) * half, DALL].T

    def q_half(b):
        Qa[0, :, COLS[b]] += mm(X[k, :, DALL], Y[k, b * half:(b + 1) * half, DALL])

    def wait_w(i, lo, n):
        def one(s):
            for h in range(2):
                wait_recv(W.at[h, rs_(i, s), pl.ds(0, kd)], r_w.at[h, i * NS + s])

        each(lo, lo + n, one)

    def send1(i, s, n, j, cols, ss, rs):
        src = Pa.at[j, rs_(1 - i, s, n), cols]
        return rcopy(src, PR.at[i, rs_(k, s, n), cols], s_p.at[ss], r_p.at[k, rs], 2, 2 * y + j)

    CA = pl.ds(0, rows)
    m31 = send1(1, 0, NS, 1, CA, 0, 0)
    m30a = send1(1, 0, NS, 0, C0, 1, 0)
    m30b = [send1(1, 2 * u, 2, 0, C1, 2 + u, 4 + u) for u in range(4)]
    m21 = [send1(0, s, n, 1, CA, 6 + g, 1 + g) for g, (s, n) in enumerate(GROUPS)]
    m20a = [send1(0, s, n, 0, C0, 9 + g, 1 + g) for g, (s, n) in enumerate(GROUPS[:2])]
    m20b = send1(0, 0, NS - 1, 0, C1, 11, 8)
    m20c = send1(0, NS - 1, 1, 0, CA, 12, 3)
    out1 = [m31, m30a, *m30b, *m21, *m20a, m20b, m20c]

    def part(r, j, cols, tcols):
        Pa[j, r, cols] = mn(W[0, r, :kd], T[0, :, tcols]) + mn(W[1, r, :kd], T[1, :, tcols])

    TJ1 = slice(2 * half, 4 * half)

    def q0send(b):
        return rcopy(Qa.at[0, :, COLS[b]], R.at[slot(0), :, COLS[b]], s_q.at[b], r_r.at[slot(0), b], 1, 0)

    @pl.when(z == 1)
    def _():
        wait_recv(X.at[1 - k, :, DALL], r_d.at[2 * NS])

        def step_u(q):
            zU(q)

            @pl.when(q < 5)
            def _():
                u_fwd(q).start()

            turn(q)

        each(0, NU, step_u)
        zU(NU, XU)
        each(NU, nd, turn)
        if xd:
            turn(nd, xd)
        each(0, 4, zD)
        wait_w(0, 0, NS)
        part(rs_(0, 0, NS), 1, CA, TJ1)
        m31.start()
        each(5, 10, lambda q: u_fwd(q).start())
        each(4, 8, zD)
        wait_sib(0, 8)
        turn_half(0)
        part(rs_(0, 0, NS), 0, C0, slice(0, half))
        m30a.start()
        each(10, NU, lambda q: u_fwd(q).start())
        u_fwd(NU, XU).start()
        q_half(0)

        @pl.when(c != 0)
        def _():
            q0send(0).start()

        for g, stop in ((0, 11), (1, 15)):
            each(8 if g == 0 else 11, stop, zD)
            s, n = GROUPS[g]
            wait_w(1, s, n)
            part(rs_(1, s, n), 1, CA, TJ1)
            m21[g].start()
            part(rs_(1, s, n), 0, C0, slice(0, half))
            m20a[g].start()
        zD(15)
        wait_sib(8, 16)
        r = pl.ds(0, rows - st)
        Pa[0, r, C1] = mm(W[0, r, :kd], Y[0, half:, DALL]) + mm(W[1, r, :kd], Y[1, half:, DALL])
        for x in m30b:
            x.start()
        m20b.start()
        q_half(1)

        @pl.when(c != 0)
        def _():
            q0send(1).start()

        turn_half(1)
        s, n = GROUPS[2]
        wait_w(1, s, n)
        part(rs_(1, s, n), 1, CA, TJ1)
        m21[2].start()
        part(rs_(1, s, n), 0, CA, slice(0, rows))
        m20c.start()

    def d_fwd(t):
        h, s = t % 2, t // 2
        return rcopy(Y.at[k, rs_(h, s), DALL], W.at[k, rs_(0, s), pl.ds(0, kd)], s_z.at[2 * NS + t], r_w.at[k, s], 1, 2 * y + h)

    def u_sib(s):
        return rcopy(Y.at[k, us_(s), UALL], Y.at[k, us_(s), UALL], s_d.at[s], r_d.at[s], z, sib)

    def q1send(s):
        return rcopy(Qa.at[1, us_(s)], R.at[c, us_(s)], s_q.at[s], r_r.at[c, s], 3, 2)

    def y2(q, w=PW):
        for h in range(2):
            wait_recv(W.at[h, :, up(q, w)], r_w.at[h, q])
        Pa[0] += mm(X[0, :, up(q, w)], W[0, :, up(q, w)]) + mm(X[1, :, up(q, w)], W[1, :, up(q, w)])

    def y3(b, q, w=PW):
        r = pl.ds(b * half, half)
        Pa[1, r, :] += mm(Y[0, r, up(q, w)], W[0, :, up(q, w)]) + mm(Y[1, r, up(q, w)], W[1, :, up(q, w)])

    def wait_ysib(s):
        wait_recv(Y.at[1 - k, us_(s), UALL], r_d.at[s])

    def s3(r, cols, n):
        return rcopy(Pa.at[1, r, cols], R.at[y, r, cols], s_p.at[n], r_r.at[y, n], 3, k)

    s3_a = [s3(pl.ds(b * half, half), C0, b) for b in range(2)]
    s3_b = [[s3(rs_(h, 2 * u, 2), C1, 2 + 4 * h + u) for u in range(4)] for h in range(2)]

    def s3_k1(s):
        return s3(us_(s), CA, s)

    def s2(h, s, n, cols, i):
        r = rs_(h, s, n)
        return rcopy(Pa.at[0, r, cols], R.at[0, r, cols], s_p.at[10 + 3 * h + i], r_r.at[0, 3 * h + i], 2, k)

    s2_k1 = [[s2(h, s, n, CA, i) for i, (s, n) in enumerate(GROUPS)] for h in range(2)]
    s2_k0 = [[s2(h, 0, NS - 1, C0, 0), s2(h, 0, NS - 1, C1, 1), s2(h, NS - 1, 1, CA, 2)] for h in range(2)]

    def add(i, r, cols, sem):
        wait_recv(PR.at[i, r, cols], sem)
        Pa[i, r, cols] += PR[i, r, cols]

    def y1_start(x):
        @pl.when(y == 1)
        def _():
            x.start()

    def strip31(s):
        wait_ysib(s)
        r = us_(s)
        Pa[1, r, :] = PR[1, r, :] + mm(Y[0, r, UALL], W[0, :, :ku]) + mm(Y[1, r, UALL], W[1, :, :ku])
        s3_k1(s).start()

    @pl.when(z == 2)
    def _():
        def step_d(t):
            wait_recv(Y.at[k, rs_(t % 2, t // 2), DALL], r_y.at[t])
            d_fwd(t).start()

            @pl.when(t == 1)
            def _():
                wait_recv(X.at[1 - k, :, UALL], r_d.at[2 * NS])

            @pl.when((k == 1) & (t >= 1))
            def _():
                y2(t - 1)

        each(0, 2 * NS, step_d)
        each(2, 2 * NS, lambda t: z2_d(t).start())

        @pl.when(k == 1)
        def _():
            y2(NU, XU)

        pl.semaphore_wait(far, n_near)

        def step_u(s):
            wait_recv(Y.at[k, us_(s), UALL], r_y.at[2 * NS + s])
            u_sib(s).start()
            Qa[1, us_(s), :] = mm(Y[k, us_(s), :], X[k])
            q1send(s).start()

            @pl.when((k == 0) & (s >= 1))
            def _():
                y2(2 * s - 2)
                y2(2 * s - 1)

            @pl.when((k == 0) & (s == 4))
            def _():
                each(0, 4, wait_ysib)
                each(0, 6, lambda q: y3(0, q))

            @pl.when((k == 0) & (s >= 4))
            def _():
                y3(0, 2 * s - 2)
                y3(0, 2 * s - 1)

            @pl.when((k == 1) & (s == 2))
            def _():
                for h in range(2):
                    wait_recv(PR.at[1, rs_(h, 0, NS)], r_p.at[h, 0])

            @pl.when((k == 1) & (s >= 2))
            def _():
                strip31(s - 2)

        each(0, NS, step_u)

        @pl.when(k == 1)
        def _():
            strip31(NS - 2)
            strip31(NS - 1)
            for i, (s, n) in enumerate(GROUPS):
                for h in range(2):
                    add(0, rs_(h, s, n), CA, r_p.at[h, 1 + i])
                    y1_start(s2_k1[h][i])

        @pl.when(k == 0)
        def _():
            y2(NU - 1)
            y2(NU, XU)
            y3(0, NU - 1)
            y3(0, NU, XU)
            add(1, pl.ds(0, half), C0, r_p.at[0, 0])
            s3_a[0].start()
            each(4, NS, wait_ysib)
            each(0, NU, lambda q: y3(1, q))
            y3(1, NU, XU)
            add(1, pl.ds(half, half), C0, r_p.at[1, 0])
            s3_a[1].start()
            for h in range(2):
                for g, (s, n) in enumerate(GROUPS[:2]):
                    add(0, rs_(h, s, n), C0, r_p.at[h, 1 + g])
                y1_start(s2_k0[h][0])
            for u in range(4):
                for h in range(2):
                    add(1, rs_(h, 2 * u, 2), C1, r_p.at[h, 4 + u])
                    s3_b[h][u].start()
            for h in range(2):
                add(0, rs_(h, 0, NS - 1), C1, r_p.at[h, 8])
                y1_start(s2_k0[h][1])
            for h in range(2):
                add(0, rs_(h, NS - 1), CA, r_p.at[h, 3])
                y1_start(s2_k0[h][2])

    @pl.when(z != 2)
    def _():
        pl.semaphore_wait(far, n_near)

    @pl.when(c > z)
    def _():
        o_ref[...] = jnp.zeros_like(o_ref)

    @pl.when(c == z)
    def _():
        for i in range(3):
            wait_recv(R.at[i], r_r.at[i, 0])
        total = Qa[dq] + R[0] + R[1] + R[2]
        diff = lax.broadcasted_iota(jnp.int32, (rows, rows), 0) - lax.broadcasted_iota(jnp.int32, (rows, rows), 1)
        o_ref[...] = jnp.where(diff >= 0, total, 0.0).astype(o_ref.dtype)

    @pl.when((z == 1) & (c == 0))
    def _():
        for i in range(3):
            for b in range(2):
                wait_recv(R.at[i, :, COLS[b]], r_r.at[i, b])
        o_ref[...] = (Qa[0] + R[0] + R[1] + R[2]).astype(o_ref.dtype)

    @pl.when((z == 2) & (y == 0))
    def _():
        @pl.when(k == 0)
        def _():
            for h in range(2):
                wait_recv(R.at[0, rs_(h, 0, NS - 1), C0], r_r.at[0, 3 * h])
                wait_recv(R.at[0, rs_(h, 0, NS - 1), C1], r_r.at[0, 3 * h + 1])
                wait_recv(R.at[0, rs_(h, NS - 1)], r_r.at[0, 3 * h + 2])

        @pl.when(k == 1)
        def _():
            for h in range(2):
                for i, (s, n) in enumerate(GROUPS):
                    wait_recv(R.at[0, rs_(h, s, n)], r_r.at[0, 3 * h + i])

        o_ref[...] = (Pa[0] + R[0]).astype(o_ref.dtype)

    @pl.when((z == 3) & (c == 2))
    def _():
        def take(s):
            for i in range(4):
                wait_recv(R.at[i, us_(s)], r_r.at[i, s])

        each(0, NS, take)
        o_ref[...] = (R[0] + R[1] + R[2] + R[3]).astype(o_ref.dtype)

    @pl.when((z == 3) & (y == 0))
    def _():
        for i in range(2):
            @pl.when(k == 0)
            def _():
                for b in range(2):
                    wait_recv(R.at[i, pl.ds(b * half, half), C0], r_r.at[i, b])
                for h in range(2):
                    for u in range(4):
                        wait_recv(R.at[i, rs_(h, 2 * u, 2), C1], r_r.at[i, 2 + 4 * h + u])

            @pl.when(k == 1)
            def _():
                each(0, NS, lambda s: wait_recv(R.at[i, us_(s)], r_r.at[i, s]))

        o_ref[...] = (R[0] + R[1]).astype(o_ref.dtype)

    @pl.when(c != z)
    def _():
        dsend.wait_send()

    @pl.when(z == 0)
    def _():
        each(0, NU, lambda q: z0_u(q).wait_send())
        z0_u(NU, XU).wait_send()
        each(0, 2 * NS, lambda t: z0_d(t).wait_send())

    @pl.when(z == 3)
    def _():
        each(0, 2 * NS, lambda t: z3_d(t).wait_send())
        each(0, NS, lambda s: z3_u(s).wait_send())

    @pl.when(z == 1)
    def _():
        x_d.wait_send()
        each(0, NU, lambda q: z1_u(q).wait_send())
        z1_u(NU, XU).wait_send()
        each(0, NU, lambda q: u_fwd(q).wait_send())
        u_fwd(NU, XU).wait_send()
        each(0, 2 * NS, lambda t: d_sib(t).wait_send())
        for x in out1:
            x.wait_send()

        @pl.when(c != 0)
        def _():
            for b in range(2):
                q0send(b).wait_send()

    @pl.when(z == 2)
    def _():
        x_u.wait_send()
        each(0, 2 * NS, lambda t: z2_d(t).wait_send())
        each(0, 2 * NS, lambda t: d_fwd(t).wait_send())
        each(0, NS, lambda s: u_sib(s).wait_send())
        each(0, NS, lambda s: q1send(s).wait_send())

        @pl.when(k == 0)
        def _():
            for x in [*s3_a, *s3_b[0], *s3_b[1]]:
                x.wait_send()

            @pl.when(y == 1)
            def _():
                for x in [*s2_k0[0], *s2_k0[1]]:
                    x.wait_send()

        @pl.when(k == 1)
        def _():
            each(0, NS, lambda s: s3_k1(s).wait_send())

            @pl.when(y == 1)
            def _():
                for x in [*s2_k1[0], *s2_k1[1]]:
                    x.wait_send()


def solution(mesh):
    def local_fn(a_local):
        rows, m = a_local.shape
        kd = m - NU * PW - XU
        f32, bf16 = jnp.float32, jnp.bfloat16
        dma = pltpu.SemaphoreType.DMA
        return pl.pallas_call(
            kernel,
            out_shape=jax.ShapeDtypeStruct((rows, rows), bf16),
            in_specs=[pl.BlockSpec(memory_space=pl.ANY)],
            out_specs=pl.BlockSpec(memory_space=pltpu.VMEM),
            scratch_shapes=[
                pltpu.VMEM((2, rows, m), bf16),
                pltpu.VMEM((2, rows, m), bf16),
                pltpu.VMEM((2, rows, kd), bf16),
                pltpu.VMEM((2, kd, 2 * rows), bf16),
                pltpu.VMEM((2, rows, rows), f32),
                pltpu.VMEM((2, rows, rows), f32),
                pltpu.VMEM((4, rows, rows), f32),
                pltpu.VMEM((2, rows, rows), f32),
                pltpu.SemaphoreType.REGULAR,
                dma((1,)), dma((4 * NS,)), dma((4 * NS,)), dma((2 * NS + 1,)), dma((2 * NS + 1,)),
                dma((2, 2 * NS)), dma((16,)), dma((2, 9)), dma((NS + 1,)), dma((4, 10)),
            ],
            compiler_params=pltpu.CompilerParams(
                collective_id=0, has_side_effects=True, vmem_limit_bytes=56 * 1024 * 1024),
        )(a_local)

    part_spec = P(("batch", "row"), "col")
    return jax.shard_map(local_fn, mesh=mesh, in_specs=(part_spec,), out_specs=part_spec, check_vma=False)
```

time: 120 us -> 112 us (0.933)
  the two profiles are of different devices: /device:TPU:8 before, /device:TPU:18 now
where the time goes in v4:
time: 112 us
  Pallas kernels  111 us (99%)
  local copies, waits for them, and re-layouts  1.57 us (1%)
    pallas_call x1, Pallas kernels, local_fn(): pl.pallas_call(kernel, out_shape=jax.ShapeDtypeStruct((rows, rows), bf16)...  111 us

profile of v4, /device:TPU:18, one launch (start us, length us, event | category | flops | bytes accessed | tf_op | source)
XLA Modules:
  0.0 112.1 jit_solution(18009430167380437673)
XLA Ops:
  0.0 110.5 %shard_map.17 = bf16[256,256]{1,0:T(8,128)(2,1)} custom-call(bf16[256,8192]{1,0:T(8,128)(2,1)} %a_ref.1), custom_call_target="tpu_custom_call" | custom-call | tf_op jit(solution)/shard_map/pallas_call | solution.py:550
  110.5 1.6 %copy.3 = bf16[256,256]{1,0:T(8,128)(2,1)} copy(bf16[256,256]{1,0:T(8,128)(2,1)} %shard_map.17) | data formatting | bytes 262144

commit v5 on v4

--- a/solution.py
+++ b/solution.py
@@ -10,7 +10,6 @@
 NU = 15
 XU = 128
 NS = 8
-GROUPS = ((0, 5), (5, 2), (7, 1))
 
 
 def mm(a, b):
@@ -21,7 +20,7 @@
     return lax.dot_general(a, b, (((1,), (0,)), ((), ())), preferred_element_type=jnp.float32)
 
 
-def kernel(a_ref, o_ref, X, Y, W, T, Pa, Qa, R, PR, far, ld, s_z, r_y, s_d, r_d, r_w, s_p, r_p, s_q, r_r):
+def kernel(a_ref, o_ref, X, Y, W, T0, T1, Pa, Pb, Qa, Qb, R, PR, far, ld, s_z, r_y, s_d, r_d, r_w, s_p, r_p, s_q, r_r):
     rows, m = a_ref.shape
     ku = NU * PW + XU
     kd = m - ku
@@ -131,6 +130,7 @@
 
     Pa[...] = jnp.zeros_like(Pa)
     Qa[...] = jnp.zeros_like(Qa)
+    Qb[...] = jnp.zeros_like(Qb)
     load.wait()
     dq = jnp.where(z == 1, 1, 0)
 
@@ -154,11 +154,13 @@
 
     def zU(q, w=PW):
         wait_recv(Y.at[k, :, up(q, w)], r_y.at[q])
-        Qa[0] += mm(X[k, :, up(q, w)], Y[k, :, up(q, w)])
+        v = mm(X[k, :, up(q, w)], Y[k, :, up(q, w)])
+        Qb[0] += v[:, :half]
+        Qb[1] += v[:, half:]
 
     def turn(p, w=PW):
         for h in range(2):
-            T[h, up(p, w), 2 * half:] = X[h, :, dn(p, w)].T
+            T1[h, up(p, w), :] = X[h, :, dn(p, w)].T
 
     def d_sib(t):
         return rcopy(Y.at[k, rs_(0, t), DALL], Y.at[k, rs_(0, t), DALL], s_d.at[t], r_d.at[t], z, sib)
@@ -167,15 +169,8 @@
         wait_recv(Y.at[k, rs_(0, t), DALL], r_y.at[2 * NS + t])
         d_sib(t).start()
 
-    def wait_sib(lo, hi):
-        each(lo, hi, lambda t: wait_recv(Y.at[1 - k, rs_(0, t), DALL], r_d.at[t]))
-
-    def turn_half(b):
-        for h in range(2):
-            T[h, :, b * half:(b + 1) * half] = Y[h, b * half:(b + 1) * half, DALL].T
-
-    def q_half(b):
-        Qa[0, :, COLS[b]] += mm(X[k, :, DALL], Y[k, b * half:(b + 1) * half, DALL])
+    def brows(b):
+        return pl.ds(pl.multiple_of(b * half, half), half)
 
     def wait_w(i, lo, n):
         def one(s):
@@ -184,27 +179,30 @@
 
         each(lo, lo + n, one)
 
-    def send1(i, s, n, j, cols, ss, rs):
-        src = Pa.at[j, rs_(1 - i, s, n), cols]
+    CA = pl.ds(0, rows)
+
+    def send1(src, i, s, n, j, cols, ss, rs):
         return rcopy(src, PR.at[i, rs_(k, s, n), cols], s_p.at[ss], r_p.at[k, rs], 2, 2 * y + j)
 
-    CA = pl.ds(0, rows)
-    m31 = send1(1, 0, NS, 1, CA, 0, 0)
-    m30a = send1(1, 0, NS, 0, C0, 1, 0)
-    m30b = [send1(1, 2 * u, 2, 0, C1, 2 + u, 4 + u) for u in range(4)]
-    m21 = [send1(0, s, n, 1, CA, 6 + g, 1 + g) for g, (s, n) in enumerate(GROUPS)]
-    m20a = [send1(0, s, n, 0, C0, 9 + g, 1 + g) for g, (s, n) in enumerate(GROUPS[:2])]
-    m20b = send1(0, 0, NS - 1, 0, C1, 11, 8)
-    m20c = send1(0, NS - 1, 1, 0, CA, 12, 3)
-    out1 = [m31, m30a, *m30b, *m21, *m20a, m20b, m20c]
-
-    def part(r, j, cols, tcols):
-        Pa[j, r, cols] = mn(W[0, r, :kd], T[0, :, tcols]) + mn(W[1, r, :kd], T[1, :, tcols])
-
-    TJ1 = slice(2 * half, 4 * half)
+    m31 = send1(Pa.at[1, rs_(0, 0, NS)], 1, 0, NS, 1, CA, 0, 0)
+
+    def m30(b, u):
+        return send1(Pb.at[b, rs_(0, 2 * u, 2)], 1, 2 * u, 2, 0, COLS[b], 1 + 4 * b + u, 4 * b + u)
+
+    def m21(g):
+        return send1(Pa.at[1, rs_(1, 2 * g, 2)], 0, 2 * g, 2, 1, CA, 9 + g, 1 + g)
+
+    def m20(b, g):
+        return send1(Pb.at[b, rs_(1, 2 * g, 2)], 0, 2 * g, 2, 0, COLS[b], 13 + 4 * b + g, 8 + 4 * b + g)
+
+    def part1(r):
+        Pa[1, r, :] = mn(W[0, r, :kd], T1[0]) + mn(W[1, r, :kd], T1[1])
+
+    def part0(r, b):
+        Pb[b, r, :] = mn(W[0, r, :kd], T0[0, b]) + mn(W[1, r, :kd], T0[1, b])
 
     def q0send(b):
-        return rcopy(Qa.at[0, :, COLS[b]], R.at[slot(0), :, COLS[b]], s_q.at[b], r_r.at[slot(0), b], 1, 0)
+        return rcopy(Qb.at[b], R.at[slot(0), :, COLS[b]], s_q.at[b], r_r.at[slot(0), b], 1, 0)
 
     @pl.when(z == 1)
     def _():
@@ -224,52 +222,66 @@
         each(NU, nd, turn)
         if xd:
             turn(nd, xd)
-        each(0, 4, zD)
-        wait_w(0, 0, NS)
-        part(rs_(0, 0, NS), 1, CA, TJ1)
-        m31.start()
-        each(5, 10, lambda q: u_fwd(q).start())
-        each(4, 8, zD)
-        wait_sib(0, 8)
-        turn_half(0)
-        part(rs_(0, 0, NS), 0, C0, slice(0, half))
-        m30a.start()
-        each(10, NU, lambda q: u_fwd(q).start())
-        u_fwd(NU, XU).start()
-        q_half(0)
-
-        @pl.when(c != 0)
-        def _():
-            q0send(0).start()
-
-        for g, stop in ((0, 11), (1, 15)):
-            each(8 if g == 0 else 11, stop, zD)
-            s, n = GROUPS[g]
-            wait_w(1, s, n)
-            part(rs_(1, s, n), 1, CA, TJ1)
-            m21[g].start()
-            part(rs_(1, s, n), 0, C0, slice(0, half))
-            m20a[g].start()
-        zD(15)
-        wait_sib(8, 16)
-        r = pl.ds(0, rows - st)
-        Pa[0, r, C1] = mm(W[0, r, :kd], Y[0, half:, DALL]) + mm(W[1, r, :kd], Y[1, half:, DALL])
-        for x in m30b:
-            x.start()
-        m20b.start()
-        q_half(1)
-
-        @pl.when(c != 0)
-        def _():
-            q0send(1).start()
-
-        turn_half(1)
-        s, n = GROUPS[2]
-        wait_w(1, s, n)
-        part(rs_(1, s, n), 1, CA, TJ1)
-        m21[2].start()
-        part(rs_(1, s, n), 0, CA, slice(0, rows))
-        m20c.start()
+
+        def step(i):
+            @pl.when(i < 2 * NS)
+            def _():
+                zD(i)
+
+            @pl.when(i == 3)
+            def _():
+                wait_w(0, 0, NS)
+                part1(rs_(0, 0, NS))
+                m31.start()
+                each(5, 10, lambda q: u_fwd(q).start())
+
+            @pl.when((i == 7) | (i == 16))
+            def _():
+                b = jnp.where(i == 7, 0, 1)
+                each(NS * b, NS * b + NS, lambda t: wait_recv(Y.at[1 - k, rs_(0, t), DALL], r_d.at[t]))
+                for h in range(2):
+                    T0[h, b] = Y[h, brows(b), DALL].T
+                part0(rs_(0, 0, NS), b)
+                for bb in range(2):
+                    @pl.when(b == bb)
+                    def _():
+                        for u in range(4):
+                            m30(bb, u).start()
+
+            @pl.when((i == 7) | (i == 19))
+            def _():
+                b = jnp.where(i == 7, 0, 1)
+                Qb[b] += mm(X[k, :, DALL], Y[k, brows(b), DALL])
+                for bb in range(2):
+                    @pl.when((b == bb) & (c != 0))
+                    def _():
+                        q0send(bb).start()
+
+            @pl.when(i == 7)
+            def _():
+                each(10, 13, lambda q: u_fwd(q).start())
+
+            @pl.when((i == 8) | (i == 9) | (i == 13) | (i == 20))
+            def _():
+                g = jnp.where(i == 20, 3, jnp.where(i == 13, 2, i - 8))
+                wait_w(1, 2 * g, 2)
+                part1(rs_(1, 2 * g, 2))
+                m21(g).start()
+                part0(rs_(1, 2 * g, 2), 0)
+                m20(0, g).start()
+
+            @pl.when(i == 9)
+            def _():
+                each(13, NU, lambda q: u_fwd(q).start())
+                u_fwd(NU, XU).start()
+
+            @pl.when(i >= 17)
+            def _():
+                g = i - 17
+                part0(rs_(1, 2 * g, 2), 1)
+                m20(1, g).start()
+
+        each(0, 21, step)
 
     def d_fwd(t):
         h, s = t % 2, t // 2
@@ -306,8 +318,10 @@
         r = rs_(h, s, n)
         return rcopy(Pa.at[0, r, cols], R.at[0, r, cols], s_p.at[10 + 3 * h + i], r_r.at[0, 3 * h + i], 2, k)
 
-    s2_k1 = [[s2(h, s, n, CA, i) for i, (s, n) in enumerate(GROUPS)] for h in range(2)]
-    s2_k0 = [[s2(h, 0, NS - 1, C0, 0), s2(h, 0, NS - 1, C1, 1), s2(h, NS - 1, 1, CA, 2)] for h in range(2)]
+    PART1 = ((0, 4), (4, 2), (6, 2))
+    PART0 = ((0, 6, C0), (0, 6, C1), (6, 2, CA))
+    s2_k1 = [[s2(h, s, n, CA, i) for i, (s, n) in enumerate(PART1)] for h in range(2)]
+    s2_k0 = [[s2(h, s, n, cols, i) for i, (s, n, cols) in enumerate(PART0)] for h in range(2)]
 
     def add(i, r, cols, sem):
         wait_recv(PR.at[i, r, cols], sem)
@@ -379,14 +393,18 @@
 
         each(0, NS, step_u)
 
+        def add21(gs, i):
+            for h in range(2):
+                for g in gs:
+                    add(0, rs_(h, 2 * g, 2), CA, r_p.at[h, 1 + g])
+                y1_start(s2_k1[h][i])
+
         @pl.when(k == 1)
         def _():
-            strip31(NS - 2)
-            strip31(NS - 1)
-            for i, (s, n) in enumerate(GROUPS):
-                for h in range(2):
-                    add(0, rs_(h, s, n), CA, r_p.at[h, 1 + i])
-                    y1_start(s2_k1[h][i])
+            add21((0, 1), 0)
+            each(NS - 2, NS, strip31)
+            add21((2,), 1)
+            add21((3,), 2)
 
         @pl.when(k == 0)
         def _():
@@ -394,26 +412,34 @@
             y2(NU, XU)
             y3(0, NU - 1)
             y3(0, NU, XU)
-            add(1, pl.ds(0, half), C0, r_p.at[0, 0])
+            for u in range(4):
+                add(1, rs_(0, 2 * u, 2), C0, r_p.at[0, u])
             s3_a[0].start()
+            for h in range(2):
+                for g in range(3):
+                    add(0, rs_(h, 2 * g, 2), C0, r_p.at[h, 8 + g])
+                y1_start(s2_k0[h][0])
             each(4, NS, wait_ysib)
-            each(0, NU, lambda q: y3(1, q))
-            y3(1, NU, XU)
-            add(1, pl.ds(half, half), C0, r_p.at[1, 0])
+
+            def low(b):
+                r = pl.ds(pl.multiple_of(b * half, half), half)
+                Pa[1, r, :] = mm(Y[0, r, UALL], W[0, :, :ku]) + mm(Y[1, r, UALL], W[1, :, :ku])
+
+            each(1 + k, 2, low)
+            for u in range(4):
+                add(1, rs_(1, 2 * u, 2), C0, r_p.at[1, u])
             s3_a[1].start()
-            for h in range(2):
-                for g, (s, n) in enumerate(GROUPS[:2]):
-                    add(0, rs_(h, s, n), C0, r_p.at[h, 1 + g])
-                y1_start(s2_k0[h][0])
             for u in range(4):
                 for h in range(2):
                     add(1, rs_(h, 2 * u, 2), C1, r_p.at[h, 4 + u])
                     s3_b[h][u].start()
             for h in range(2):
-                add(0, rs_(h, 0, NS - 1), C1, r_p.at[h, 8])
+                for g in range(3):
+                    add(0, rs_(h, 2 * g, 2), C1, r_p.at[h, 12 + g])
                 y1_start(s2_k0[h][1])
             for h in range(2):
-                add(0, rs_(h, NS - 1), CA, r_p.at[h, 3])
+                add(0, rs_(h, 6, 2), C0, r_p.at[h, 11])
+                add(0, rs_(h, 6, 2), C1, r_p.at[h, 15])
                 y1_start(s2_k0[h][2])
 
     @pl.when(z != 2)
@@ -434,24 +460,22 @@
 
     @pl.when((z == 1) & (c == 0))
     def _():
-        for i in range(3):
-            for b in range(2):
+        for b in range(2):
+            for i in range(3):
                 wait_recv(R.at[i, :, COLS[b]], r_r.at[i, b])
-        o_ref[...] = (Qa[0] + R[0] + R[1] + R[2]).astype(o_ref.dtype)
+            o_ref[:, COLS[b]] = (Qb[b] + R[0, :, COLS[b]] + R[1, :, COLS[b]] + R[2, :, COLS[b]]).astype(o_ref.dtype)
 
     @pl.when((z == 2) & (y == 0))
     def _():
-        @pl.when(k == 0)
-        def _():
-            for h in range(2):
-                wait_recv(R.at[0, rs_(h, 0, NS - 1), C0], r_r.at[0, 3 * h])
-                wait_recv(R.at[0, rs_(h, 0, NS - 1), C1], r_r.at[0, 3 * h + 1])
-                wait_recv(R.at[0, rs_(h, NS - 1)], r_r.at[0, 3 * h + 2])
-
-        @pl.when(k == 1)
-        def _():
-            for h in range(2):
-                for i, (s, n) in enumerate(GROUPS):
+        for h in range(2):
+            @pl.when(k == 0)
+            def _():
+                for i, (s, n, cols) in enumerate(PART0):
+                    wait_recv(R.at[0, rs_(h, s, n), cols], r_r.at[0, 3 * h + i])
+
+            @pl.when(k == 1)
+            def _():
+                for i, (s, n) in enumerate(PART1):
                     wait_recv(R.at[0, rs_(h, s, n)], r_r.at[0, 3 * h + i])
 
         o_ref[...] = (Pa[0] + R[0]).astype(o_ref.dtype)
@@ -505,8 +529,13 @@
         each(0, NU, lambda q: u_fwd(q).wait_send())
         u_fwd(NU, XU).wait_send()
         each(0, 2 * NS, lambda t: d_sib(t).wait_send())
-        for x in out1:
-            x.wait_send()
+        m31.wait_send()
+        for b in range(2):
+            for u in range(4):
+                m30(b, u).wait_send()
+                m20(b, u).wait_send()
+        for g in range(4):
+            m21(g).wait_send()
 
         @pl.when(c != 0)
         def _():
@@ -549,21 +578,24 @@
         dma = pltpu.SemaphoreType.DMA
         return pl.pallas_call(
             kernel,
-            out_shape=jax.ShapeDtypeStruct((rows, rows), bf16),
+            out_shape=pltpu.VMEM((rows, rows), bf16),
             in_specs=[pl.BlockSpec(memory_space=pl.ANY)],
             out_specs=pl.BlockSpec(memory_space=pltpu.VMEM),
             scratch_shapes=[
                 pltpu.VMEM((2, rows, m), bf16),
                 pltpu.VMEM((2, rows, m), bf16),
                 pltpu.VMEM((2, rows, kd), bf16),
-                pltpu.VMEM((2, kd, 2 * rows), bf16),
+                pltpu.VMEM((2, 2, kd, rows // 2), bf16),
+                pltpu.VMEM((2, kd, rows), bf16),
                 pltpu.VMEM((2, rows, rows), f32),
+                pltpu.VMEM((2, rows, rows // 2), f32),
                 pltpu.VMEM((2, rows, rows), f32),
+                pltpu.VMEM((2, rows, rows // 2), f32),
                 pltpu.VMEM((4, rows, rows), f32),
                 pltpu.VMEM((2, rows, rows), f32),
                 pltpu.SemaphoreType.REGULAR,
                 dma((1,)), dma((4 * NS,)), dma((4 * NS,)), dma((2 * NS + 1,)), dma((2 * NS + 1,)),
-                dma((2, 2 * NS)), dma((16,)), dma((2, 9)), dma((NS + 1,)), dma((4, 10)),
+                dma((2, 2 * NS)), dma((21,)), dma((2, 16)), dma((NS + 1,)), dma((4, 10)),
             ],
             compiler_params=pltpu.CompilerParams(
                 collective_id=0, has_side_effects=True, vmem_limit_bytes=56 * 1024 * 1024),

time: 112 us -> 109 us (0.973)
  the two profiles are of different devices: /device:TPU:18 before, /device:TPU:24 now
where the time goes in v5:
time: 109 us; the launch traced here: 108 us
  Pallas kernels  107 us (98%)
    pallas_call x1, Pallas kernels, local_fn(): pl.pallas_call(kernel, out_shape=pltpu.VMEM((rows, rows), bf16), in_specs...  107 us

profile of v5, /device:TPU:24, one launch (start us, length us, event | category | flops | bytes accessed | tf_op | source)
XLA Modules:
  0.0 107.8 jit_solution(9546755262156049432)
XLA Ops:
  0.0 107.2 %shard_map.17 = bf16[256,256]{1,0:T(8,128)(2,1)S(1)} custom-call(bf16[256,8192]{1,0:T(8,128)(2,1)} %a_ref.1), custom_call_target="tpu_custom_call" | custom-call | tf_op jit(solution)/shard_map/pallas_call | solution.py:579
  107.2 0.7 copy.3

commit v6 on v5

v6 whole, which is shorter than its diff:
```python
import jax
import jax.numpy as jnp
from jax import lax
from jax.experimental import pallas as pl
from jax.experimental.pallas import tpu as pltpu
from jax.sharding import PartitionSpec as P

MESH = pl.DeviceIdType.MESH
PW = 256
NU = 15
XU = 128
NS = 8


def mm(a, b):
    return lax.dot_general(a, b, (((1,), (1,)), ((), ())), preferred_element_type=jnp.float32)


def mn(a, b):
    return lax.dot_general(a, b, (((1,), (0,)), ((), ())), preferred_element_type=jnp.float32)


def kernel(a_ref, o_ref, X, Y, W, T0, T1, Pa, Pb, Qa, Qb, R, PR, far, ld, s_z, r_y, r_d, r_w, r_p, r_r):
    rows, m = a_ref.shape
    ku = NU * PW + XU
    kd = m - ku
    nd, xd = kd // PW, kd % PW
    half = rows // 2
    st = half // NS
    us = rows // NS
    z = lax.axis_index("row")
    c = lax.axis_index("col")
    y = c // 2
    k = c % 2
    sib = 2 * y + 1 - k

    def rcopy(src, dst, ss, rs, row, col):
        return pltpu.make_async_remote_copy(
            src_ref=src, dst_ref=dst, send_sem=ss, recv_sem=rs, device_id={"row": row, "col": col}, device_id_type=MESH)

    def wait_recv(ref, sem):
        pltpu.make_async_copy(ref, ref, sem).wait()

    def up(p, w=PW):
        return pl.ds(pl.multiple_of(p * PW, 128), w)

    def dn(p, w=PW):
        return pl.ds(pl.multiple_of(ku + p * PW, 128), w)

    def rs_(h, s, n=1):
        return pl.ds(pl.multiple_of(h * half + s * st, st), n * st)

    def us_(s):
        return pl.ds(pl.multiple_of(s * us, us), us)

    DALL = pl.ds(ku, kd)
    UALL = pl.ds(0, ku)
    C0, C1 = pl.ds(0, half), pl.ds(half, half)
    COLS = (C0, C1)

    def each(lo, hi, fn):
        lax.fori_loop(lo, hi, lambda i, u: (fn(i), u)[1], 0)

    load = pltpu.make_async_copy(a_ref, X.at[k], ld.at[0])
    load.start()

    def near(sem):
        for dz in (-1, 1):
            @pl.when((z + dz >= 0) & (z + dz <= 3))
            def _():
                for kk in range(2):
                    pl.semaphore_signal(sem, inc=1, device_id={"row": z + dz, "col": 2 * y + kk}, device_id_type=MESH)
        for dc in range(1, 4):
            pl.semaphore_signal(sem, inc=1, device_id={"row": z, "col": (c + dc) % 4}, device_id_type=MESH)

    n_near = jnp.where((z == 0) | (z == 3), 5, 7)
    bar = pltpu.get_barrier_semaphore()
    near(bar)
    pl.semaphore_wait(bar, n_near)

    def z0_u(q, w=PW):
        return rcopy(a_ref.at[:, up(q, w)], Y.at[k, :, up(q, w)], s_z.at[0], r_y.at[q], 1, c)

    def z0_d(t):
        r = rs_(0, t)
        return rcopy(a_ref.at[r, DALL], Y.at[k, r, DALL], s_z.at[0], r_y.at[2 * NS + t], 1, c)

    def z3_d(t):
        r = rs_(t % 2, t // 2)
        return rcopy(a_ref.at[r, DALL], Y.at[k, r, DALL], s_z.at[0], r_y.at[t], 2, c)

    def z3_u(s):
        r = us_(s)
        return rcopy(a_ref.at[r, UALL], Y.at[k, r, UALL], s_z.at[0], r_y.at[2 * NS + s], 2, c)

    def z1_u(q, w=PW):
        return rcopy(a_ref.at[:, up(q, w)], W.at[k, :, up(q, w)], s_z.at[0], r_w.at[q], 2, 2 * y + 1)

    def z2_d(t):
        h, s = t % 2, t // 2
        return rcopy(a_ref.at[rs_(h, s), DALL], W.at[k, rs_(1, s), pl.ds(0, kd)], s_z.at[0], r_w.at[1 + s // 2], 1, 2 * y + h)

    @pl.when(z == 0)
    def _():
        each(0, NU, lambda q: z0_u(q).start())
        z0_u(NU, XU).start()
        each(0, 2 * NS, lambda t: z0_d(t).start())

    @pl.when(z == 3)
    def _():
        each(0, 2 * NS, lambda t: z3_d(t).start())
        each(0, NS, lambda s: z3_u(s).start())

    x_d = rcopy(a_ref.at[:, DALL], X.at[k, :, DALL], s_z.at[1], r_d.at[NS], z, sib)
    x_u = rcopy(a_ref.at[:, UALL], X.at[k, :, UALL], s_z.at[1], r_d.at[NS], z, sib)

    @pl.when(z == 1)
    def _():
        each(0, NU, lambda q: z1_u(q).start())
        z1_u(NU, XU).start()
        x_d.start()

    @pl.when(z == 2)
    def _():
        z2_d(0).start()
        z2_d(1).start()
        x_u.start()

    near(far)

    Pa[...] = jnp.zeros_like(Pa)
    Qa[...] = jnp.zeros_like(Qa)
    Qb[...] = jnp.zeros_like(Qb)
    load.wait()
    dq = jnp.where(z == 1, 1, 0)

    def diag(p):
        cs = pl.ds(pl.multiple_of(p * 512, 512), 512)
        Qa[dq] += mm(X[k, :, cs], X[k, :, cs])

    each(0, m // 512, diag)

    def slot(owner):
        return (c - owner + 3) % 4

    dsend = rcopy(Qa.at[dq], R.at[slot(z)], s_z.at[3], r_r.at[0], z, z)

    @pl.when(c != z)
    def _():
        dsend.start()

    def u_fwd(q, w=PW):
        return rcopy(Y.at[k, :, up(q, w)], W.at[k, :, up(q, w)], s_z.at[0], r_w.at[q], 2, 2 * y)

    def zU(q, w=PW):
        wait_recv(Y.at[k, :, up(q, w)], r_y.at[q])
        v = mm(X[k, :, up(q, w)], Y[k, :, up(q, w)])
        Qb[0] += v[:, :half]
        Qb[1] += v[:, half:]

    def turn(p, w=PW):
        for h in range(2):
            T1[h, up(p, w), :] = X[h, :, dn(p, w)].T

    def d_sib(t):
        return rcopy(Y.at[k, rs_(0, t), DALL], Y.at[k, rs_(0, t), DALL], s_z.at[1], r_d.at[t // NS], z, sib)

    def zD(t):
        wait_recv(Y.at[k, rs_(0, t), DALL], r_y.at[2 * NS + t])
        d_sib(t).start()

    def brows(b):
        return pl.ds(pl.multiple_of(b * half, half), half)

    def wait_w(r, n):
        wait_recv(W.at[:, r, pl.ds(0, kd)], r_w.at[n])

    CA = pl.ds(0, rows)

    def send1(src, i, s, n, j, cols, rs):
        return rcopy(src, PR.at[i, rs_(k, s, n), cols], s_z.at[2], r_p.at[rs], 2, 2 * y + j)

    m31 = send1(Pa.at[1, rs_(0, 0, NS)], 1, 0, NS, 1, CA, 0)

    def m30(b, u):
        return send1(Pb.at[b, rs_(0, 2 * u, 2)], 1, 2 * u, 2, 0, COLS[b], b + b * u)

    def m21(g):
        return send1(Pa.at[1, rs_(1, 2 * g, 2)], 0, 2 * g, 2, 1, CA, 1 + g // 2 + g // 3)

    def m20(b, g):
        return send1(Pb.at[b, rs_(1, 2 * g, 2)], 0, 2 * g, 2, 0, COLS[b], jnp.where(g == 3, 7, 5 + b))

    def part1(r):
        Pa[1, r, :] = mn(W[0, r, :kd], T1[0]) + mn(W[1, r, :kd], T1[1])

    def part0(r, b):
        Pb[b, r, :] = mn(W[0, r, :kd], T0[0, b]) + mn(W[1, r, :kd], T0[1, b])

    def q0send(b):
        return rcopy(Qb.at[b], R.at[slot(0), :, COLS[b]], s_z.at[4], r_r.at[b], 1, 0)

    @pl.when(z == 1)
    def _():
        wait_recv(X.at[1 - k, :, DALL], r_d.at[NS])

        def step_u(q):
            zU(q)

            @pl.when(q < 5)
            def _():
                u_fwd(q).start()

            turn(q)

        each(0, NU, step_u)
        zU(NU, XU)
        each(NU, nd, turn)
        if xd:
            turn(nd, xd)

        def step(i):
            @pl.when(i < 2 * NS)
            def _():
                zD(i)

            @pl.when(i == 3)
            def _():
                wait_w(rs_(0, 0, NS), 0)
                part1(rs_(0, 0, NS))
                m31.start()
                each(5, 10, lambda q: u_fwd(q).start())

            @pl.when((i == 7) | (i == 16))
            def _():
                b = jnp.where(i == 7, 0, 1)
                wait_recv(Y.at[1 - k, brows(b), DALL], r_d.at[b])
                for h in range(2):
                    T0[h, b] = Y[h, brows(b), DALL].T
                part0(rs_(0, 0, NS), b)
                for bb in range(2):
                    @pl.when(b == bb)
                    def _():
                        for u in range(4):
                            m30(bb, u).start()

            @pl.when((i == 7) | (i == 19))
            def _():
                b = jnp.where(i == 7, 0, 1)
                Qb[b] += mm(X[k, :, DALL], Y[k, brows(b), DALL])
                for bb in range(2):
                    @pl.when((b == bb) & (c != 0))
                    def _():
                        q0send(bb).start()

            @pl.when(i == 7)
            def _():
                each(10, 13, lambda q: u_fwd(q).start())

            @pl.when((i == 8) | (i == 9) | (i == 13) | (i == 20))
            def _():
                g = jnp.where(i == 20, 3, jnp.where(i == 13, 2, i - 8))
                wait_w(rs_(1, 2 * g, 2), 1 + g)
                part1(rs_(1, 2 * g, 2))
                m21(g).start()
                part0(rs_(1, 2 * g, 2), 0)
                m20(0, g).start()

            @pl.when(i == 9)
            def _():
                each(13, NU, lambda q: u_fwd(q).start())
                u_fwd(NU, XU).start()

            @pl.when(i >= 17)
            def _():
                g = i - 17
                part0(rs_(1, 2 * g, 2), 1)
                m20(1, g).start()

        each(0, 21, step)

    def d_fwd(t):
        h, s = t % 2, t // 2
        return rcopy(Y.at[k, rs_(h, s), DALL], W.at[k, rs_(0, s), pl.ds(0, kd)], s_z.at[0], r_w.at[0], 1, 2 * y + h)

    def u_sib(s):
        return rcopy(Y.at[k, us_(s), UALL], Y.at[k, us_(s), UALL], s_z.at[1], r_d.at[s], z, sib)

    def q1send(s):
        return rcopy(Qa.at[1, us_(s)], R.at[c, us_(s)], s_z.at[4], r_r.at[0], 3, 2)

    def y2(q, w=PW):
        wait_recv(W.at[:, :, up(q, w)], r_w.at[q])
        Pa[0] += mm(X[0, :, up(q, w)], W[0, :, up(q, w)]) + mm(X[1, :, up(q, w)], W[1, :, up(q, w)])

    def y3(b, q, w=PW):
        r = pl.ds(b * half, half)
        Pa[1, r, :] += mm(Y[0, r, up(q, w)], W[0, :, up(q, w)]) + mm(Y[1, r, up(q, w)], W[1, :, up(q, w)])

    def wait_ysib(s):
        wait_recv(Y.at[1 - k, us_(s), UALL], r_d.at[s])

    def s3(r, cols, n):
        return rcopy(Pa.at[1, r, cols], R.at[y, r, cols], s_z.at[2], r_r.at[0], 3, k)

    s3_a = [s3(pl.ds(b * half, half), C0, b) for b in range(2)]
    s3_b = [[s3(rs_(h, 2 * u, 2), C1, 2 + 4 * h + u) for u in range(4)] for h in range(2)]

    def s3_k1(s):
        return s3(us_(s), CA, s)

    def s2(h, s, n, cols, i):
        r = rs_(h, s, n)
        return rcopy(Pa.at[0, r, cols], R.at[0, r, cols], s_z.at[2], r_r.at[0], 2, k)

    PART1 = ((0, 4), (4, 2), (6, 2))
    PART0 = ((0, 6, C0), (0, 6, C1), (6, 2, CA))
    s2_k1 = [[s2(h, s, n, CA, i) for i, (s, n) in enumerate(PART1)] for h in range(2)]
    s2_k0 = [[s2(h, s, n, cols, i) for i, (s, n, cols) in enumerate(PART0)] for h in range(2)]

    def wait_pr(n, cols, sem):
        wait_recv(PR.at[0, pl.ds(0, n), cols], r_p.at[sem])

    def add(i, r, cols):
        Pa[i, r, cols] += PR[i, r, cols]

    def y1_start(x):
        @pl.when(y == 1)
        def _():
            x.start()

    def strip31(s):
        wait_ysib(s)
        r = us_(s)
        Pa[1, r, :] = PR[1, r, :] + mm(Y[0, r, UALL], W[0, :, :ku]) + mm(Y[1, r, UALL], W[1, :, :ku])
        s3_k1(s).start()

    @pl.when(z == 2)
    def _():
        def step_d(t):
            wait_recv(Y.at[k, rs_(t % 2, t // 2), DALL], r_y.at[t])
            d_fwd(t).start()

            @pl.when(t == 1)
            def _():
                wait_recv(X.at[1 - k, :, UALL], r_d.at[NS])

            @pl.when((k == 1) & (t >= 1))
            def _():
                y2(t - 1)

        each(0, 2 * NS, step_d)
        each(2, 2 * NS, lambda t: z2_d(t).start())

        @pl.when(k == 1)
        def _():
            y2(NU, XU)

        pl.semaphore_wait(far, n_near)

        def step_u(s):
            wait_recv(Y.at[k, us_(s), UALL], r_y.at[2 * NS + s])
            u_sib(s).start()
            Qa[1, us_(s), :] = mm(Y[k, us_(s), :], X[k])
            q1send(s).start()

            @pl.when((k == 0) & (s >= 1))
            def _():
                y2(2 * s - 2)
                y2(2 * s - 1)

            @pl.when((k == 0) & (s == 4))
            def _():
                each(0, 4, wait_ysib)
                each(0, 6, lambda q: y3(0, q))

            @pl.when((k == 0) & (s >= 4))
            def _():
                y3(0, 2 * s - 2)
                y3(0, 2 * s - 1)

            @pl.when((k == 1) & (s == 2))
            def _():
                wait_recv(PR.at[1], r_p.at[0])

            @pl.when((k == 1) & (s >= 2))
            def _():
                strip31(s - 2)

        each(0, NS, step_u)

        def add21(gs, i):
            wait_pr(64 * len(gs), CA, 1 + i)
            for h in range(2):
                add(0, rs_(h, 2 * gs[0], 2 * len(gs)), CA)
                y1_start(s2_k1[h][i])

        @pl.when(k == 1)
        def _():
            add21((0, 1), 0)
            each(NS - 2, NS, strip31)
            add21((2,), 1)
            add21((3,), 2)

        @pl.when(k == 0)
        def _():
            y2(NU - 1)
            y2(NU, XU)
            y3(0, NU - 1)
            y3(0, NU, XU)
            wait_pr(rows, C0, 0)
            add(1, pl.ds(0, half), C0)
            s3_a[0].start()
            wait_pr(192, C0, 5)
            for h in range(2):
                add(0, rs_(h, 0, 6), C0)
                y1_start(s2_k0[h][0])
            each(4, NS, wait_ysib)

            def low(b):
                r = pl.ds(pl.multiple_of(b * half, half), half)
                Pa[1, r, :] = mm(Y[0, r, UALL], W[0, :, :ku]) + mm(Y[1, r, UALL], W[1, :, :ku])

            each(1 + k, 2, low)
            add(1, pl.ds(half, half), C0)
            s3_a[1].start()
            for u in range(4):
                wait_pr(64, C1, 1 + u)
                for h in range(2):
                    add(1, rs_(h, 2 * u, 2), C1)
                    s3_b[h][u].start()
            wait_pr(192, C1, 6)
            for h in range(2):
                add(0, rs_(h, 0, 6), C1)
                y1_start(s2_k0[h][1])
            wait_pr(64, CA, 7)
            for h in range(2):
                add(0, rs_(h, 6, 2), CA)
                y1_start(s2_k0[h][2])

    @pl.when(z != 2)
    def _():
        pl.semaphore_wait(far, n_near)

    @pl.when(c > z)
    def _():
        o_ref[...] = jnp.zeros_like(o_ref)

    @pl.when(c == z)
    def _():
        wait_recv(R.at[pl.ds(0, 3)], r_r.at[0])
        total = Qa[dq] + R[0] + R[1] + R[2]
        diff = lax.broadcasted_iota(jnp.int32, (rows, rows), 0) - lax.broadcasted_iota(jnp.int32, (rows, rows), 1)
        o_ref[...] = jnp.where(diff >= 0, total, 0.0).astype(o_ref.dtype)

    @pl.when((z == 1) & (c == 0))
    def _():
        for b in range(2):
            wait_recv(R.at[pl.ds(0, 3), :, COLS[b]], r_r.at[b])
            o_ref[:, COLS[b]] = (Qb[b] + R[0, :, COLS[b]] + R[1, :, COLS[b]] + R[2, :, COLS[b]]).astype(o_ref.dtype)

    @pl.when((z == 2) & (y == 0))
    def _():
        wait_recv(R.at[0], r_r.at[0])
        o_ref[...] = (Pa[0] + R[0]).astype(o_ref.dtype)

    @pl.when((z == 3) & (c == 2))
    def _():
        wait_recv(R, r_r.at[0])
        o_ref[...] = (R[0] + R[1] + R[2] + R[3]).astype(o_ref.dtype)

    @pl.when((z == 3) & (y == 0))
    def _():
        wait_recv(R.at[pl.ds(0, 2)], r_r.at[0])
        o_ref[...] = (R[0] + R[1]).astype(o_ref.dtype)

    @pl.when(c != z)
    def _():
        wait_recv(Qa.at[0], s_z.at[3])

    @pl.when((z == 0) | (z == 3))
    def _():
        wait_recv(X.at[k], s_z.at[0])

    @pl.when(z == 1)
    def _():
        wait_recv(W.at[:, :, pl.ds(0, ku)], s_z.at[0])
        wait_recv(W.at[:, :, pl.ds(0, kd)], s_z.at[1])
        wait_recv(Pa, s_z.at[2])

        @pl.when(c != 0)
        def _():
            wait_recv(Qb, s_z.at[4])

    @pl.when(z == 2)
    def _():
        wait_recv(W.at[:, :, pl.ds(0, kd)], s_z.at[0])
        wait_recv(W.at[:, :, pl.ds(0, ku)], s_z.at[1])
        wait_recv(Qa.at[1], s_z.at[4])

        @pl.when(y == 0)
        def _():
            wait_recv(Pa.at[0], s_z.at[2])

        @pl.when(y == 1)
        def _():
            wait_recv(Pa, s_z.at[2])


def solution(mesh):
    def local_fn(a_local):
        rows, m = a_local.shape
        kd = m - NU * PW - XU
        f32, bf16 = jnp.float32, jnp.bfloat16
        dma = pltpu.SemaphoreType.DMA
        return pl.pallas_call(
            kernel,
            out_shape=pltpu.VMEM((rows, rows), bf16),
            in_specs=[pl.BlockSpec(memory_space=pl.ANY)],
            out_specs=pl.BlockSpec(memory_space=pltpu.VMEM),
            scratch_shapes=[
                pltpu.VMEM((2, rows, m), bf16),
                pltpu.VMEM((2, rows, m), bf16),
                pltpu.VMEM((2, rows, kd), bf16),
                pltpu.VMEM((2, 2, kd, rows // 2), bf16),
                pltpu.VMEM((2, kd, rows), bf16),
                pltpu.VMEM((2, rows, rows), f32),
                pltpu.VMEM((2, rows, rows // 2), f32),
                pltpu.VMEM((2, rows, rows), f32),
                pltpu.VMEM((2, rows, rows // 2), f32),
                pltpu.VMEM((4, rows, rows), f32),
                pltpu.VMEM((2, rows, rows), f32),
                pltpu.SemaphoreType.REGULAR,
                dma((1,)), dma((5,)), dma((4 * NS,)), dma((NS + 1,)), dma((NU + 1,)), dma((8,)), dma((2,)),
            ],
            compiler_params=pltpu.CompilerParams(
                collective_id=0, has_side_effects=True, vmem_limit_bytes=56 * 1024 * 1024),
        )(a_local)

    part_spec = P(("batch", "row"), "col")
    return jax.shard_map(local_fn, mesh=mesh, in_specs=(part_spec,), out_specs=part_spec, check_vma=False)
```

time: 109 us -> 107 us (0.982)
    pallas_call x1, Pallas kernels: 107 us -> 106 us  [local_fn(): pl.pallas_call(kernel, out_shape=pltpu.VMEM((rows, rows), bf16), in_specs...]
where the time goes in v6:
time: 107 us; the launch traced here: 106 us
  Pallas kernels  106 us (99%)
    pallas_call x1, Pallas kernels, local_fn(): pl.pallas_call(kernel, out_shape=pltpu.VMEM((rows, rows), bf16), in_specs...  106 us

profile of v6, /device:TPU:24, one launch (start us, length us, event | category | flops | bytes accessed | tf_op | source)
XLA Modules:
  0.0 106.2 jit_solution(15796318234422496609)
XLA Ops:
  0.0 105.5 %shard_map.17 = bf16[256,256]{1,0:T(8,128)(2,1)S(1)} custom-call(bf16[256,8192]{1,0:T(8,128)(2,1)} %a_ref.1), custom_call_target="tpu_custom_call" | custom-call | tf_op jit(solution)/shard_map/pallas_call | solution.py:516
  105.5 0.7 copy.3

commit v7 on v6

--- a/solution.py
+++ b/solution.py
@@ -20,7 +20,7 @@
     return lax.dot_general(a, b, (((1,), (0,)), ((), ())), preferred_element_type=jnp.float32)
 
 
-def kernel(a_ref, o_ref, X, Y, W, T0, T1, Pa, Pb, Qa, Qb, R, PR, far, ld, s_z, r_y, r_d, r_w, r_p, r_r):
+def kernel(a_ref, o_ref, X, Y, W, T0, T1, Pa, Pb, Qa, Qb, R, PR, XA, XB, far, ld, s_z, r_y, r_d, r_w, r_p, r_r, r_x):
     rows, m = a_ref.shape
     ku = NU * PW + XU
     kd = m - ku
@@ -176,20 +176,50 @@
         wait_recv(W.at[:, r, pl.ds(0, kd)], r_w.at[n])
 
     CA = pl.ds(0, rows)
-
-    def send1(src, i, s, n, j, cols, rs):
-        return rcopy(src, PR.at[i, rs_(k, s, n), cols], s_z.at[2], r_p.at[rs], 2, 2 * y + j)
-
-    m31 = send1(Pa.at[1, rs_(0, 0, NS)], 1, 0, NS, 1, CA, 0)
+    peer = (c + 2) % 4
+
+    def r3(u):
+        return rs_(0, 4 * u, 4)
+
+    def r2(g):
+        return rs_(1, 2 * g, 2)
+
+    def xsend(src, dst, n):
+        return rcopy(src, dst, s_z.at[2], r_x.at[n], 1, peer)
+
+    x31 = xsend(Pa.at[1, rs_(0, 0, NS)], XA.at[rs_(0, 0, NS)], 0)
+
+    def x30(b, u):
+        return xsend(Pb.at[b, r3(u)], XB.at[b, r3(u)], 1 + 2 * b + u)
+
+    def x21(g):
+        return xsend(Pa.at[1, r2(g)], XA.at[r2(g)], 5 + g)
+
+    def x20(b, g):
+        return xsend(Pb.at[b, r2(g)], XB.at[b, r2(g)], jnp.where(b == 0, 5 + g, 8))
+
+    def msend(src, i, s, n, j, cols, rs):
+        return rcopy(src, PR.at[i, rs_(k, s, n), cols], s_z.at[2], r_p.at[rs], 2, j)
+
+    m31 = msend(Pa.at[1, rs_(0, 0, NS)], 1, 0, NS, 1, CA, 0)
 
     def m30(b, u):
-        return send1(Pb.at[b, rs_(0, 2 * u, 2)], 1, 2 * u, 2, 0, COLS[b], b + b * u)
+        src = Pb.at[b, r3(u)]
+        if b == 0:
+            return msend(src, 1, 4 * u, 4, 0, C0, 0)
+        return rcopy(src, R.at[2, rs_(k, 4 * u, 4), C1], s_z.at[2], r_r.at[1], 3, 0)
 
     def m21(g):
-        return send1(Pa.at[1, rs_(1, 2 * g, 2)], 0, 2 * g, 2, 1, CA, 1 + g // 2 + g // 3)
+        return msend(Pa.at[1, r2(g)], 0, 2 * g, 2, 1, CA, jnp.where(g == 3, 2, 1))
 
     def m20(b, g):
-        return send1(Pb.at[b, rs_(1, 2 * g, 2)], 0, 2 * g, 2, 0, COLS[b], jnp.where(g == 3, 7, 5 + b))
+        return msend(Pb.at[b, r2(g)], 0, 2 * g, 2, 0, COLS[b], jnp.where(g == 3, 3, 1 + b))
+
+    def d2(src, j, cols):
+        return rcopy(src, R.at[1, rs_(k, 6, 2), cols], s_z.at[2], r_r.at[1], 2, j)
+
+    d21 = d2(Pa.at[1, r2(3)], 1, CA)
+    d20 = [d2(Pb.at[b, r2(3)], 0, COLS[b]) for b in range(2)]
 
     def part1(r):
         Pa[1, r, :] = mn(W[0, r, :kd], T1[0]) + mn(W[1, r, :kd], T1[1])
@@ -219,6 +249,14 @@
         if xd:
             turn(nd, xd)
 
+        pl.semaphore_wait(far, n_near)
+
+        def merge30(b):
+            for u in range(2):
+                wait_recv(XB.at[b, r3(u)], r_x.at[1 + 2 * b + u])
+                Pb[b, r3(u), :] += XB[b, r3(u), :]
+                m30(b, u).start()
+
         def step(i):
             @pl.when(i < 2 * NS)
             def _():
@@ -228,8 +266,18 @@
             def _():
                 wait_w(rs_(0, 0, NS), 0)
                 part1(rs_(0, 0, NS))
+
+                @pl.when(y == 1)
+                def _():
+                    x31.start()
+
+                each(5, 10, lambda q: u_fwd(q).start())
+
+            @pl.when((i == 5) & (y == 0))
+            def _():
+                wait_recv(XA.at[rs_(0, 0, NS)], r_x.at[0])
+                Pa[1, rs_(0, 0, NS), :] += XA[rs_(0, 0, NS), :]
                 m31.start()
-                each(5, 10, lambda q: u_fwd(q).start())
 
             @pl.when((i == 7) | (i == 16))
             def _():
@@ -239,10 +287,10 @@
                     T0[h, b] = Y[h, brows(b), DALL].T
                 part0(rs_(0, 0, NS), b)
                 for bb in range(2):
-                    @pl.when(b == bb)
+                    @pl.when((b == bb) & (y == 1))
                     def _():
-                        for u in range(4):
-                            m30(bb, u).start()
+                        for u in range(2):
+                            x30(bb, u).start()
 
             @pl.when((i == 7) | (i == 19))
             def _():
@@ -255,29 +303,65 @@
 
             @pl.when(i == 7)
             def _():
-                each(10, 13, lambda q: u_fwd(q).start())
+                each(10, NU, lambda q: u_fwd(q).start())
+                u_fwd(NU, XU).start()
+
+            @pl.when((i == 9) & (y == 0))
+            def _():
+                merge30(0)
+
+            @pl.when((i == 20) & (y == 0))
+            def _():
+                merge30(1)
 
             @pl.when((i == 8) | (i == 9) | (i == 13) | (i == 20))
             def _():
                 g = jnp.where(i == 20, 3, jnp.where(i == 13, 2, i - 8))
-                wait_w(rs_(1, 2 * g, 2), 1 + g)
-                part1(rs_(1, 2 * g, 2))
+                wait_w(r2(g), 1 + g)
+                part1(r2(g))
+                part0(r2(g), 0)
+
+                @pl.when((y == 1) & (i < 20))
+                def _():
+                    x21(g).start()
+                    x20(0, g).start()
+
+            @pl.when(((i == 10) | (i == 11) | (i == 15)) & (y == 0))
+            def _():
+                g = jnp.where(i == 15, 2, i - 10)
+                wait_recv(XA.at[pl.ds(0, 48)], r_x.at[5 + g])
+                Pa[1, r2(g), :] += XA[r2(g), :]
+                Pb[0, r2(g), :] += XB[0, r2(g), :]
                 m21(g).start()
-                part0(rs_(1, 2 * g, 2), 0)
                 m20(0, g).start()
 
-            @pl.when(i == 9)
-            def _():
-                each(13, NU, lambda q: u_fwd(q).start())
-                u_fwd(NU, XU).start()
-
             @pl.when(i >= 17)
             def _():
                 g = i - 17
-                part0(rs_(1, 2 * g, 2), 1)
+                part0(r2(g), 1)
+
+                @pl.when((y == 1) & (i < 20))
+                def _():
+                    x20(1, g).start()
+
+        each(0, 21, step)
+
+        @pl.when(y == 1)
+        def _():
+            d21.start()
+            for x in d20:
+                x.start()
+
+        @pl.when(y == 0)
+        def _():
+            m21(3).start()
+            m20(0, 3).start()
+            m20(1, 3).start()
+            wait_recv(XB.at[0, pl.ds(0, 96)], r_x.at[8])
+            r = rs_(1, 0, 6)
+            Pb[1, r, :] += XB[1, r, :]
+            for g in range(3):
                 m20(1, g).start()
-
-        each(0, 21, step)
 
     def d_fwd(t):
         h, s = t % 2, t // 2
@@ -300,40 +384,27 @@
     def wait_ysib(s):
         wait_recv(Y.at[1 - k, us_(s), UALL], r_d.at[s])
 
-    def s3(r, cols, n):
-        return rcopy(Pa.at[1, r, cols], R.at[y, r, cols], s_z.at[2], r_r.at[0], 3, k)
-
-    s3_a = [s3(pl.ds(b * half, half), C0, b) for b in range(2)]
-    s3_b = [[s3(rs_(h, 2 * u, 2), C1, 2 + 4 * h + u) for u in range(4)] for h in range(2)]
-
-    def s3_k1(s):
-        return s3(us_(s), CA, s)
-
-    def s2(h, s, n, cols, i):
-        r = rs_(h, s, n)
-        return rcopy(Pa.at[0, r, cols], R.at[0, r, cols], s_z.at[2], r_r.at[0], 2, k)
-
-    PART1 = ((0, 4), (4, 2), (6, 2))
-    PART0 = ((0, 6, C0), (0, 6, C1), (6, 2, CA))
-    s2_k1 = [[s2(h, s, n, CA, i) for i, (s, n) in enumerate(PART1)] for h in range(2)]
-    s2_k0 = [[s2(h, s, n, cols, i) for i, (s, n, cols) in enumerate(PART0)] for h in range(2)]
+    def s3(r):
+        return rcopy(Pa.at[1, r], R.at[y, r], s_z.at[2], r_r.at[0], 3, k)
+
+    s2 = rcopy(Pa.at[0], R.at[0], s_z.at[2], r_r.at[0], 2, k)
+
+    def add(i, r, cols):
+        Pa[i, r, cols] += PR[i, r, cols]
 
     def wait_pr(n, cols, sem):
         wait_recv(PR.at[0, pl.ds(0, n), cols], r_p.at[sem])
-
-    def add(i, r, cols):
-        Pa[i, r, cols] += PR[i, r, cols]
-
-    def y1_start(x):
-        @pl.when(y == 1)
-        def _():
-            x.start()
 
     def strip31(s):
         wait_ysib(s)
         r = us_(s)
-        Pa[1, r, :] = PR[1, r, :] + mm(Y[0, r, UALL], W[0, :, :ku]) + mm(Y[1, r, UALL], W[1, :, :ku])
-        s3_k1(s).start()
+        Pa[1, r, :] = mm(Y[0, r, UALL], W[0, :, :ku]) + mm(Y[1, r, UALL], W[1, :, :ku])
+
+        @pl.when(y == 0)
+        def _():
+            add(1, r, CA)
+
+        s3(r).start()
 
     @pl.when(z == 2)
     def _():
@@ -352,69 +423,88 @@
         each(0, 2 * NS, step_d)
         each(2, 2 * NS, lambda t: z2_d(t).start())
 
+        pl.semaphore_wait(far, n_near)
+
         @pl.when(k == 1)
         def _():
             y2(NU, XU)
 
-        pl.semaphore_wait(far, n_near)
+            @pl.when(y == 1)
+            def _():
+                s2.start()
+
+
+        def q1(s):
+            Qa[1, us_(s), :] = mm(Y[k, us_(s), :], X[k])
+            q1send(s).start()
 
         def step_u(s):
             wait_recv(Y.at[k, us_(s), UALL], r_y.at[2 * NS + s])
             u_sib(s).start()
-            Qa[1, us_(s), :] = mm(Y[k, us_(s), :], X[k])
-            q1send(s).start()
 
             @pl.when((k == 0) & (s >= 1))
             def _():
-                y2(2 * s - 2)
                 y2(2 * s - 1)
 
+            @pl.when(k == 0)
+            def _():
+                y2(2 * s)
+
             @pl.when((k == 0) & (s == 4))
             def _():
                 each(0, 4, wait_ysib)
-                each(0, 6, lambda q: y3(0, q))
+                each(0, 7, lambda q: y3(0, q))
 
             @pl.when((k == 0) & (s >= 4))
             def _():
-                y3(0, 2 * s - 2)
                 y3(0, 2 * s - 1)
-
-            @pl.when((k == 1) & (s == 2))
+                y3(0, 2 * s)
+
+            @pl.when((k == 1) & (y == 0) & (s == 4))
             def _():
                 wait_recv(PR.at[1], r_p.at[0])
 
-            @pl.when((k == 1) & (s >= 2))
-            def _():
-                strip31(s - 2)
+            @pl.when((k == 1) & (s >= 4) & (s <= 6))
+            def _():
+                strip31(2 * s - 8)
+                strip31(2 * s - 7)
+
+            @pl.when(s < NS - 1)
+            def _():
+                q1(s)
 
         each(0, NS, step_u)
 
-        def add21(gs, i):
-            wait_pr(64 * len(gs), CA, 1 + i)
-            for h in range(2):
-                add(0, rs_(h, 2 * gs[0], 2 * len(gs)), CA)
-                y1_start(s2_k1[h][i])
-
         @pl.when(k == 1)
         def _():
-            add21((0, 1), 0)
             each(NS - 2, NS, strip31)
-            add21((2,), 1)
-            add21((3,), 2)
+            q1(NS - 1)
+
+            @pl.when(y == 0)
+            def _():
+                wait_pr(192, CA, 1)
+                for h in range(2):
+                    add(0, rs_(h, 0, 6), CA)
+                wait_pr(64, CA, 2)
+                for h in range(2):
+                    add(0, rs_(h, 6, 2), CA)
 
         @pl.when(k == 0)
         def _():
-            y2(NU - 1)
             y2(NU, XU)
-            y3(0, NU - 1)
+
+            @pl.when(y == 1)
+            def _():
+                s2.start()
+
             y3(0, NU, XU)
-            wait_pr(rows, C0, 0)
-            add(1, pl.ds(0, half), C0)
-            s3_a[0].start()
-            wait_pr(192, C0, 5)
-            for h in range(2):
-                add(0, rs_(h, 0, 6), C0)
-                y1_start(s2_k0[h][0])
+
+            @pl.when(y == 0)
+            def _():
+                wait_pr(rows, C0, 0)
+                add(1, pl.ds(0, half), C0)
+
+            s3(pl.ds(0, half)).start()
             each(4, NS, wait_ysib)
 
             def low(b):
@@ -422,23 +512,27 @@
                 Pa[1, r, :] = mm(Y[0, r, UALL], W[0, :, :ku]) + mm(Y[1, r, UALL], W[1, :, :ku])
 
             each(1 + k, 2, low)
-            add(1, pl.ds(half, half), C0)
-            s3_a[1].start()
-            for u in range(4):
-                wait_pr(64, C1, 1 + u)
+
+            @pl.when(y == 0)
+            def _():
+                add(1, pl.ds(half, half), C0)
+
+            s3(pl.ds(half, half)).start()
+            q1(NS - 1)
+
+            @pl.when(y == 0)
+            def _():
+                wait_pr(192, C0, 1)
                 for h in range(2):
-                    add(1, rs_(h, 2 * u, 2), C1)
-                    s3_b[h][u].start()
-            wait_pr(192, C1, 6)
-            for h in range(2):
-                add(0, rs_(h, 0, 6), C1)
-                y1_start(s2_k0[h][1])
-            wait_pr(64, CA, 7)
-            for h in range(2):
-                add(0, rs_(h, 6, 2), CA)
-                y1_start(s2_k0[h][2])
-
-    @pl.when(z != 2)
+                    add(0, rs_(h, 0, 6), C0)
+                wait_pr(64, CA, 3)
+                for h in range(2):
+                    add(0, rs_(h, 6, 2), CA)
+                wait_pr(192, C1, 2)
+                for h in range(2):
+                    add(0, rs_(h, 0, 6), C1)
+
+    @pl.when((z == 0) | (z == 3))
     def _():
         pl.semaphore_wait(far, n_near)
 
@@ -462,6 +556,9 @@
     @pl.when((z == 2) & (y == 0))
     def _():
         wait_recv(R.at[0], r_r.at[0])
+        wait_recv(R.at[1, pl.ds(0, 64)], r_r.at[1])
+        for h in range(2):
+            Pa[0, rs_(h, 6, 2), :] += R[1, rs_(h, 6, 2), :]
         o_ref[...] = (Pa[0] + R[0]).astype(o_ref.dtype)
 
     @pl.when((z == 3) & (c == 2))
@@ -472,6 +569,12 @@
     @pl.when((z == 3) & (y == 0))
     def _():
         wait_recv(R.at[pl.ds(0, 2)], r_r.at[0])
+
+        @pl.when(k == 0)
+        def _():
+            wait_recv(R.at[2, :, C1], r_r.at[1])
+            R[0, :, C1] += R[2, :, C1]
+
         o_ref[...] = (R[0] + R[1]).astype(o_ref.dtype)
 
     @pl.when(c != z)
@@ -530,8 +633,10 @@
                 pltpu.VMEM((2, rows, rows // 2), f32),
                 pltpu.VMEM((4, rows, rows), f32),
                 pltpu.VMEM((2, rows, rows), f32),
+                pltpu.VMEM((rows, rows), f32),
+                pltpu.VMEM((2, rows, rows // 2), f32),
                 pltpu.SemaphoreType.REGULAR,
-                dma((1,)), dma((5,)), dma((4 * NS,)), dma((NS + 1,)), dma((NU + 1,)), dma((8,)), dma((2,)),
+                dma((1,)), dma((5,)), dma((4 * NS,)), dma((NS + 1,)), dma((NU + 1,)), dma((4,)), dma((2,)), dma((9,)),
             ],
             compiler_params=pltpu.CompilerParams(
                 collective_id=0, has_side_effects=True, vmem_limit_bytes=56 * 1024 * 1024),

time: 107 us -> 107 us (level); the launches traced: 106 us -> 105 us
  Pallas kernels: 106 us -> 104 us
    pallas_call x1, Pallas kernels: 106 us -> 104 us  [local_fn(): pl.pallas_call(kernel, out_shape=pltpu.VMEM((rows, rows), bf16), in_specs...]
where the time goes in v7:
time: 107 us; the launch traced here: 105 us
  Pallas kernels  104 us (97%)
    pallas_call x1, Pallas kernels, local_fn(): pl.pallas_call(kernel, out_shape=pltpu.VMEM((rows, rows), bf16), in_specs...  104 us

profile of v7, /device:TPU:24, one launch (start us, length us, event | category | flops | bytes accessed | tf_op | source)
XLA Modules:
  0.0 104.6 jit_solution(991134502700917702)
XLA Ops:
  0.0 103.9 %shard_map.17 = bf16[256,256]{1,0:T(8,128)(2,1)S(1)} custom-call(bf16[256,8192]{1,0:T(8,128)(2,1)} %a_ref.1), custom_call_target="tpu_custom_call" | custom-call | tf_op jit(solution)/shard_map/pallas_call | solution.py:619
  103.9 0.7 copy.3

commit v8 on v7

--- a/solution.py
+++ b/solution.py
@@ -20,7 +20,7 @@
     return lax.dot_general(a, b, (((1,), (0,)), ((), ())), preferred_element_type=jnp.float32)
 
 
-def kernel(a_ref, o_ref, X, Y, W, T0, T1, Pa, Pb, Qa, Qb, R, PR, XA, XB, far, ld, s_z, r_y, r_d, r_w, r_p, r_r, r_x):
+def kernel(a_ref, o_ref, X, Y, W, T0, T1, Pa, Pb, Qa, QD, R, PR, XA, XB, far, ld, s_z, r_y, r_d, r_w, r_p, r_r, r_x):
     rows, m = a_ref.shape
     ku = NU * PW + XU
     kd = m - ku
@@ -98,7 +98,7 @@
 
     def z2_d(t):
         h, s = t % 2, t // 2
-        return rcopy(a_ref.at[rs_(h, s), DALL], W.at[k, rs_(1, s), pl.ds(0, kd)], s_z.at[0], r_w.at[1 + s // 2], 1, 2 * y + h)
+        return rcopy(a_ref.at[rs_(h, s), DALL], W.at[k, rs_(1, s), pl.ds(0, kd)], s_z.at[0], r_w.at[jnp.where(s < 6, 1 + s // 2, s - 2)], 1, 2 * y + h)
 
     @pl.when(z == 0)
     def _():
@@ -130,7 +130,6 @@
 
     Pa[...] = jnp.zeros_like(Pa)
     Qa[...] = jnp.zeros_like(Qa)
-    Qb[...] = jnp.zeros_like(Qb)
     load.wait()
     dq = jnp.where(z == 1, 1, 0)
 
@@ -154,9 +153,7 @@
 
     def zU(q, w=PW):
         wait_recv(Y.at[k, :, up(q, w)], r_y.at[q])
-        v = mm(X[k, :, up(q, w)], Y[k, :, up(q, w)])
-        Qb[0] += v[:, :half]
-        Qb[1] += v[:, half:]
+        Qa[0] += mm(X[k, :, up(q, w)], Y[k, :, up(q, w)])
 
     def turn(p, w=PW):
         for h in range(2):
@@ -181,8 +178,8 @@
     def r3(u):
         return rs_(0, 4 * u, 4)
 
-    def r2(g):
-        return rs_(1, 2 * g, 2)
+    def r2(s, n=2):
+        return rs_(1, s, n)
 
     def xsend(src, dst, n):
         return rcopy(src, dst, s_z.at[2], r_x.at[n], 1, peer)
@@ -192,11 +189,11 @@
     def x30(b, u):
         return xsend(Pb.at[b, r3(u)], XB.at[b, r3(u)], 1 + 2 * b + u)
 
-    def x21(g):
-        return xsend(Pa.at[1, r2(g)], XA.at[r2(g)], 5 + g)
-
-    def x20(b, g):
-        return xsend(Pb.at[b, r2(g)], XB.at[b, r2(g)], jnp.where(b == 0, 5 + g, 8))
+    def x21(s, n, rs):
+        return xsend(Pa.at[1, r2(s, n)], XA.at[r2(s, n)], rs)
+
+    def x20(b, s, n, rs):
+        return xsend(Pb.at[b, r2(s, n)], XB.at[b, r2(s, n)], rs)
 
     def msend(src, i, s, n, j, cols, rs):
         return rcopy(src, PR.at[i, rs_(k, s, n), cols], s_z.at[2], r_p.at[rs], 2, j)
@@ -207,19 +204,19 @@
         src = Pb.at[b, r3(u)]
         if b == 0:
             return msend(src, 1, 4 * u, 4, 0, C0, 0)
-        return rcopy(src, R.at[2, rs_(k, 4 * u, 4), C1], s_z.at[2], r_r.at[1], 3, 0)
-
-    def m21(g):
-        return msend(Pa.at[1, r2(g)], 0, 2 * g, 2, 1, CA, jnp.where(g == 3, 2, 1))
-
-    def m20(b, g):
-        return msend(Pb.at[b, r2(g)], 0, 2 * g, 2, 0, COLS[b], jnp.where(g == 3, 3, 1 + b))
+        return rcopy(src, R.at[2 + y, rs_(k, 4 * u, 4), C1], s_z.at[2], r_r.at[1], 3, 0)
+
+    def m21(s, n, rs):
+        return msend(Pa.at[1, r2(s, n)], 0, s, n, 1, CA, rs)
+
+    def m20(b, s, n, rs):
+        return msend(Pb.at[b, r2(s, n)], 0, s, n, 0, COLS[b], rs)
 
     def d2(src, j, cols):
-        return rcopy(src, R.at[1, rs_(k, 6, 2), cols], s_z.at[2], r_r.at[1], 2, j)
-
-    d21 = d2(Pa.at[1, r2(3)], 1, CA)
-    d20 = [d2(Pb.at[b, r2(3)], 0, COLS[b]) for b in range(2)]
+        return rcopy(src, R.at[1, rs_(k, 7), cols], s_z.at[2], r_r.at[1], 2, j)
+
+    d21 = d2(Pa.at[1, r2(7, 1)], 1, CA)
+    d20 = [d2(Pb.at[b, r2(7, 1)], 0, COLS[b]) for b in range(2)]
 
     def part1(r):
         Pa[1, r, :] = mn(W[0, r, :kd], T1[0]) + mn(W[1, r, :kd], T1[1])
@@ -227,8 +224,10 @@
     def part0(r, b):
         Pb[b, r, :] = mn(W[0, r, :kd], T0[0, b]) + mn(W[1, r, :kd], T0[1, b])
 
-    def q0send(b):
-        return rcopy(Qb.at[b], R.at[slot(0), :, COLS[b]], s_z.at[4], r_r.at[b], 1, 0)
+    q_u = rcopy(Qa.at[0], R.at[slot(0)], s_z.at[4], r_r.at[0], 1, 0)
+
+    def q_d(b):
+        return rcopy(QD.at[b], PR.at[y, rs_(k, 0, NS), COLS[b]], s_z.at[4], r_r.at[1], 1, 0)
 
     @pl.when(z == 1)
     def _():
@@ -249,13 +248,11 @@
         if xd:
             turn(nd, xd)
 
+        @pl.when(c != 0)
+        def _():
+            q_u.start()
+
         pl.semaphore_wait(far, n_near)
-
-        def merge30(b):
-            for u in range(2):
-                wait_recv(XB.at[b, r3(u)], r_x.at[1 + 2 * b + u])
-                Pb[b, r3(u), :] += XB[b, r3(u), :]
-                m30(b, u).start()
 
         def step(i):
             @pl.when(i < 2 * NS)
@@ -286,20 +283,25 @@
                 for h in range(2):
                     T0[h, b] = Y[h, brows(b), DALL].T
                 part0(rs_(0, 0, NS), b)
-                for bb in range(2):
-                    @pl.when((b == bb) & (y == 1))
-                    def _():
-                        for u in range(2):
-                            x30(bb, u).start()
-
-            @pl.when((i == 7) | (i == 19))
+                @pl.when((b == 0) & (y == 1))
+                def _():
+                    for u in range(2):
+                        x30(0, u).start()
+
+                @pl.when(b == 1)
+                def _():
+                    for u in range(2):
+                        m30(1, u).start()
+
+            @pl.when((i == 7) | (i == 20))
             def _():
                 b = jnp.where(i == 7, 0, 1)
-                Qb[b] += mm(X[k, :, DALL], Y[k, brows(b), DALL])
+                r = rs_(k, 0, NS)
+                QD[b] = mn(X[0, r, DALL], T0[0, b]) + mn(X[1, r, DALL], T0[1, b])
                 for bb in range(2):
                     @pl.when((b == bb) & (c != 0))
                     def _():
-                        q0send(bb).start()
+                        q_d(bb).start()
 
             @pl.when(i == 7)
             def _():
@@ -308,43 +310,62 @@
 
             @pl.when((i == 9) & (y == 0))
             def _():
-                merge30(0)
-
-            @pl.when((i == 20) & (y == 0))
-            def _():
-                merge30(1)
-
-            @pl.when((i == 8) | (i == 9) | (i == 13) | (i == 20))
-            def _():
-                g = jnp.where(i == 20, 3, jnp.where(i == 13, 2, i - 8))
-                wait_w(r2(g), 1 + g)
-                part1(r2(g))
-                part0(r2(g), 0)
-
-                @pl.when((y == 1) & (i < 20))
+                for u in range(2):
+                    wait_recv(XB.at[0, r3(u)], r_x.at[1 + u])
+                    Pb[0, r3(u), :] += XB[0, r3(u), :]
+                    m30(0, u).start()
+
+            @pl.when((i == 8) | (i == 9) | (i == 13))
+            def _():
+                g = jnp.where(i == 13, 2, i - 8)
+                wait_w(r2(2 * g), 1 + g)
+                part1(r2(2 * g))
+                part0(r2(2 * g), 0)
+
+                @pl.when(y == 1)
                 def _():
-                    x21(g).start()
-                    x20(0, g).start()
+                    x21(2 * g, 2, 5 + g).start()
+                    x20(0, 2 * g, 2, 5 + g).start()
 
             @pl.when(((i == 10) | (i == 11) | (i == 15)) & (y == 0))
             def _():
                 g = jnp.where(i == 15, 2, i - 10)
                 wait_recv(XA.at[pl.ds(0, 48)], r_x.at[5 + g])
-                Pa[1, r2(g), :] += XA[r2(g), :]
-                Pb[0, r2(g), :] += XB[0, r2(g), :]
-                m21(g).start()
-                m20(0, g).start()
-
-            @pl.when(i >= 17)
+                Pa[1, r2(2 * g), :] += XA[r2(2 * g), :]
+                Pb[0, r2(2 * g), :] += XB[0, r2(2 * g), :]
+                m21(2 * g, 2, 1).start()
+                m20(0, 2 * g, 2, 1).start()
+
+            @pl.when((i >= 17) & (i < 20))
             def _():
                 g = i - 17
-                part0(r2(g), 1)
-
-                @pl.when((y == 1) & (i < 20))
+                part0(r2(2 * g), 1)
+
+                @pl.when(y == 1)
                 def _():
-                    x20(1, g).start()
-
-        each(0, 21, step)
+                    x20(1, 2 * g, 2, 8).start()
+
+            @pl.when((i == 14) | (i == 21))
+            def _():
+                t = jnp.where(i == 14, 6, 7)
+                wait_w(r2(t, 1), t - 2)
+                part1(r2(t, 1))
+                part0(r2(t, 1), 0)
+
+                @pl.when((y == 1) & (i == 14))
+                def _():
+                    x21(6, 1, 8).start()
+                    x20(0, 6, 1, 8).start()
+
+            @pl.when(i >= 20)
+            def _():
+                part0(r2(i - 14, 1), 1)
+
+                @pl.when((y == 1) & (i == 20))
+                def _():
+                    x20(1, 6, 1, 8).start()
+
+        each(0, 22, step)
 
         @pl.when(y == 1)
         def _():
@@ -354,14 +375,16 @@
 
         @pl.when(y == 0)
         def _():
-            m21(3).start()
-            m20(0, 3).start()
-            m20(1, 3).start()
-            wait_recv(XB.at[0, pl.ds(0, 96)], r_x.at[8])
-            r = rs_(1, 0, 6)
-            Pb[1, r, :] += XB[1, r, :]
-            for g in range(3):
-                m20(1, g).start()
+            m21(7, 1, 2).start()
+            m20(0, 7, 1, 3).start()
+            m20(1, 7, 1, 3).start()
+            wait_recv(XA.at[pl.ds(0, 80)], r_x.at[8])
+            Pb[1, r2(0, 7), :] += XB[1, r2(0, 7), :]
+            m20(1, 0, 7, 2).start()
+            Pa[1, r2(6, 1), :] += XA[r2(6, 1), :]
+            m21(6, 1, 2).start()
+            Pb[0, r2(6, 1), :] += XB[0, r2(6, 1), :]
+            m20(0, 6, 1, 3).start()
 
     def d_fwd(t):
         h, s = t % 2, t // 2
@@ -466,10 +489,9 @@
 
             @pl.when((k == 1) & (s >= 4) & (s <= 6))
             def _():
-                strip31(2 * s - 8)
-                strip31(2 * s - 7)
-
-            @pl.when(s < NS - 1)
+                each(2 * s - 8, 2 * s - 6, strip31)
+
+            @pl.when((k == 1) | (s < NS - 1))
             def _():
                 q1(s)
 
@@ -478,7 +500,6 @@
         @pl.when(k == 1)
         def _():
             each(NS - 2, NS, strip31)
-            q1(NS - 1)
 
             @pl.when(y == 0)
             def _():
@@ -505,6 +526,7 @@
                 add(1, pl.ds(0, half), C0)
 
             s3(pl.ds(0, half)).start()
+            each(NS - 1, NS + k, q1)
             each(4, NS, wait_ysib)
 
             def low(b):
@@ -518,19 +540,19 @@
                 add(1, pl.ds(half, half), C0)
 
             s3(pl.ds(half, half)).start()
-            q1(NS - 1)
 
             @pl.when(y == 0)
             def _():
                 wait_pr(192, C0, 1)
                 for h in range(2):
                     add(0, rs_(h, 0, 6), C0)
-                wait_pr(64, CA, 3)
+                wait_pr(224, C1, 2)
                 for h in range(2):
-                    add(0, rs_(h, 6, 2), CA)
-                wait_pr(192, C1, 2)
+                    add(0, rs_(h, 0, 7), C1)
+                wait_pr(96, C0, 3)
                 for h in range(2):
-                    add(0, rs_(h, 0, 6), C1)
+                    add(0, rs_(h, 6, 2), C0)
+                    add(0, rs_(h, 7), C1)
 
     @pl.when((z == 0) | (z == 3))
     def _():
@@ -549,16 +571,19 @@
 
     @pl.when((z == 1) & (c == 0))
     def _():
+        wait_recv(R.at[pl.ds(0, 3)], r_r.at[0])
+        Qa[0] += R[0] + R[1] + R[2]
+        wait_recv(R.at[pl.ds(0, 3), pl.ds(0, half)], r_r.at[1])
         for b in range(2):
-            wait_recv(R.at[pl.ds(0, 3), :, COLS[b]], r_r.at[b])
-            o_ref[:, COLS[b]] = (Qb[b] + R[0, :, COLS[b]] + R[1, :, COLS[b]] + R[2, :, COLS[b]]).astype(o_ref.dtype)
+            PR[0, pl.ds(0, half), COLS[b]] = QD[b]
+        o_ref[...] = (Qa[0] + PR[0] + PR[1]).astype(o_ref.dtype)
 
     @pl.when((z == 2) & (y == 0))
     def _():
         wait_recv(R.at[0], r_r.at[0])
-        wait_recv(R.at[1, pl.ds(0, 64)], r_r.at[1])
+        wait_recv(R.at[1, pl.ds(0, 32)], r_r.at[1])
         for h in range(2):
-            Pa[0, rs_(h, 6, 2), :] += R[1, rs_(h, 6, 2), :]
+            Pa[0, rs_(h, 7), :] += R[1, rs_(h, 7), :]
         o_ref[...] = (Pa[0] + R[0]).astype(o_ref.dtype)
 
     @pl.when((z == 3) & (c == 2))
@@ -572,8 +597,8 @@
 
         @pl.when(k == 0)
         def _():
-            wait_recv(R.at[2, :, C1], r_r.at[1])
-            R[0, :, C1] += R[2, :, C1]
+            wait_recv(R.at[2], r_r.at[1])
+            R[0, :, C1] += R[2, :, C1] + R[3, :, C1]
 
         o_ref[...] = (R[0] + R[1]).astype(o_ref.dtype)
 
@@ -593,7 +618,7 @@
 
         @pl.when(c != 0)
         def _():
-            wait_recv(Qb, s_z.at[4])
+            wait_recv(R.at[pl.ds(0, 3), pl.ds(0, half)], s_z.at[4])
 
     @pl.when(z == 2)
     def _():
@@ -630,7 +655,7 @@
                 pltpu.VMEM((2, rows, rows), f32),
                 pltpu.VMEM((2, rows, rows // 2), f32),
                 pltpu.VMEM((2, rows, rows), f32),
-                pltpu.VMEM((2, rows, rows // 2), f32),
+                pltpu.VMEM((2, rows // 2, rows // 2), f32),
                 pltpu.VMEM((4, rows, rows), f32),
                 pltpu.VMEM((2, rows, rows), f32),
                 pltpu.VMEM((rows, rows), f32),

time: 107 us -> 106 us (level)
  no operation moved by 1% of the time
where the time goes in v8:
time: 106 us; the launch traced here: 105 us
  Pallas kernels  104 us (98%)
    pallas_call x1, Pallas kernels, local_fn(): pl.pallas_call(kernel, out_shape=pltpu.VMEM((rows, rows), bf16), in_specs...  104 us

profile of v8, /device:TPU:24, one launch (start us, length us, event | category | flops | bytes accessed | tf_op | source)
XLA Modules:
  0.0 104.6 jit_solution(14214383111185554652)
XLA Ops:
  0.0 104.0 %shard_map.17 = bf16[256,256]{1,0:T(8,128)(2,1)S(1)} custom-call(bf16[256,8192]{1,0:T(8,128)(2,1)} %a_ref.1), custom_call_target="tpu_custom_call" | custom-call | tf_op jit(solution)/shard_map/pallas_call | solution.py:644
  104.0 0.7 copy.3

commit v9 on v8

--- a/solution.py
+++ b/solution.py
@@ -130,6 +130,7 @@
 
     Pa[...] = jnp.zeros_like(Pa)
     Qa[...] = jnp.zeros_like(Qa)
+    Pb[...] = jnp.zeros_like(Pb)
     load.wait()
     dq = jnp.where(z == 1, 1, 0)
 
@@ -204,7 +205,10 @@
         src = Pb.at[b, r3(u)]
         if b == 0:
             return msend(src, 1, 4 * u, 4, 0, C0, 0)
-        return rcopy(src, R.at[2 + y, rs_(k, 4 * u, 4), C1], s_z.at[2], r_r.at[1], 3, 0)
+        return rcopy(src, R.at[2, rs_(k, 4 * u, 4), C1], s_z.at[2], r_r.at[1], 3, 0)
+
+    def m30r(u):
+        return rcopy(Pb.at[1, r3(u)], PR.at[1, rs_(k, 4 * u, 4), C1], s_z.at[2], r_p.at[1 + u], 2, 2)
 
     def m21(s, n, rs):
         return msend(Pa.at[1, r2(s, n)], 0, s, n, 1, CA, rs)
@@ -276,24 +280,51 @@
                 Pa[1, rs_(0, 0, NS), :] += XA[rs_(0, 0, NS), :]
                 m31.start()
 
-            @pl.when((i == 7) | (i == 16))
-            def _():
-                b = jnp.where(i == 7, 0, 1)
-                wait_recv(Y.at[1 - k, brows(b), DALL], r_d.at[b])
-                for h in range(2):
-                    T0[h, b] = Y[h, brows(b), DALL].T
-                part0(rs_(0, 0, NS), b)
-                @pl.when((b == 0) & (y == 1))
-                def _():
-                    for u in range(2):
-                        x30(0, u).start()
-
-                @pl.when(b == 1)
+            @pl.when(i == 16)
+            def _():
+                def chunk(n):
+                    ch = jnp.where(n == 0, k, 1 - k)
+
+                    @pl.when(n == 1)
+                    def _():
+                        wait_recv(Y.at[1 - k, brows(1), DALL], r_d.at[1])
+
+                    Pb[1, pl.ds(0, rows - st), :] += mm(W[ch, pl.ds(0, rows - st), :kd], Y[ch, brows(1), DALL])
+
+                each(0, 2, chunk)
+
+                @pl.when(y == 0)
                 def _():
                     for u in range(2):
                         m30(1, u).start()
 
-            @pl.when((i == 7) | (i == 20))
+                @pl.when(y == 1)
+                def _():
+                    for u in range(2):
+                        m30r(u).start()
+                    x20(1, 0, 7, 8).start()
+
+            @pl.when((i == 7) | (i == 17))
+            def _():
+                b = jnp.where(i == 7, 0, 1)
+
+                @pl.when(b == 0)
+                def _():
+                    wait_recv(Y.at[1 - k, brows(0), DALL], r_d.at[0])
+
+                for h in range(2):
+                    T0[h, b] = Y[h, brows(b), DALL].T
+
+                @pl.when(b == 0)
+                def _():
+                    part0(rs_(0, 0, NS), 0)
+
+                    @pl.when(y == 1)
+                    def _():
+                        for u in range(2):
+                            x30(0, u).start()
+
+            @pl.when((i == 7) | (i == 17))
             def _():
                 b = jnp.where(i == 7, 0, 1)
                 r = rs_(k, 0, NS)
@@ -336,16 +367,15 @@
                 m21(2 * g, 2, 1).start()
                 m20(0, 2 * g, 2, 1).start()
 
-            @pl.when((i >= 17) & (i < 20))
-            def _():
-                g = i - 17
-                part0(r2(2 * g), 1)
-
-                @pl.when(y == 1)
-                def _():
-                    x20(1, 2 * g, 2, 8).start()
-
-            @pl.when((i == 14) | (i == 21))
+            @pl.when((i == 17) & (y == 0))
+            def _():
+                wait_recv(XA.at[pl.ds(0, 24)], r_x.at[3])
+                Pa[1, r2(6, 1), :] += XA[r2(6, 1), :]
+                m21(6, 1, 2).start()
+                Pb[0, r2(6, 1), :] += XB[0, r2(6, 1), :]
+                m20(0, 6, 1, 3).start()
+
+            @pl.when((i == 14) | (i == 18))
             def _():
                 t = jnp.where(i == 14, 6, 7)
                 wait_w(r2(t, 1), t - 2)
@@ -354,18 +384,14 @@
 
                 @pl.when((y == 1) & (i == 14))
                 def _():
-                    x21(6, 1, 8).start()
-                    x20(0, 6, 1, 8).start()
-
-            @pl.when(i >= 20)
-            def _():
-                part0(r2(i - 14, 1), 1)
-
-                @pl.when((y == 1) & (i == 20))
+                    x21(6, 1, 3).start()
+                    x20(0, 6, 1, 3).start()
+
+                @pl.when(i == 18)
                 def _():
-                    x20(1, 6, 1, 8).start()
-
-        each(0, 22, step)
+                    part0(r2(7, 1), 1)
+
+        each(0, 19, step)
 
         @pl.when(y == 1)
         def _():
@@ -378,13 +404,9 @@
             m21(7, 1, 2).start()
             m20(0, 7, 1, 3).start()
             m20(1, 7, 1, 3).start()
-            wait_recv(XA.at[pl.ds(0, 80)], r_x.at[8])
+            wait_recv(XB.at[1, r2(0, 7)], r_x.at[8])
             Pb[1, r2(0, 7), :] += XB[1, r2(0, 7), :]
             m20(1, 0, 7, 2).start()
-            Pa[1, r2(6, 1), :] += XA[r2(6, 1), :]
-            m21(6, 1, 2).start()
-            Pb[0, r2(6, 1), :] += XB[0, r2(6, 1), :]
-            m20(0, 6, 1, 3).start()
 
     def d_fwd(t):
         h, s = t % 2, t // 2
@@ -411,6 +433,10 @@
         return rcopy(Pa.at[1, r], R.at[y, r], s_z.at[2], r_r.at[0], 3, k)
 
     s2 = rcopy(Pa.at[0], R.at[0], s_z.at[2], r_r.at[0], 2, k)
+
+    def relay(h, u):
+        r = rs_(h, 4 * u, 4)
+        return rcopy(PR.at[1, r, C1], R.at[3, r, C1], s_z.at[3], r_r.at[1], 3, 0)
 
     def add(i, r, cols):
         Pa[i, r, cols] += PR[i, r, cols]
@@ -540,6 +566,13 @@
                 add(1, pl.ds(half, half), C0)
 
             s3(pl.ds(half, half)).start()
+
+            @pl.when(y == 1)
+            def _():
+                for u in range(2):
+                    wait_pr(128, C1, 1 + u)
+                    for h in range(2):
+                        relay(h, u).start()
 
             @pl.when(y == 0)
             def _():
@@ -633,6 +666,10 @@
         @pl.when(y == 1)
         def _():
             wait_recv(Pa, s_z.at[2])
+
+            @pl.when(k == 0)
+            def _():
+                wait_recv(PR.at[1, :, C1], s_z.at[3])
 
 
 def solution(mesh):

time: 106 us -> 105 us (level)
  no operation moved by 1% of the time
where the time goes in v9:
time: 105 us; the launch traced here: 104 us
  Pallas kernels  104 us (99%)
    pallas_call x1, Pallas kernels, local_fn(): pl.pallas_call(kernel, out_shape=pltpu.VMEM((rows, rows), bf16), in_specs...  104 us

profile of v9, /device:TPU:24, one launch (start us, length us, event | category | flops | bytes accessed | tf_op | source)
XLA Modules:
  0.0 104.4 jit_solution(7911121983669713179)
XLA Ops:
  0.0 103.7 %shard_map.17 = bf16[256,256]{1,0:T(8,128)(2,1)S(1)} custom-call(bf16[256,8192]{1,0:T(8,128)(2,1)} %a_ref.1), custom_call_target="tpu_custom_call" | custom-call | tf_op jit(solution)/shard_map/pallas_call | solution.py:681
  103.8 0.7 copy.3

commit v10 on v9

--- a/solution.py
+++ b/solution.py
@@ -380,6 +380,15 @@
                 t = jnp.where(i == 14, 6, 7)
                 wait_w(r2(t, 1), t - 2)
                 part1(r2(t, 1))
+
+                @pl.when((y == 1) & (i == 18))
+                def _():
+                    d21.start()
+
+                @pl.when((y == 0) & (i == 18))
+                def _():
+                    m21(7, 1, 2).start()
+
                 part0(r2(t, 1), 0)
 
                 @pl.when((y == 1) & (i == 14))
@@ -387,26 +396,30 @@
                     x21(6, 1, 3).start()
                     x20(0, 6, 1, 3).start()
 
+                @pl.when((y == 1) & (i == 18))
+                def _():
+                    d20[0].start()
+
+                @pl.when((y == 0) & (i == 18))
+                def _():
+                    m20(0, 7, 1, 3).start()
+                    wait_recv(XB.at[1, r2(0, 7)], r_x.at[8])
+                    Pb[1, r2(0, 7), :] += XB[1, r2(0, 7), :]
+                    m20(1, 0, 7, 2).start()
+
                 @pl.when(i == 18)
                 def _():
                     part0(r2(7, 1), 1)
 
+                    @pl.when(y == 1)
+                    def _():
+                        d20[1].start()
+
+                    @pl.when(y == 0)
+                    def _():
+                        m20(1, 7, 1, 3).start()
+
         each(0, 19, step)
-
-        @pl.when(y == 1)
-        def _():
-            d21.start()
-            for x in d20:
-                x.start()
-
-        @pl.when(y == 0)
-        def _():
-            m21(7, 1, 2).start()
-            m20(0, 7, 1, 3).start()
-            m20(1, 7, 1, 3).start()
-            wait_recv(XB.at[1, r2(0, 7)], r_x.at[8])
-            Pb[1, r2(0, 7), :] += XB[1, r2(0, 7), :]
-            m20(1, 0, 7, 2).start()
 
     def d_fwd(t):
         h, s = t % 2, t // 2
@@ -433,6 +446,10 @@
         return rcopy(Pa.at[1, r], R.at[y, r], s_z.at[2], r_r.at[0], 3, k)
 
     s2 = rcopy(Pa.at[0], R.at[0], s_z.at[2], r_r.at[0], 2, k)
+
+    TOP = pl.ds(0, half)
+    hop1 = rcopy(Pa.at[1, TOP], PR.at[0, TOP], s_z.at[2], r_p.at[0], 3, 2)
+    hop2 = rcopy(PR.at[0, TOP], R.at[1, TOP], s_z.at[1], r_r.at[0], 3, 0)
 
     def relay(h, u):
         r = rs_(h, 4 * u, 4)
@@ -551,8 +568,15 @@
                 wait_pr(rows, C0, 0)
                 add(1, pl.ds(0, half), C0)
 
-            s3(pl.ds(0, half)).start()
-            each(NS - 1, NS + k, q1)
+
+            @pl.when(y == 0)
+            def _():
+                s3(pl.ds(0, half)).start()
+
+            @pl.when(y == 1)
+            def _():
+                hop1.start()
+
             each(4, NS, wait_ysib)
 
             def low(b):
@@ -566,6 +590,7 @@
                 add(1, pl.ds(half, half), C0)
 
             s3(pl.ds(half, half)).start()
+            each(NS - 1, NS + k, q1)
 
             @pl.when(y == 1)
             def _():
@@ -621,6 +646,8 @@
 
     @pl.when((z == 3) & (c == 2))
     def _():
+        wait_recv(PR.at[0, TOP], r_p.at[0])
+        hop2.start()
         wait_recv(R, r_r.at[0])
         o_ref[...] = (R[0] + R[1] + R[2] + R[3]).astype(o_ref.dtype)
 
@@ -642,6 +669,10 @@
     @pl.when((z == 0) | (z == 3))
     def _():
         wait_recv(X.at[k], s_z.at[0])
+
+    @pl.when((z == 3) & (c == 2))
+    def _():
+        wait_recv(PR.at[0, TOP], s_z.at[1])
 
     @pl.when(z == 1)
     def _():

time: 105 us -> 106 us (level)
  no operation moved by 1% of the time
where the time goes in v10:
time: 106 us; the launch traced here: 105 us
  Pallas kernels  105 us (99%)
    pallas_call x1, Pallas kernels, local_fn(): pl.pallas_call(kernel, out_shape=pltpu.VMEM((rows, rows), bf16), in_specs...  105 us

profile of v10, /device:TPU:24, one launch (start us, length us, event | category | flops | bytes accessed | tf_op | source)
XLA Modules:
  0.0 105.4 jit_solution(1631232493851646037)
XLA Ops:
  0.0 104.7 %shard_map.17 = bf16[256,256]{1,0:T(8,128)(2,1)S(1)} custom-call(bf16[256,8192]{1,0:T(8,128)(2,1)} %a_ref.1), custom_call_target="tpu_custom_call" | custom-call | tf_op jit(solution)/shard_map/pallas_call | solution.py:712
  104.7 0.7 copy.3

commit v11 on v10

--- a/solution.py
+++ b/solution.py
@@ -208,7 +208,7 @@
         return rcopy(src, R.at[2, rs_(k, 4 * u, 4), C1], s_z.at[2], r_r.at[1], 3, 0)
 
     def m30r(u):
-        return rcopy(Pb.at[1, r3(u)], PR.at[1, rs_(k, 4 * u, 4), C1], s_z.at[2], r_p.at[1 + u], 2, 2)
+        return rcopy(Pb.at[1, r3(u)], PR.at[1, rs_(k, 4 * u, 4), C1], s_z.at[2], r_p.at[1], 2, 2)
 
     def m21(s, n, rs):
         return msend(Pa.at[1, r2(s, n)], 0, s, n, 1, CA, rs)
@@ -442,18 +442,10 @@
     def wait_ysib(s):
         wait_recv(Y.at[1 - k, us_(s), UALL], r_d.at[s])
 
-    def s3(r):
-        return rcopy(Pa.at[1, r], R.at[y, r], s_z.at[2], r_r.at[0], 3, k)
+    def s3(r, cols=CA):
+        return rcopy(Pa.at[1, r, cols], R.at[y, r, cols], s_z.at[2], r_r.at[0], 3, k)
 
     s2 = rcopy(Pa.at[0], R.at[0], s_z.at[2], r_r.at[0], 2, k)
-
-    TOP = pl.ds(0, half)
-    hop1 = rcopy(Pa.at[1, TOP], PR.at[0, TOP], s_z.at[2], r_p.at[0], 3, 2)
-    hop2 = rcopy(PR.at[0, TOP], R.at[1, TOP], s_z.at[1], r_r.at[0], 3, 0)
-
-    def relay(h, u):
-        r = rs_(h, 4 * u, 4)
-        return rcopy(PR.at[1, r, C1], R.at[3, r, C1], s_z.at[3], r_r.at[1], 3, 0)
 
     def add(i, r, cols):
         Pa[i, r, cols] += PR[i, r, cols]
@@ -505,26 +497,26 @@
             q1send(s).start()
 
         def step_u(s):
+            @pl.when((k == 0) & (s >= 1))
+            def _():
+                y2(2 * s - 1)
+
+            @pl.when(k == 0)
+            def _():
+                y2(2 * s)
+
+            @pl.when((k == 0) & (s == 4))
+            def _():
+                each(0, 4, wait_ysib)
+                each(0, 7, lambda q: y3(0, q))
+
+            @pl.when((k == 0) & (s >= 4))
+            def _():
+                y3(0, 2 * s - 1)
+                y3(0, 2 * s)
+
             wait_recv(Y.at[k, us_(s), UALL], r_y.at[2 * NS + s])
             u_sib(s).start()
-
-            @pl.when((k == 0) & (s >= 1))
-            def _():
-                y2(2 * s - 1)
-
-            @pl.when(k == 0)
-            def _():
-                y2(2 * s)
-
-            @pl.when((k == 0) & (s == 4))
-            def _():
-                each(0, 4, wait_ysib)
-                each(0, 7, lambda q: y3(0, q))
-
-            @pl.when((k == 0) & (s >= 4))
-            def _():
-                y3(0, 2 * s - 1)
-                y3(0, 2 * s)
 
             @pl.when((k == 1) & (y == 0) & (s == 4))
             def _():
@@ -575,7 +567,7 @@
 
             @pl.when(y == 1)
             def _():
-                hop1.start()
+                s3(pl.ds(0, half), C0).start()
 
             each(4, NS, wait_ysib)
 
@@ -589,15 +581,21 @@
             def _():
                 add(1, pl.ds(half, half), C0)
 
-            s3(pl.ds(half, half)).start()
+            @pl.when(y == 0)
+            def _():
+                s3(pl.ds(half, half)).start()
+
+            @pl.when(y == 1)
+            def _():
+                s3(pl.ds(half, half), C0).start()
+
             each(NS - 1, NS + k, q1)
 
             @pl.when(y == 1)
             def _():
-                for u in range(2):
-                    wait_pr(128, C1, 1 + u)
-                    for h in range(2):
-                        relay(h, u).start()
+                wait_pr(rows, C1, 1)
+                add(1, CA, C1)
+                s3(CA, C1).start()
 
             @pl.when(y == 0)
             def _():
@@ -646,8 +644,6 @@
 
     @pl.when((z == 3) & (c == 2))
     def _():
-        wait_recv(PR.at[0, TOP], r_p.at[0])
-        hop2.start()
         wait_recv(R, r_r.at[0])
         o_ref[...] = (R[0] + R[1] + R[2] + R[3]).astype(o_ref.dtype)
 
@@ -657,8 +653,8 @@
 
         @pl.when(k == 0)
         def _():
-            wait_recv(R.at[2], r_r.at[1])
-            R[0, :, C1] += R[2, :, C1] + R[3, :, C1]
+            wait_recv(R.at[2, :, C1], r_r.at[1])
+            R[0, :, C1] += R[2, :, C1]
 
         o_ref[...] = (R[0] + R[1]).astype(o_ref.dtype)
 
@@ -669,10 +665,6 @@
     @pl.when((z == 0) | (z == 3))
     def _():
         wait_recv(X.at[k], s_z.at[0])
-
-    @pl.when((z == 3) & (c == 2))
-    def _():
-        wait_recv(PR.at[0, TOP], s_z.at[1])
 
     @pl.when(z == 1)
     def _():
@@ -697,10 +689,6 @@
         @pl.when(y == 1)
         def _():
             wait_recv(Pa, s_z.at[2])
-
-            @pl.when(k == 0)
-            def _():
-                wait_recv(PR.at[1, :, C1], s_z.at[3])
 
 
 def solution(mesh):

time: 106 us -> 104 us (0.981)
  Pallas kernels: 105 us -> 103 us
    pallas_call x1, Pallas kernels: 105 us -> 103 us  [local_fn(): pl.pallas_call(kernel, out_shape=pltpu.VMEM((rows, rows), bf16), in_specs...]
where the time goes in v11:
time: 104 us; the launch traced here: 103 us
  Pallas kernels  103 us (99%)
    pallas_call x1, Pallas kernels, local_fn(): pl.pallas_call(kernel, out_shape=pltpu.VMEM((rows, rows), bf16), in_specs...  103 us

profile of v11, /device:TPU:24, one launch (start us, length us, event | category | flops | bytes accessed | tf_op | source)
XLA Modules:
  0.0 103.5 jit_solution(8550188890689738966)
XLA Ops:
  0.0 102.8 %shard_map.17 = bf16[256,256]{1,0:T(8,128)(2,1)S(1)} custom-call(bf16[256,8192]{1,0:T(8,128)(2,1)} %a_ref.1), custom_call_target="tpu_custom_call" | custom-call | tf_op jit(solution)/shard_map/pallas_call | solution.py:700
  102.8 0.7 copy.3

commit v12 on v11

--- a/solution.py
+++ b/solution.py
@@ -62,7 +62,6 @@
         lax.fori_loop(lo, hi, lambda i, u: (fn(i), u)[1], 0)
 
     load = pltpu.make_async_copy(a_ref, X.at[k], ld.at[0])
-    load.start()
 
     def near(sem):
         for dz in (-1, 1):
@@ -76,6 +75,7 @@
     n_near = jnp.where((z == 0) | (z == 3), 5, 7)
     bar = pltpu.get_barrier_semaphore()
     near(bar)
+    load.start()
     pl.semaphore_wait(bar, n_near)
 
     def z0_u(q, w=PW):
@@ -208,7 +208,7 @@
         return rcopy(src, R.at[2, rs_(k, 4 * u, 4), C1], s_z.at[2], r_r.at[1], 3, 0)
 
     def m30r(u):
-        return rcopy(Pb.at[1, r3(u)], PR.at[1, rs_(k, 4 * u, 4), C1], s_z.at[2], r_p.at[1], 2, 2)
+        return rcopy(Pb.at[1, r3(u)], PR.at[1, rs_(k, 4 * u, 4), C1], s_z.at[2], r_p.at[1 + u], 2, 2)
 
     def m21(s, n, rs):
         return msend(Pa.at[1, r2(s, n)], 0, s, n, 1, CA, rs)
@@ -478,6 +478,9 @@
             def _():
                 y2(t - 1)
 
+            r = rs_(t % 2, t // 2)
+            Qa[1, r, :] = mm(Y[k, r, DALL], X[k, :, DALL])
+
         each(0, 2 * NS, step_d)
         each(2, 2 * NS, lambda t: z2_d(t).start())
 
@@ -493,7 +496,7 @@
 
 
         def q1(s):
-            Qa[1, us_(s), :] = mm(Y[k, us_(s), :], X[k])
+            Qa[1, us_(s), :] += mm(Y[k, us_(s), UALL], X[k, :, UALL])
             q1send(s).start()
 
         def step_u(s):
@@ -593,9 +596,11 @@
 
             @pl.when(y == 1)
             def _():
-                wait_pr(rows, C1, 1)
-                add(1, CA, C1)
-                s3(CA, C1).start()
+                for u in range(2):
+                    wait_pr(half, C1, 1 + u)
+                    for h in range(2):
+                        add(1, rs_(h, 4 * u, 4), C1)
+                        s3(rs_(h, 4 * u, 4), C1).start()
 
             @pl.when(y == 0)
             def _():

time: 104 us -> 103 us (level)
  no operation moved by 1% of the time
where the time goes in v12:
time: 103 us
  Pallas kernels  102 us (99%)
    pallas_call x1, Pallas kernels, local_fn(): pl.pallas_call(kernel, out_shape=pltpu.VMEM((rows, rows), bf16), in_specs...  102 us

profile of v12, /device:TPU:24, one launch (start us, length us, event | category | flops | bytes accessed | tf_op | source)
XLA Modules:
  0.0 103.1 jit_solution(2802904024052371925)
XLA Ops:
  0.0 102.4 %shard_map.17 = bf16[256,256]{1,0:T(8,128)(2,1)S(1)} custom-call(bf16[256,8192]{1,0:T(8,128)(2,1)} %a_ref.1), custom_call_target="tpu_custom_call" | custom-call | tf_op jit(solution)/shard_map/pallas_call | solution.py:705
  102.4 0.7 copy.3

commit v13 on v12

--- a/solution.py
+++ b/solution.py
@@ -199,7 +199,7 @@
     def msend(src, i, s, n, j, cols, rs):
         return rcopy(src, PR.at[i, rs_(k, s, n), cols], s_z.at[2], r_p.at[rs], 2, j)
 
-    m31 = msend(Pa.at[1, rs_(0, 0, NS)], 1, 0, NS, 1, CA, 0)
+    m31 = msend(Pa.at[1, rs_(0, 0, NS)], 1, 0, NS, 3, CA, 0)
 
     def m30(b, u):
         src = Pb.at[b, r3(u)]
@@ -268,13 +268,13 @@
                 wait_w(rs_(0, 0, NS), 0)
                 part1(rs_(0, 0, NS))
 
-                @pl.when(y == 1)
+                @pl.when(y == 0)
                 def _():
                     x31.start()
 
                 each(5, 10, lambda q: u_fwd(q).start())
 
-            @pl.when((i == 5) & (y == 0))
+            @pl.when((i == 5) & (y == 1))
             def _():
                 wait_recv(XA.at[rs_(0, 0, NS)], r_x.at[0])
                 Pa[1, rs_(0, 0, NS), :] += XA[rs_(0, 0, NS), :]
@@ -458,7 +458,7 @@
         r = us_(s)
         Pa[1, r, :] = mm(Y[0, r, UALL], W[0, :, :ku]) + mm(Y[1, r, UALL], W[1, :, :ku])
 
-        @pl.when(y == 0)
+        @pl.when(y == 1)
         def _():
             add(1, r, CA)
 
@@ -521,7 +521,7 @@
             wait_recv(Y.at[k, us_(s), UALL], r_y.at[2 * NS + s])
             u_sib(s).start()
 
-            @pl.when((k == 1) & (y == 0) & (s == 4))
+            @pl.when((k == 1) & (y == 1) & (s == 4))
             def _():
                 wait_recv(PR.at[1], r_p.at[0])
 
@@ -557,6 +557,7 @@
                 s2.start()
 
             y3(0, NU, XU)
+            each(NS - 1, NS - y, q1)
 
             @pl.when(y == 0)
             def _():
@@ -592,7 +593,7 @@
             def _():
                 s3(pl.ds(half, half), C0).start()
 
-            each(NS - 1, NS + k, q1)
+            each(NS - 1, NS - 1 + y, q1)
 
             @pl.when(y == 1)
             def _():

time: 103 us -> 103 us (level)
  no operation moved by 1% of the time
where the time goes in v13:
time: 103 us
  Pallas kernels  102 us (99%)
    pallas_call x1, Pallas kernels, local_fn(): pl.pallas_call(kernel, out_shape=pltpu.VMEM((rows, rows), bf16), in_specs...  102 us

profile of v13, /device:TPU:24, one launch (start us, length us, event | category | flops | bytes accessed | tf_op | source)
XLA Modules:
  0.0 103.1 jit_solution(15913041839121560356)
XLA Ops:
  0.0 102.4 %shard_map.17 = bf16[256,256]{1,0:T(8,128)(2,1)S(1)} custom-call(bf16[256,8192]{1,0:T(8,128)(2,1)} %a_ref.1), custom_call_target="tpu_custom_call" | custom-call | tf_op jit(solution)/shard_map/pallas_call | solution.py:706
  102.4 0.7 copy.3

commit v14 on v13

--- a/solution.py
+++ b/solution.py
@@ -205,10 +205,7 @@
         src = Pb.at[b, r3(u)]
         if b == 0:
             return msend(src, 1, 4 * u, 4, 0, C0, 0)
-        return rcopy(src, R.at[2, rs_(k, 4 * u, 4), C1], s_z.at[2], r_r.at[1], 3, 0)
-
-    def m30r(u):
-        return rcopy(Pb.at[1, r3(u)], PR.at[1, rs_(k, 4 * u, 4), C1], s_z.at[2], r_p.at[1 + u], 2, 2)
+        return rcopy(src, R.at[2 + y, rs_(k, 4 * u, 4), C1], s_z.at[2], r_r.at[1], 3, 0)
 
     def m21(s, n, rs):
         return msend(Pa.at[1, r2(s, n)], 0, s, n, 1, CA, rs)
@@ -300,9 +297,10 @@
 
                 @pl.when(y == 1)
                 def _():
+                    x20(1, 0, 4, 8).start()
+                    x20(1, 4, 3, 4).start()
                     for u in range(2):
-                        m30r(u).start()
-                    x20(1, 0, 7, 8).start()
+                        m30(1, u).start()
 
             @pl.when((i == 7) | (i == 17))
             def _():
@@ -403,9 +401,10 @@
                 @pl.when((y == 0) & (i == 18))
                 def _():
                     m20(0, 7, 1, 3).start()
-                    wait_recv(XB.at[1, r2(0, 7)], r_x.at[8])
-                    Pb[1, r2(0, 7), :] += XB[1, r2(0, 7), :]
-                    m20(1, 0, 7, 2).start()
+                    for f, n, x in ((0, 4, 8), (4, 3, 4)):
+                        wait_recv(XB.at[1, r2(f, n)], r_x.at[x])
+                        Pb[1, r2(f, n), :] += XB[1, r2(f, n), :]
+                        m20(1, f, n, 2).start()
 
                 @pl.when(i == 18)
                 def _():
@@ -565,14 +564,7 @@
                 add(1, pl.ds(0, half), C0)
 
 
-            @pl.when(y == 0)
-            def _():
-                s3(pl.ds(0, half)).start()
-
-            @pl.when(y == 1)
-            def _():
-                s3(pl.ds(0, half), C0).start()
-
+            s3(pl.ds(0, half)).start()
             each(4, NS, wait_ysib)
 
             def low(b):
@@ -585,23 +577,8 @@
             def _():
                 add(1, pl.ds(half, half), C0)
 
-            @pl.when(y == 0)
-            def _():
-                s3(pl.ds(half, half)).start()
-
-            @pl.when(y == 1)
-            def _():
-                s3(pl.ds(half, half), C0).start()
-
+            s3(pl.ds(half, half)).start()
             each(NS - 1, NS - 1 + y, q1)
-
-            @pl.when(y == 1)
-            def _():
-                for u in range(2):
-                    wait_pr(half, C1, 1 + u)
-                    for h in range(2):
-                        add(1, rs_(h, 4 * u, 4), C1)
-                        s3(rs_(h, 4 * u, 4), C1).start()
 
             @pl.when(y == 0)
             def _():
@@ -659,8 +636,8 @@
 
         @pl.when(k == 0)
         def _():
-            wait_recv(R.at[2, :, C1], r_r.at[1])
-            R[0, :, C1] += R[2, :, C1]
+            wait_recv(R.at[2], r_r.at[1])
+            R[0, :, C1] += R[2, :, C1] + R[3, :, C1]
 
         o_ref[...] = (R[0] + R[1]).astype(o_ref.dtype)
 

time: 103 us -> 103 us (level)
  no operation moved by 1% of the time
where the time goes in v14:
time: 103 us
  Pallas kernels  103 us (100%)
    pallas_call x1, Pallas kernels, local_fn(): pl.pallas_call(kernel, out_shape=pltpu.VMEM((rows, rows), bf16), in_specs...  103 us

profile of v14, /device:TPU:24, one launch (start us, length us, event | category | flops | bytes accessed | tf_op | source)
XLA Modules:
  0.0 103.3 jit_solution(5237983794259301250)
XLA Ops:
  0.0 102.6 %shard_map.17 = bf16[256,256]{1,0:T(8,128)(2,1)S(1)} custom-call(bf16[256,8192]{1,0:T(8,128)(2,1)} %a_ref.1), custom_call_target="tpu_custom_call" | custom-call | tf_op jit(solution)/shard_map/pallas_call | solution.py:683
  102.7 0.7 copy.3

commit v15 on v13

--- a/solution.py
+++ b/solution.py
@@ -287,6 +287,7 @@
 
                     @pl.when(n == 1)
                     def _():
+                        T0[k, 1] = Y[k, brows(1), DALL].T
                         wait_recv(Y.at[1 - k, brows(1), DALL], r_d.at[1])
 
                     Pb[1, pl.ds(0, rows - st), :] += mm(W[ch, pl.ds(0, rows - st), :kd], Y[ch, brows(1), DALL])
@@ -302,7 +303,8 @@
                 def _():
                     for u in range(2):
                         m30r(u).start()
-                    x20(1, 0, 7, 8).start()
+                    x20(1, 0, 4, 8).start()
+                    x20(1, 4, 3, 4).start()
 
             @pl.when((i == 7) | (i == 17))
             def _():
@@ -312,11 +314,11 @@
                 def _():
                     wait_recv(Y.at[1 - k, brows(0), DALL], r_d.at[0])
 
-                for h in range(2):
-                    T0[h, b] = Y[h, brows(b), DALL].T
+                T0[1 - k, b] = Y[1 - k, brows(b), DALL].T
 
                 @pl.when(b == 0)
                 def _():
+                    T0[k, 0] = Y[k, brows(0), DALL].T
                     part0(rs_(0, 0, NS), 0)
 
                     @pl.when(y == 1)
@@ -403,9 +405,10 @@
                 @pl.when((y == 0) & (i == 18))
                 def _():
                     m20(0, 7, 1, 3).start()
-                    wait_recv(XB.at[1, r2(0, 7)], r_x.at[8])
-                    Pb[1, r2(0, 7), :] += XB[1, r2(0, 7), :]
-                    m20(1, 0, 7, 2).start()
+                    for f, n, x in ((0, 4, 8), (4, 3, 4)):
+                        wait_recv(XB.at[1, r2(f, n)], r_x.at[x])
+                        Pb[1, r2(f, n), :] += XB[1, r2(f, n), :]
+                        m20(1, f, n, 2).start()
 
                 @pl.when(i == 18)
                 def _():

time: 103 us -> 104 us (level)
  no operation moved by 1% of the time
where the time goes in v15:
time: 104 us; the launch traced here: 103 us
  Pallas kernels  103 us (99%)
    pallas_call x1, Pallas kernels, local_fn(): pl.pallas_call(kernel, out_shape=pltpu.VMEM((rows, rows), bf16), in_specs...  103 us

profile of v15, /device:TPU:24, one launch (start us, length us, event | category | flops | bytes accessed | tf_op | source)
XLA Modules:
  0.0 103.4 jit_solution(5208416219491014848)
XLA Ops:
  0.0 102.7 %shard_map.17 = bf16[256,256]{1,0:T(8,128)(2,1)S(1)} custom-call(bf16[256,8192]{1,0:T(8,128)(2,1)} %a_ref.1), custom_call_target="tpu_custom_call" | custom-call | tf_op jit(solution)/shard_map/pallas_call | solution.py:709
  102.7 0.7 copy.3

commit v16 on v15

--- a/solution.py
+++ b/solution.py
@@ -208,7 +208,7 @@
         return rcopy(src, R.at[2, rs_(k, 4 * u, 4), C1], s_z.at[2], r_r.at[1], 3, 0)
 
     def m30r(u):
-        return rcopy(Pb.at[1, r3(u)], PR.at[1, rs_(k, 4 * u, 4), C1], s_z.at[2], r_p.at[1 + u], 2, 2)
+        return rcopy(Pb.at[1, rs_(0, 2 * u, 2)], PR.at[1, rs_(k, 2 * u, 2), C1], s_z.at[2], r_p.at[1 + u], 2, 2)
 
     def m21(s, n, rs):
         return msend(Pa.at[1, r2(s, n)], 0, s, n, 1, CA, rs)
@@ -258,6 +258,9 @@
 
         pl.semaphore_wait(far, n_near)
 
+        def turn0(h, b, lo, hi):
+            T0[h, b, lo:hi, :] = Y[h, brows(b), pl.ds(ku + lo, hi - lo)].T
+
         def step(i):
             @pl.when(i < 2 * NS)
             def _():
@@ -287,7 +290,7 @@
 
                     @pl.when(n == 1)
                     def _():
-                        T0[k, 1] = Y[k, brows(1), DALL].T
+                        turn0(k, 1, 0, 2048)
                         wait_recv(Y.at[1 - k, brows(1), DALL], r_d.at[1])
 
                     Pb[1, pl.ds(0, rows - st), :] += mm(W[ch, pl.ds(0, rows - st), :kd], Y[ch, brows(1), DALL])
@@ -301,7 +304,7 @@
 
                 @pl.when(y == 1)
                 def _():
-                    for u in range(2):
+                    for u in range(4):
                         m30r(u).start()
                     x20(1, 0, 4, 8).start()
                     x20(1, 4, 3, 4).start()
@@ -314,11 +317,12 @@
                 def _():
                     wait_recv(Y.at[1 - k, brows(0), DALL], r_d.at[0])
 
-                T0[1 - k, b] = Y[1 - k, brows(b), DALL].T
+                turn0(1 - k, b, 0, kd)
+                turn0(k, b, 2048, kd)
 
                 @pl.when(b == 0)
                 def _():
-                    T0[k, 0] = Y[k, brows(0), DALL].T
+                    turn0(k, 0, 0, 2048)
                     part0(rs_(0, 0, NS), 0)
 
                     @pl.when(y == 1)
@@ -600,11 +604,11 @@
 
             @pl.when(y == 1)
             def _():
-                for u in range(2):
-                    wait_pr(half, C1, 1 + u)
+                for u in range(4):
+                    wait_pr(64, C1, 1 + u)
                     for h in range(2):
-                        add(1, rs_(h, 4 * u, 4), C1)
-                        s3(rs_(h, 4 * u, 4), C1).start()
+                        add(1, rs_(h, 2 * u, 2), C1)
+                        s3(rs_(h, 2 * u, 2), C1).start()
 
             @pl.when(y == 0)
             def _():
@@ -726,7 +730,7 @@
                 pltpu.VMEM((rows, rows), f32),
                 pltpu.VMEM((2, rows, rows // 2), f32),
                 pltpu.SemaphoreType.REGULAR,
-                dma((1,)), dma((5,)), dma((4 * NS,)), dma((NS + 1,)), dma((NU + 1,)), dma((4,)), dma((2,)), dma((9,)),
+                dma((1,)), dma((5,)), dma((4 * NS,)), dma((NS + 1,)), dma((NU + 1,)), dma((5,)), dma((2,)), dma((9,)),
             ],
             compiler_params=pltpu.CompilerParams(
                 collective_id=0, has_side_effects=True, vmem_limit_bytes=56 * 1024 * 1024),

time: 104 us -> 103 us (level)
  no operation moved by 1% of the time
where the time goes in v16:
time: 103 us
  Pallas kernels  102 us (99%)
    pallas_call x1, Pallas kernels, local_fn(): pl.pallas_call(kernel, out_shape=pltpu.VMEM((rows, rows), bf16), in_specs...  102 us

profile of v16, /device:TPU:24, one launch (start us, length us, event | category | flops | bytes accessed | tf_op | source)
XLA Modules:
  0.0 103.1 jit_solution(14286093628635430414)
XLA Ops:
  0.0 102.4 %shard_map.17 = bf16[256,256]{1,0:T(8,128)(2,1)S(1)} custom-call(bf16[256,8192]{1,0:T(8,128)(2,1)} %a_ref.1), custom_call_target="tpu_custom_call" | custom-call | tf_op jit(solution)/shard_map/pallas_call | solution.py:713
  102.5 0.7 copy.3

commit v17 on v14

--- a/solution.py
+++ b/solution.py
@@ -202,10 +202,10 @@
     m31 = msend(Pa.at[1, rs_(0, 0, NS)], 1, 0, NS, 3, CA, 0)
 
     def m30(b, u):
-        src = Pb.at[b, r3(u)]
-        if b == 0:
-            return msend(src, 1, 4 * u, 4, 0, C0, 0)
-        return rcopy(src, R.at[2 + y, rs_(k, 4 * u, 4), C1], s_z.at[2], r_r.at[1], 3, 0)
+        return msend(Pb.at[b, r3(u)], 1, 4 * u, 4, 0, C0, 0)
+
+    def m30r(u):
+        return rcopy(Pb.at[1, rs_(0, 2 * u, 2)], PR.at[1, rs_(k, 2 * u, 2), C1], s_z.at[2], r_p.at[1 + u], 2, 2 * y)
 
     def m21(s, n, rs):
         return msend(Pa.at[1, r2(s, n)], 0, s, n, 1, CA, rs)
@@ -255,6 +255,9 @@
 
         pl.semaphore_wait(far, n_near)
 
+        def turn0(h, b, lo, hi):
+            T0[h, b, lo:hi, :] = Y[h, brows(b), pl.ds(ku + lo, hi - lo)].T
+
         def step(i):
             @pl.when(i < 2 * NS)
             def _():
@@ -284,23 +287,20 @@
 
                     @pl.when(n == 1)
                     def _():
+                        turn0(k, 1, 0, 2048)
                         wait_recv(Y.at[1 - k, brows(1), DALL], r_d.at[1])
 
                     Pb[1, pl.ds(0, rows - st), :] += mm(W[ch, pl.ds(0, rows - st), :kd], Y[ch, brows(1), DALL])
 
                 each(0, 2, chunk)
 
-                @pl.when(y == 0)
-                def _():
-                    for u in range(2):
-                        m30(1, u).start()
+                for u in range(4):
+                    m30r(u).start()
 
                 @pl.when(y == 1)
                 def _():
                     x20(1, 0, 4, 8).start()
                     x20(1, 4, 3, 4).start()
-                    for u in range(2):
-                        m30(1, u).start()
 
             @pl.when((i == 7) | (i == 17))
             def _():
@@ -310,11 +310,12 @@
                 def _():
                     wait_recv(Y.at[1 - k, brows(0), DALL], r_d.at[0])
 
-                for h in range(2):
-                    T0[h, b] = Y[h, brows(b), DALL].T
+                turn0(1 - k, b, 0, kd)
+                turn0(k, b, 2048, kd)
 
                 @pl.when(b == 0)
                 def _():
+                    turn0(k, 0, 0, 2048)
                     part0(rs_(0, 0, NS), 0)
 
                     @pl.when(y == 1)
@@ -363,7 +364,7 @@
                 Pa[1, r2(2 * g), :] += XA[r2(2 * g), :]
                 Pb[0, r2(2 * g), :] += XB[0, r2(2 * g), :]
                 m21(2 * g, 2, 1).start()
-                m20(0, 2 * g, 2, 1).start()
+                m20(0, 2 * g, 2, 5).start()
 
             @pl.when((i == 17) & (y == 0))
             def _():
@@ -371,7 +372,7 @@
                 Pa[1, r2(6, 1), :] += XA[r2(6, 1), :]
                 m21(6, 1, 2).start()
                 Pb[0, r2(6, 1), :] += XB[0, r2(6, 1), :]
-                m20(0, 6, 1, 3).start()
+                m20(0, 6, 1, 7).start()
 
             @pl.when((i == 14) | (i == 18))
             def _():
@@ -400,11 +401,11 @@
 
                 @pl.when((y == 0) & (i == 18))
                 def _():
-                    m20(0, 7, 1, 3).start()
+                    m20(0, 7, 1, 7).start()
                     for f, n, x in ((0, 4, 8), (4, 3, 4)):
                         wait_recv(XB.at[1, r2(f, n)], r_x.at[x])
                         Pb[1, r2(f, n), :] += XB[1, r2(f, n), :]
-                        m20(1, f, n, 2).start()
+                        m20(1, f, n, 6).start()
 
                 @pl.when(i == 18)
                 def _():
@@ -416,7 +417,7 @@
 
                     @pl.when(y == 0)
                     def _():
-                        m20(1, 7, 1, 3).start()
+                        m20(1, 7, 1, 7).start()
 
         each(0, 19, step)
 
@@ -564,7 +565,8 @@
                 add(1, pl.ds(0, half), C0)
 
 
-            s3(pl.ds(0, half)).start()
+            s3(pl.ds(0, half), C0).start()
+
             each(4, NS, wait_ysib)
 
             def low(b):
@@ -577,18 +579,24 @@
             def _():
                 add(1, pl.ds(half, half), C0)
 
-            s3(pl.ds(half, half)).start()
+            s3(pl.ds(half, half), C0).start()
             each(NS - 1, NS - 1 + y, q1)
 
+            for u in range(4):
+                wait_pr(64, C1, 1 + u)
+                for h in range(2):
+                    add(1, rs_(h, 2 * u, 2), C1)
+                    s3(rs_(h, 2 * u, 2), C1).start()
+
             @pl.when(y == 0)
             def _():
-                wait_pr(192, C0, 1)
+                wait_pr(192, C0, 5)
                 for h in range(2):
                     add(0, rs_(h, 0, 6), C0)
-                wait_pr(224, C1, 2)
+                wait_pr(224, C1, 6)
                 for h in range(2):
                     add(0, rs_(h, 0, 7), C1)
-                wait_pr(96, C0, 3)
+                wait_pr(96, C0, 7)
                 for h in range(2):
                     add(0, rs_(h, 6, 2), C0)
                     add(0, rs_(h, 7), C1)
@@ -633,11 +641,6 @@
     @pl.when((z == 3) & (y == 0))
     def _():
         wait_recv(R.at[pl.ds(0, 2)], r_r.at[0])
-
-        @pl.when(k == 0)
-        def _():
-            wait_recv(R.at[2], r_r.at[1])
-            R[0, :, C1] += R[2, :, C1] + R[3, :, C1]
 
         o_ref[...] = (R[0] + R[1]).astype(o_ref.dtype)
 
@@ -700,7 +703,7 @@
                 pltpu.VMEM((rows, rows), f32),
                 pltpu.VMEM((2, rows, rows // 2), f32),
                 pltpu.SemaphoreType.REGULAR,
-                dma((1,)), dma((5,)), dma((4 * NS,)), dma((NS + 1,)), dma((NU + 1,)), dma((4,)), dma((2,)), dma((9,)),
+                dma((1,)), dma((5,)), dma((4 * NS,)), dma((NS + 1,)), dma((NU + 1,)), dma((8,)), dma((2,)), dma((9,)),
             ],
             compiler_params=pltpu.CompilerParams(
                 collective_id=0, has_side_effects=True, vmem_limit_bytes=56 * 1024 * 1024),

time: 103 us -> 103 us (level)
  no operation moved by 1% of the time
where the time goes in v17:
time: 103 us
  Pallas kernels  102 us (99%)
    pallas_call x1, Pallas kernels, local_fn(): pl.pallas_call(kernel, out_shape=pltpu.VMEM((rows, rows), bf16), in_specs...  102 us

profile of v17, /device:TPU:24, one launch (start us, length us, event | category | flops | bytes accessed | tf_op | source)
XLA Modules:
  0.0 103.1 jit_solution(207851447554709645)
XLA Ops:
  0.0 102.4 %shard_map.17 = bf16[256,256]{1,0:T(8,128)(2,1)S(1)} custom-call(bf16[256,8192]{1,0:T(8,128)(2,1)} %a_ref.1), custom_call_target="tpu_custom_call" | custom-call | tf_op jit(solution)/shard_map/pallas_call | solution.py:686
  102.4 0.7 copy.3

commit v18 on v17

--- a/solution.py
+++ b/solution.py
@@ -8,7 +8,7 @@
 MESH = pl.DeviceIdType.MESH
 PW = 256
 NU = 15
-XU = 128
+XU = 256
 NS = 8
 
 

time: 103 us -> 105 us (1.019)
  Pallas kernels: 102 us -> 104 us
    pallas_call x1, Pallas kernels: 102 us -> 104 us  [local_fn(): pl.pallas_call(kernel, out_shape=pltpu.VMEM((rows, rows), bf16), in_specs...]
where the time goes in v18:
time: 105 us
  Pallas kernels  104 us (99%)
    pallas_call x1, Pallas kernels, local_fn(): pl.pallas_call(kernel, out_shape=pltpu.VMEM((rows, rows), bf16), in_specs...  104 us

profile of v18, /device:TPU:24, one launch (start us, length us, event | category | flops | bytes accessed | tf_op | source)
XLA Modules:
  0.0 104.7 jit_solution(851841298390296770)
XLA Ops:
  0.0 104.1 %shard_map.17 = bf16[256,256]{1,0:T(8,128)(2,1)S(1)} custom-call(bf16[256,8192]{1,0:T(8,128)(2,1)} %a_ref.1), custom_call_target="tpu_custom_call" | custom-call | tf_op jit(solution)/shard_map/pallas_call | solution.py:686
  104.1 0.7 copy.3

commit v19 on v17

--- a/solution.py
+++ b/solution.py
@@ -79,11 +79,11 @@
     pl.semaphore_wait(bar, n_near)
 
     def z0_u(q, w=PW):
-        return rcopy(a_ref.at[:, up(q, w)], Y.at[k, :, up(q, w)], s_z.at[0], r_y.at[q], 1, c)
+        return rcopy(a_ref.at[:, up(q, w)], Y.at[k, :, up(q, w)], s_z.at[0], r_y.at[q // 2], 1, c)
 
     def z0_d(t):
         r = rs_(0, t)
-        return rcopy(a_ref.at[r, DALL], Y.at[k, r, DALL], s_z.at[0], r_y.at[2 * NS + t], 1, c)
+        return rcopy(a_ref.at[r, DALL], Y.at[k, r, DALL], s_z.at[0], r_y.at[NS + t], 1, c)
 
     def z3_d(t):
         r = rs_(t % 2, t // 2)
@@ -153,7 +153,7 @@
         return rcopy(Y.at[k, :, up(q, w)], W.at[k, :, up(q, w)], s_z.at[0], r_w.at[q], 2, 2 * y)
 
     def zU(q, w=PW):
-        wait_recv(Y.at[k, :, up(q, w)], r_y.at[q])
+        wait_recv(Y.at[k, :, up(q, w)], r_y.at[q // 2])
         Qa[0] += mm(X[k, :, up(q, w)], Y[k, :, up(q, w)])
 
     def turn(p, w=PW):
@@ -164,7 +164,7 @@
         return rcopy(Y.at[k, rs_(0, t), DALL], Y.at[k, rs_(0, t), DALL], s_z.at[1], r_d.at[t // NS], z, sib)
 
     def zD(t):
-        wait_recv(Y.at[k, rs_(0, t), DALL], r_y.at[2 * NS + t])
+        wait_recv(Y.at[k, rs_(0, t), DALL], r_y.at[NS + t])
         d_sib(t).start()
 
     def brows(b):
@@ -234,17 +234,19 @@
     def _():
         wait_recv(X.at[1 - k, :, DALL], r_d.at[NS])
 
-        def step_u(q):
-            zU(q)
-
-            @pl.when(q < 5)
-            def _():
-                u_fwd(q).start()
-
-            turn(q)
-
-        each(0, NU, step_u)
-        zU(NU, XU)
+        def step_u(p):
+            zU(2 * p, 2 * PW)
+
+            @pl.when(p < 3)
+            def _():
+                each(2 * p, 2 * p + 2, lambda q: u_fwd(q).start())
+
+            turn(2 * p)
+            turn(2 * p + 1)
+
+        each(0, NU // 2, step_u)
+        zU(NU - 1, PW + XU)
+        turn(NU - 1)
         each(NU, nd, turn)
         if xd:
             turn(nd, xd)
@@ -272,7 +274,7 @@
                 def _():
                     x31.start()
 
-                each(5, 10, lambda q: u_fwd(q).start())
+                each(6, 10, lambda q: u_fwd(q).start())
 
             @pl.when((i == 5) & (y == 1))
             def _():
@@ -703,7 +705,7 @@
                 pltpu.VMEM((rows, rows), f32),
                 pltpu.VMEM((2, rows, rows // 2), f32),
                 pltpu.SemaphoreType.REGULAR,
-                dma((1,)), dma((5,)), dma((4 * NS,)), dma((NS + 1,)), dma((NU + 1,)), dma((8,)), dma((2,)), dma((9,)),
+                dma((1,)), dma((5,)), dma((3 * NS,)), dma((NS + 1,)), dma((NU + 1,)), dma((8,)), dma((2,)), dma((9,)),
             ],
             compiler_params=pltpu.CompilerParams(
                 collective_id=0, has_side_effects=True, vmem_limit_bytes=56 * 1024 * 1024),

time: 103 us -> 103 us (level)
  no operation moved by 1% of the time
where the time goes in v19:
time: 103 us
  Pallas kernels  102 us (99%)
    pallas_call x1, Pallas kernels, local_fn(): pl.pallas_call(kernel, out_shape=pltpu.VMEM((rows, rows), bf16), in_specs...  102 us

profile of v19, /device:TPU:24, one launch (start us, length us, event | category | flops | bytes accessed | tf_op | source)
XLA Modules:
  0.0 103.0 jit_solution(4029065444371443047)
XLA Ops:
  0.0 102.3 %shard_map.17 = bf16[256,256]{1,0:T(8,128)(2,1)S(1)} custom-call(bf16[256,8192]{1,0:T(8,128)(2,1)} %a_ref.1), custom_call_target="tpu_custom_call" | custom-call | tf_op jit(solution)/shard_map/pallas_call | solution.py:688
  102.3 0.7 copy.3

commit v20 on v19

--- a/solution.py
+++ b/solution.py
@@ -94,7 +94,7 @@
         return rcopy(a_ref.at[r, UALL], Y.at[k, r, UALL], s_z.at[0], r_y.at[2 * NS + s], 2, c)
 
     def z1_u(q, w=PW):
-        return rcopy(a_ref.at[:, up(q, w)], W.at[k, :, up(q, w)], s_z.at[0], r_w.at[q], 2, 2 * y + 1)
+        return rcopy(a_ref.at[:, up(q, w)], W.at[k, :, up(q, w)], s_z.at[0], r_w.at[(q + 1) // 2], 2, 2 * y + 1)
 
     def z2_d(t):
         h, s = t % 2, t // 2
@@ -150,7 +150,7 @@
         dsend.start()
 
     def u_fwd(q, w=PW):
-        return rcopy(Y.at[k, :, up(q, w)], W.at[k, :, up(q, w)], s_z.at[0], r_w.at[q], 2, 2 * y)
+        return rcopy(Y.at[k, :, up(q, w)], W.at[k, :, up(q, w)], s_z.at[0], r_w.at[(q + 1) // 2], 2, 2 * y)
 
     def zU(q, w=PW):
         wait_recv(Y.at[k, :, up(q, w)], r_y.at[q // 2])
@@ -434,7 +434,14 @@
         return rcopy(Qa.at[1, us_(s)], R.at[c, us_(s)], s_z.at[4], r_r.at[0], 3, 2)
 
     def y2(q, w=PW):
-        wait_recv(W.at[:, :, up(q, w)], r_w.at[q])
+        @pl.when((q == 0) | (q == NU))
+        def _():
+            wait_recv(W.at[:, :, up(q, w)], r_w.at[(q + 1) // 2])
+
+        @pl.when((q % 2 == 1) & (q < NU))
+        def _():
+            wait_recv(W.at[:, :, pl.ds(0, 2 * PW)], r_w.at[(q + 1) // 2])
+
         Pa[0] += mm(X[0, :, up(q, w)], W[0, :, up(q, w)]) + mm(X[1, :, up(q, w)], W[1, :, up(q, w)])
 
     def y3(b, q, w=PW):
@@ -705,7 +712,7 @@
                 pltpu.VMEM((rows, rows), f32),
                 pltpu.VMEM((2, rows, rows // 2), f32),
                 pltpu.SemaphoreType.REGULAR,
-                dma((1,)), dma((5,)), dma((3 * NS,)), dma((NS + 1,)), dma((NU + 1,)), dma((8,)), dma((2,)), dma((9,)),
+                dma((1,)), dma((5,)), dma((3 * NS,)), dma((NS + 1,)), dma((9,)), dma((8,)), dma((2,)), dma((9,)),
             ],
             compiler_params=pltpu.CompilerParams(
                 collective_id=0, has_side_effects=True, vmem_limit_bytes=56 * 1024 * 1024),

time: 103 us -> 103 us (level)
  no operation moved by 1% of the time
where the time goes in v20:
time: 103 us
  Pallas kernels  102 us (99%)
    pallas_call x1, Pallas kernels, local_fn(): pl.pallas_call(kernel, out_shape=pltpu.VMEM((rows, rows), bf16), in_specs...  102 us

profile of v20, /device:TPU:24, one launch (start us, length us, event | category | flops | bytes accessed | tf_op | source)
XLA Modules:
  0.0 102.9 jit_solution(14470491754821038561)
XLA Ops:
  0.0 102.3 %shard_map.17 = bf16[256,256]{1,0:T(8,128)(2,1)S(1)} custom-call(bf16[256,8192]{1,0:T(8,128)(2,1)} %a_ref.1), custom_call_target="tpu_custom_call" | custom-call | tf_op jit(solution)/shard_map/pallas_call | solution.py:695
  102.3 0.7 copy.3
